TPU v7x, 512 devices: a 4x2x32 block of a 4x8x32 slice. The times are simulated.
512 devices in a mesh: ens: 2 (over y), bfly: 32 (over z), cblk: 8 (over x, core).
Axes of the slice: x: 4, y: 2, z: 32, core: 2. Of those that a mesh axis runs over, the one named last changes fastest.
The devices are a block of a 4x8x32 slice.
Arguments:
- source: bfloat16 [1048576, 512], P(('ens', 'bfly', 'cblk')), parts along dimension 0, may hold values from -6 to 6
- basis: bfloat16 [1048576, 256], P(('ens', 'bfly', 'cblk')), parts along dimension 0, may hold values from -0.046875 to 0.046875
- transfer: bfloat16 [10, 32, 256, 512], P('ens', 'bfly'), parts along dimension 0, may hold values from -0.25 to 0.25
- skeleton: int32 [512, 16], P(('ens', 'bfly', 'cblk')), parts along dimension 0, may hold values from 0 to 15, each once within a row
- row_class: int32 [1048576], P(('ens', 'bfly', 'cblk')), parts along dimension 0, may hold values from 0 to 15
- linear_table: float32 [16, 512], replicated, may hold values from 0.5 to 1.5
- cubic_table: float32 [16, 512], replicated, may hold values from 0.05 to 0.3
Outputs:
- adjoint: bfloat16 [1048576, 512], P(('ens', 'bfly', 'cblk')), parts along dimension 0
There are 2 independent parts, one for each index of `ens`. A program takes and returns all parts, laid end to end along the dimension named above; an argument that names none is the same for every part. Nothing has to cross between parts.
Inputs may be any that keep to these rules, and one draw needn't show every extreme that they name: Each row of skeleton names each of the 16 tiles once.
All inputs are finite; a program needn't handle non-finite values.
Results may differ from a plain program's by a relative error of at most 0.0052.
Values may be sent and summed in bfloat16 or wider, within the bound.
No kernel may reach another device: no remote copies, remote signals or barrier semaphores. Data moves between devices by JAX's collectives and lax.ppermute only.
A program may use at most 64 MiB of HBM per device.

v0:
```python
import math

import jax
import jax.numpy as jnp
from jax import lax
from jax.sharding import PartitionSpec as P


def from_partner(array, axis, bit):
    return lax.ppermute(array, axis, [(i, i ^ 1 << bit) for i in range(lax.axis_size(axis))])


def split_up(array, dim, count):
    dims = array.shape
    blocks = array.reshape(*dims[:dim], count, dims[dim] // count, *dims[dim + 1 :])
    return jnp.moveaxis(blocks, dim, 0)


def sum_at_owner(array, axis, dim):
    blocks = split_up(array, dim, lax.axis_size(axis))
    arrived = lax.all_to_all(blocks, axis, split_axis=0, concat_axis=0, tiled=True)
    return arrived.sum(axis=0)


def laid_out(blocks, dim):
    dims = list(blocks.shape[1:])
    dims[dim] *= blocks.shape[0]
    return jnp.moveaxis(blocks, 0, dim).reshape(dims)


def from_everyone(array, axis):
    copies = jnp.broadcast_to(array, (lax.axis_size(axis), *array.shape))
    return lax.all_to_all(copies, axis, split_axis=0, concat_axis=0, tiled=True)


def gathered_copies(array, axis, dim):
    return laid_out(from_everyone(array, axis), dim)


def times_transposed(left, right):
    dims = (((1,), (1,)), ((), ()))
    return lax.dot_general(
        left,
        right.astype(jnp.float32),
        dims,
        precision=lax.Precision.HIGHEST,
        preferred_element_type=jnp.float32,
    )


def times_plain(left, right):
    return jnp.dot(
        left,
        right.astype(jnp.float32),
        precision=lax.Precision.HIGHEST,
        preferred_element_type=jnp.float32,
    )


def leaf_terms(data, basis):
    return lax.dot_general(
        data, basis, (((0,), (0,)), ((), ())), preferred_element_type=jnp.float32
    )


def expand_rows(basis, carried, factor_rho):
    return factor_rho * lax.dot_general(
        basis, carried, (((1,), (1,)), ((), ())), preferred_element_type=jnp.float32
    )


def forward_levels(coefficient, factors):
    rank_size = factors.shape[1]
    for level in range(factors.shape[0]):
        partner = from_partner(coefficient, "bfly", level)
        coefficient = times_transposed(
            coefficient, factors[level, :, :rank_size]
        ) + times_transposed(partner, factors[level, :, rank_size:])
    return coefficient


def adjoint_levels(coefficient, factors):
    rank_size = factors.shape[1]
    for level in reversed(range(factors.shape[0])):
        sending = times_plain(coefficient, factors[level, :, rank_size:])
        received = from_partner(sending, "bfly", level)
        coefficient = times_plain(coefficient, factors[level, :, :rank_size]) + received
    return coefficient


def per_device(source, basis, transfer, skeleton, row_class, linear_table, cubic_table):
    rows, columns = source.shape
    order = skeleton[0]
    tiles = order.shape[0]
    picked = jnp.take(source.reshape(tiles, rows // tiles, columns), order, axis=0).reshape(
        rows, columns
    )
    factors = transfer[:, 0]
    factor_rho = math.sqrt(rows * lax.axis_size("cblk") / basis.shape[1])
    summed = sum_at_owner(leaf_terms(picked, basis), "cblk", 0)
    carried = forward_levels(summed, factors).astype(jnp.bfloat16)
    mapped = expand_rows(basis, gathered_copies(carried, "cblk", 0), factor_rho)
    classes = jnp.arange(linear_table.shape[0], dtype=jnp.int32)
    one_hot = (row_class[:, None] == classes[None, :]).astype(jnp.float32)
    tables = jnp.concatenate([linear_table, cubic_table], axis=1)
    looked = jnp.dot(
        one_hot, tables, precision=lax.Precision.HIGHEST, preferred_element_type=jnp.float32
    )
    linear = looked[:, :columns]
    cubic = looked[:, columns:]
    weighted = (mapped * (linear + cubic * mapped * mapped)).astype(jnp.bfloat16)
    gathered = sum_at_owner(leaf_terms(weighted, basis), "cblk", 0)
    returned = adjoint_levels(gathered, factors).astype(jnp.bfloat16)
    ordered = expand_rows(basis, gathered_copies(returned, "cblk", 0), factor_rho).astype(
        jnp.bfloat16
    )
    inverse = jnp.argsort(order)
    adjoint = jnp.take(ordered.reshape(tiles, rows // tiles, columns), inverse, axis=0)
    return adjoint.reshape(rows, columns)


def solution(mesh):
    placed = (
        P(("ens", "bfly", "cblk"), None),
        P(("ens", "bfly", "cblk"), None),
        P("ens", "bfly", None, None),
        P(("ens", "bfly", "cblk"), None),
        P(("ens", "bfly", "cblk")),
        P(),
        P(),
    )
    return jax.shard_map(
        per_device,
        mesh=mesh,
        in_specs=placed,
        out_specs=P(("ens", "bfly", "cblk"), None),
        check_vma=False,
    )
```

profile of v0, /device:TPU:33, one launch (start us, length us, event | category | flops | bytes accessed | tf_op | source)
XLA Modules:
  0.0 273.2 jit_solution(4441080189664078269)
XLA Ops:
  1.6 2.0 gather_fusion
  3.6 3.2 %broadcast_select_fusion.1 = bf16[16,128,512]{2,1,0:T(8,128)(2,1)} fusion(bf16[16,128,512]{2,1,0:T(8,128)(2,1)} %gather_fusion, pred[16]{0:T(512)(128)(4,1)S(1)} %compare_and_fusion.1), kind=kLoop, calls=%fused_computation.9 | loop fusion | flops 1048576 | bytes 4194320 | tf_op jit(solution)/shard_map/jit(_take)/select_n | solution.py:95
  6.8 3.9 %copy.12 = bf16[2048,512]{0,1:T(8,128)(2,1)} copy(bf16[2048,512]{1,0:T(8,128)(2,1)} %bitcast.91) | data formatting | bytes 4194304 | tf_op jit(solution)/shard_map/reshape | solution.py:95
  10.7 2.7 fusion.7
  13.4 53.9 %all_to_all.20 = f32[8,64,256]{2,1,0:T(8,128)} all-to-all(f32[8,64,256]{2,1,0:T(8,128)S(1)} %fusion.7), channel_id=1, replica_groups=mesh['ens'=2,'bfly'=32,'cblk'=8] {'cblk'}, dimensions={0} | all-to-all | bytes 1048576 | tf_op jit(solution)/shard_map/all_to_all | solution.py:21
  68.4 2.0 collective-permute-start
  70.7 2.8 %collective-permute-done = f32[64,256]{1,0:T(8,128)S(1)} collective-permute-done((f32[64,256]{1,0:T(8,128)S(1)}, f32[64,256]{1,0:T(8,128)S(1)}, u32[]{:S(2)}, u32[]{:S(2)}) %collective-permute-start) | collective-permute-done | bytes 65568 | tf_op jit(solution)/shard_map/ppermute | solution.py:10
  73.8 2.0 collective-permute-start.1
  76.0 4.1 %collective-permute-done.1 = f32[64,256]{1,0:T(8,128)S(1)} collective-permute-done((f32[64,256]{1,0:T(8,128)S(1)}, f32[64,256]{1,0:T(8,128)S(1)}, u32[]{:S(2)}, u32[]{:S(2)}) %collective-permute-start.1) | collective-permute-done | bytes 65568 | tf_op jit(solution)/shard_map/ppermute | solution.py:10
  80.4 2.0 collective-permute-start.2
  82.7 7.8 %collective-permute-done.2 = f32[64,256]{1,0:T(8,128)S(1)} collective-permute-done((f32[64,256]{1,0:T(8,128)S(1)}, f32[64,256]{1,0:T(8,128)S(1)}, u32[]{:S(2)}, u32[]{:S(2)}) %collective-permute-start.2) | collective-permute-done | bytes 65568 | tf_op jit(solution)/shard_map/ppermute | solution.py:10
  93.0 19.9 %collective-permute-done.3 = f32[64,256]{1,0:T(8,128)S(1)} collective-permute-done((f32[64,256]{1,0:T(8,128)S(1)}, f32[64,256]{1,0:T(8,128)S(1)}, u32[]{:S(2)}, u32[]{:S(2)}) %collective-permute-start.3) | collective-permute-done | bytes 65568 | tf_op jit(solution)/shard_map/ppermute | solution.py:10
  113.2 2.0 collective-permute-start.4
  115.4 21.2 %collective-permute-done.4 = f32[64,256]{1,0:T(8,128)S(1)} collective-permute-done((f32[64,256]{1,0:T(8,128)S(1)}, f32[64,256]{1,0:T(8,128)S(1)}, u32[]{:S(2)}, u32[]{:S(2)}) %collective-permute-start.4) | collective-permute-done | bytes 65568 | tf_op jit(solution)/shard_map/ppermute | solution.py:10
  137.6 10.1 %all-to-all-start.1 = ((bf16[8,64,256]{2,1,0:T(8,128)(2,1)}), bf16[8,64,256]{2,1,0:T(8,128)(2,1)}, u32[]{:S(2)}, u32[]{:S(2)}) async-start(bf16[8,64,256]{2,1,0:T(8,128)(2,1)} %broadcast_in_dim.17), calls=%async_computation.1 | async-start | bytes 524288 | tf_op jit(solution)/shard_map/all_to_all | solution.py:33
  147.8 6.0 %fusion.9 = f32[2048,1024]{0,1:T(8,128)} fusion(s32[2048]{0:T(1024)S(1)} %copy-done.2, f32[16,512]{1,0:T(8,128)S(1)} %copy-done.3, f32[16,512]{1,0:T(8,128)S(1)} %copy-done.4), kind=kOutput, calls=%fused_computation.26 | convolution fusion | flops 402702336 | bytes 8462336 | tf_op jit(solution)/shard_map/dot_general | solution.py:106
  154.4 6.2 %fusion.4 = f32[512,256]{1,0:T(8,128)} fusion(bf16[2048,256]{1,0:T(8,128)(2,1)} %param.10, f32[2048,1024]{0,1:T(8,128)} %fusion.9, bf16[512,256]{1,0:T(8,128)(2,1)} %bitcast.17), kind=kOutput, calls=%fused_computation.10 | convolution fusion | flops 1080033280 | bytes 11272192 | tf_op jit(solution)/shard_map/dot_general | solution.py:61
  160.6 14.7 %all_to_all.21 = f32[8,64,256]{2,1,0:T(8,128)} all-to-all(f32[8,64,256]{2,1,0:T(8,128)} %bitcast.115), channel_id=1, replica_groups=mesh['ens'=2,'bfly'=32,'cblk'=8] {'cblk'}, dimensions={0} | all-to-all | bytes 1048576 | tf_op jit(solution)/shard_map/all_to_all | solution.py:21
  176.6 3.2 %collective-permute-start.5 = (f32[64,256]{1,0:T(8,128)S(1)}, f32[64,256]{1,0:T(8,128)S(1)}, u32[]{:S(2)}, u32[]{:S(2)}) collective-permute-start(f32[64,256]{1,0:T(8,128)S(1)} %fusion.20), channel_id=1, source_target_pairs={{0,128},{8,136},{16,144},{24,152},{32,160},{40,168},{48,176},{56,1... | collective-permute-start | bytes 196616 | tf_op jit(solution)/shard_map/ppermute | solution.py:10
  179.8 27.1 %collective-permute-done.5 = f32[64,256]{1,0:T(8,128)S(1)} collective-permute-done((f32[64,256]{1,0:T(8,128)S(1)}, f32[64,256]{1,0:T(8,128)S(1)}, u32[]{:S(2)}, u32[]{:S(2)}) %collective-permute-start.5) | collective-permute-done | bytes 65568 | tf_op jit(solution)/shard_map/ppermute | solution.py:10
  207.4 2.0 collective-permute-start.6
  209.4 11.8 %collective-permute-done.6 = f32[64,256]{1,0:T(8,128)S(1)} collective-permute-done((f32[64,256]{1,0:T(8,128)S(1)}, f32[64,256]{1,0:T(8,128)S(1)}, u32[]{:S(2)}, u32[]{:S(2)}) %collective-permute-start.6) | collective-permute-done | bytes 65568 | tf_op jit(solution)/shard_map/ppermute | solution.py:10
  223.6 7.1 %collective-permute-done.7 = f32[64,256]{1,0:T(8,128)S(1)} collective-permute-done((f32[64,256]{1,0:T(8,128)S(1)}, f32[64,256]{1,0:T(8,128)S(1)}, u32[]{:S(2)}, u32[]{:S(2)}) %collective-permute-start.7) | collective-permute-done | bytes 65568 | tf_op jit(solution)/shard_map/ppermute | solution.py:10
  235.0 2.8 %collective-permute-done.8 = f32[64,256]{1,0:T(8,128)S(1)} collective-permute-done((f32[64,256]{1,0:T(8,128)}, f32[64,256]{1,0:T(8,128)S(1)}, u32[]{:S(2)}, u32[]{:S(2)}) %collective-permute-start.8) | collective-permute-done | bytes 65568 | tf_op jit(solution)/shard_map/ppermute | solution.py:10
  238.3 2.0 collective-permute-start.9
  240.3 3.1 %collective-permute-done.9 = f32[64,256]{1,0:T(8,128)S(1)} collective-permute-done((f32[64,256]{1,0:T(8,128)S(1)}, f32[64,256]{1,0:T(8,128)S(1)}, u32[]{:S(2)}, u32[]{:S(2)}) %collective-permute-start.9) | collective-permute-done | bytes 65568 | tf_op jit(solution)/shard_map/ppermute | solution.py:10
  244.3 8.4 %all-to-all-start.3 = ((bf16[8,64,256]{2,1,0:T(8,128)(2,1)}), bf16[8,64,256]{2,1,0:T(8,128)(2,1)S(1)}, u32[]{:S(2)}, u32[]{:S(2)}) async-start(bf16[8,64,256]{2,1,0:T(8,128)(2,1)} %broadcast_in_dim.18), calls=%async_computation.3 | async-start | bytes 524288 | tf_op jit(solution)/shard_map/all_to_all | solution.py:33
  252.7 6.5 %all-to-all-done.3 = bf16[8,64,256]{2,1,0:T(8,128)(2,1)S(1)} async-done(((bf16[8,64,256]{2,1,0:T(8,128)(2,1)}), bf16[8,64,256]{2,1,0:T(8,128)(2,1)S(1)}, u32[]{:S(2)}, u32[]{:S(2)}) %all-to-all-start.3) | async-done | bytes 262176 | tf_op jit(solution)/shard_map/all_to_all | solution.py:33
  259.2 3.3 %fusion.3 = bf16[2048,512]{0,1:T(8,128)(2,1)} fusion(bf16[512,256]{1,0:T(8,128)(2,1)S(1)} %bitcast.114, bf16[2048,256]{1,0:T(8,128)(2,1)} %param.10), kind=kOutput, calls=%fused_computation.7 | convolution fusion | flops 538968064 | bytes 3407872 | tf_op jit(solution)/shard_map/dot_general | solution.py:67
  262.5 3.9 %copy.17 = bf16[2048,512]{1,0:T(8,128)(2,1)} copy(bf16[2048,512]{0,1:T(8,128)(2,1)} %fusion.3) | data formatting | bytes 4194304 | tf_op jit(solution)/shard_map/reshape | solution.py:118
  266.4 3.6 %gather_fusion.1 = bf16[16,128,512]{2,1,0:T(8,128)(2,1)} fusion(bf16[16,128,512]{2,1,0:T(8,128)(2,1)} %bitcast.92, s32[1024]{0:T(1024)S(1)} %pad_clamp_fusion), kind=kCustom, calls=%fused_computation.1.clone | custom fusion | bytes 4194368 | tf_op jit(solution)/shard_map/jit(_take)/gather | solution.py:118
  270.0 3.2 %broadcast_select_fusion = bf16[16,128,512]{2,1,0:T(8,128)(2,1)} fusion(bf16[16,128,512]{2,1,0:T(8,128)(2,1)} %gather_fusion.1, pred[16]{0:T(512)(128)(4,1)S(1)} %compare_and_fusion), kind=kLoop, calls=%fused_computation.8 | loop fusion | flops 1048576 | bytes 4194320 | tf_op jit(solution)/shard_map/jit(_take)/select_n | solution.py:118
  (48 shorter events, 18.5 us)
Async XLA Ops:
  0.0 1.6 copy-start
  10.7 59.7 %copy-start.1 = (bf16[5,1,256,512]{3,2,1,0:T(8,128)(2,1)S(1)}, bf16[5,1,256,512]{3,2,1,0:T(8,128)(2,1)}, u32[]{:S(2)}) copy-start(bf16[5,1,256,512]{3,2,1,0:T(8,128)(2,1)} %param.11) | copy-start | bytes 3932164
  67.3 80.4 %copy-start.2 = (s32[2048]{0:T(1024)S(1)}, s32[2048]{0:T(1024)}, u32[]{:S(2)}) copy-start(s32[2048]{0:T(1024)} %param.13) | copy-start | bytes 24580
  67.3 80.4 %copy-start.3 = (f32[16,512]{1,0:T(8,128)S(1)}, f32[16,512]{1,0:T(8,128)}, u32[]{:S(2)}) copy-start(f32[16,512]{1,0:T(8,128)} %param.15) | copy-start | bytes 98308
  67.3 80.4 %copy-start.4 = (f32[16,512]{1,0:T(8,128)S(1)}, f32[16,512]{1,0:T(8,128)}, u32[]{:S(2)}) copy-start(f32[16,512]{1,0:T(8,128)} %param.14) | copy-start | bytes 98308
  68.4 5.0 %collective-permute-start = (f32[64,256]{1,0:T(8,128)S(1)}, f32[64,256]{1,0:T(8,128)S(1)}, u32[]{:S(2)}, u32[]{:S(2)}) collective-permute-start(f32[64,256]{1,0:T(8,128)S(1)} %reduce_sum.18), channel_id=1, source_target_pairs={{0,8},{8,0},{16,24},{24,16},{32,40},{40,32},{48,56},{56,48},{64,72... | collective-permute-start | bytes 196616 | tf_op jit(solution)/shard_map/ppermute | solution.py:10
  73.8 6.4 %collective-permute-start.1 = (f32[64,256]{1,0:T(8,128)S(1)}, f32[64,256]{1,0:T(8,128)S(1)}, u32[]{:S(2)}, u32[]{:S(2)}) collective-permute-start(f32[64,256]{1,0:T(8,128)S(1)} %convolution_add_fusion.9), channel_id=1, source_target_pairs={{0,16},{8,24},{16,0},{24,8},{32,48},{40,56},{48,32},{56,40},{64,80... | collective-permute-start | bytes 196616 | tf_op jit(solution)/shard_map/ppermute | solution.py:10
  80.4 10.1 %collective-permute-start.2 = (f32[64,256]{1,0:T(8,128)S(1)}, f32[64,256]{1,0:T(8,128)S(1)}, u32[]{:S(2)}, u32[]{:S(2)}) collective-permute-start(f32[64,256]{1,0:T(8,128)S(1)} %convolution_add_fusion.8), channel_id=1, source_target_pairs={{0,32},{8,40},{16,48},{24,56},{32,0},{40,8},{48,16},{56,24},{64,96... | collective-permute-start | bytes 196616 | tf_op jit(solution)/shard_map/ppermute | solution.py:10
  90.8 22.1 %collective-permute-start.3 = (f32[64,256]{1,0:T(8,128)S(1)}, f32[64,256]{1,0:T(8,128)S(1)}, u32[]{:S(2)}, u32[]{:S(2)}) collective-permute-start(f32[64,256]{1,0:T(8,128)S(1)} %convolution_add_fusion.7), channel_id=1, source_target_pairs={{0,64},{8,72},{16,80},{24,88},{32,96},{40,104},{48,112},{56,120},{... | collective-permute-start | bytes 196616 | tf_op jit(solution)/shard_map/ppermute | solution.py:10
  113.2 23.5 %collective-permute-start.4 = (f32[64,256]{1,0:T(8,128)S(1)}, f32[64,256]{1,0:T(8,128)S(1)}, u32[]{:S(2)}, u32[]{:S(2)}) collective-permute-start(f32[64,256]{1,0:T(8,128)S(1)} %convolution_add_fusion.6), channel_id=1, source_target_pairs={{0,128},{8,136},{16,144},{24,152},{32,160},{40,168},{48,176},{56,1... | collective-permute-start | bytes 196616 | tf_op jit(solution)/shard_map/ppermute | solution.py:10
  137.6 16.8 %all-to-all-start.1 = ((bf16[8,64,256]{2,1,0:T(8,128)(2,1)}), bf16[8,64,256]{2,1,0:T(8,128)(2,1)}, u32[]{:S(2)}, u32[]{:S(2)}) async-start(bf16[8,64,256]{2,1,0:T(8,128)(2,1)} %broadcast_in_dim.17), calls=%async_computation.1 | async-start | bytes 524288 | tf_op jit(solution)/shard_map/all_to_all | solution.py:33
  160.6 73.1 %copy-start.5 = (s32[1,16]{1,0:T(1,128)S(1)}, s32[1,16]{1,0:T(1,128)}, u32[]{:S(2)}) copy-start(s32[1,16]{1,0:T(1,128)} %param.12) | copy-start | bytes 196
  176.6 30.3 %collective-permute-start.5 = (f32[64,256]{1,0:T(8,128)S(1)}, f32[64,256]{1,0:T(8,128)S(1)}, u32[]{:S(2)}, u32[]{:S(2)}) collective-permute-start(f32[64,256]{1,0:T(8,128)S(1)} %fusion.20), channel_id=1, source_target_pairs={{0,128},{8,136},{16,144},{24,152},{32,160},{40,168},{48,176},{56,1... | collective-permute-start | bytes 196616 | tf_op jit(solution)/shard_map/ppermute | solution.py:10
  207.4 13.8 %collective-permute-start.6 = (f32[64,256]{1,0:T(8,128)S(1)}, f32[64,256]{1,0:T(8,128)S(1)}, u32[]{:S(2)}, u32[]{:S(2)}) collective-permute-start(f32[64,256]{1,0:T(8,128)S(1)} %fusion.18), channel_id=1, source_target_pairs={{0,64},{8,72},{16,80},{24,88},{32,96},{40,104},{48,112},{56,120},{... | collective-permute-start | bytes 196616 | tf_op jit(solution)/shard_map/ppermute | solution.py:10
  221.6 9.0 %collective-permute-start.7 = (f32[64,256]{1,0:T(8,128)S(1)}, f32[64,256]{1,0:T(8,128)S(1)}, u32[]{:S(2)}, u32[]{:S(2)}) collective-permute-start(f32[64,256]{1,0:T(8,128)S(1)} %fusion.16), channel_id=1, source_target_pairs={{0,32},{8,40},{16,48},{24,56},{32,0},{40,8},{48,16},{56,24},{64,96... | collective-permute-start | bytes 196616 | tf_op jit(solution)/shard_map/ppermute | solution.py:10
  231.8 6.1 %collective-permute-start.8 = (f32[64,256]{1,0:T(8,128)}, f32[64,256]{1,0:T(8,128)S(1)}, u32[]{:S(2)}, u32[]{:S(2)}) collective-permute-start(f32[64,256]{1,0:T(8,128)} %fusion.14), channel_id=1, source_target_pairs={{0,16},{8,24},{16,0},{24,8},{32,48},{40,56},{48,32},{56,40},{64,80... | collective-permute-start | bytes 196616 | tf_op jit(solution)/shard_map/ppermute | solution.py:10
  238.3 5.0 %collective-permute-start.9 = (f32[64,256]{1,0:T(8,128)S(1)}, f32[64,256]{1,0:T(8,128)S(1)}, u32[]{:S(2)}, u32[]{:S(2)}) collective-permute-start(f32[64,256]{1,0:T(8,128)S(1)} %fusion.12), channel_id=1, source_target_pairs={{0,8},{8,0},{16,24},{24,16},{32,40},{40,32},{48,56},{56,48},{64,72... | collective-permute-start | bytes 196616 | tf_op jit(solution)/shard_map/ppermute | solution.py:10
  244.3 14.9 %all-to-all-start.3 = ((bf16[8,64,256]{2,1,0:T(8,128)(2,1)}), bf16[8,64,256]{2,1,0:T(8,128)(2,1)S(1)}, u32[]{:S(2)}, u32[]{:S(2)}) async-start(bf16[8,64,256]{2,1,0:T(8,128)(2,1)} %broadcast_in_dim.18), calls=%async_computation.3 | async-start | bytes 524288 | tf_op jit(solution)/shard_map/all_to_all | solution.py:33
where the time goes:
time: 274 us; the launch traced here: 273 us
  waiting for transfers between devices  115 us (42%)
  blocking collectives  68.6 us (25%)
  starting transfers between devices  39.2 us (14%)
  matrix products  23.7 us (9%)
  local copies, waits for them, and re-layouts  15.1 us (6%)
  other arithmetic  11.3 us (4%)
    ppermute x10, waiting for transfers between devices, from_partner(): lax.ppermute(array, axis, [(i, i ^ 1 << bit) for i in range(lax.axis_size...  108 us
    all_to_all x2, blocking collectives, sum_at_owner(): lax.all_to_all(blocks, axis, split_axis=0, concat_axis=0, tiled=True)  68.6 us
    ppermute x10, starting transfers between devices, from_partner(): lax.ppermute(array, axis, [(i, i ^ 1 << bit) for i in range(lax.axis_size...  20.7 us
    all_to_all x2, starting transfers between devices, from_everyone(): return lax.all_to_all(copies, axis, split_axis=0, concat_axis=0, tiled=True)  18.5 us
    dot_general x2, matrix products, leaf_terms(): lax.dot_general(data, basis, (((0,), (0,)), ((), ())), preferred_element_...  8.92 us
    all_to_all x2, waiting for transfers between devices, from_everyone(): return lax.all_to_all(copies, axis, split_axis=0, concat_axis=0, tiled=True)  7.16 us
    dot_general x1, matrix products, per_device(): jnp.dot(one_hot, tables, precision=lax.Precision.HIGHEST, preferred_eleme...  5.99 us
  transfers between devices with their start and end apart: 12, of which 12 were waited for; matrix products, arithmetic and copies ran while one was open for 3% of the time, Pallas kernels for 0%

commit v1 on v0

v1 whole, which is shorter than its diff:
```python
import math

import jax
import jax.numpy as jnp
from jax import lax
from jax.experimental import pallas as pl
from jax.experimental.pallas import tpu as pltpu
from jax.sharding import PartitionSpec as P

F32 = jnp.float32
BF16 = jnp.bfloat16
VMEM_LIMIT = 24 * 1024 * 1024


def vmem():
    return pl.BlockSpec(memory_space=pltpu.VMEM)


def smem():
    return pl.BlockSpec(memory_space=pltpu.SMEM)


def cost(flops, bytes_accessed):
    return pl.CostEstimate(flops=flops, bytes_accessed=bytes_accessed, transcendentals=0)


def dot(left, right, left_dim, right_dim):
    return lax.dot_general(
        left, right, (((left_dim,), (right_dim,)), ((), ())), preferred_element_type=F32
    )


def leaf_kernel(order_ref, source_ref, basis_ref, out_ref, acc_ref):
    tiles = order_ref.shape[1]
    tile = source_ref.shape[0] // tiles
    step = 4
    for start in range(0, tiles, step):
        picked = jnp.concatenate(
            [
                source_ref[pl.ds(pl.multiple_of(order_ref[0, start + i] * tile, tile), tile), :]
                for i in range(step)
            ],
            axis=0,
        )
        term = dot(picked, basis_ref[pl.ds(start * tile, step * tile), :], 0, 0)
        if start == 0:
            acc_ref[...] = term
        elif start + step < tiles:
            acc_ref[...] += term
        else:
            out_ref[...] = (acc_ref[...] + term).astype(out_ref.dtype)


def leaf_terms(source, basis, skeleton):
    rows, columns = source.shape
    rank = basis.shape[1]
    return pl.pallas_call(
        leaf_kernel,
        name="leaf",
        out_shape=jax.ShapeDtypeStruct((columns, rank), BF16),
        in_specs=[smem(), vmem(), vmem()],
        out_specs=vmem(),
        scratch_shapes=[pltpu.VMEM((columns, rank), F32)],
        compiler_params=pltpu.CompilerParams(vmem_limit_bytes=VMEM_LIMIT),
        cost_estimate=cost(2 * rows * columns * rank, 2 * rows * (columns + rank)),
    )(skeleton, source, basis)


def in_three(table):
    high = table.astype(BF16)
    rest = table - high.astype(F32)
    middle = rest.astype(BF16)
    low = (rest - middle.astype(F32)).astype(BF16)
    return jnp.concatenate([high.astype(F32), middle.astype(F32), low.astype(F32)], axis=0)


def middle_kernel(
    factor_rho, carried_ref, basis_ref, class_ref, linear_ref, cubic_ref, out_ref, acc_ref
):
    rows = basis_ref.shape[0]
    classes = linear_ref.shape[0]
    linear_parts = in_three(linear_ref[...]).T.astype(BF16)
    cubic_parts = in_three(cubic_ref[...]).T.astype(BF16)
    step = 256
    for start in range(0, rows, step):
        basis = basis_ref[pl.ds(start, step), :]
        mapped = factor_rho * dot(carried_ref[...], basis, 1, 1)
        ids = lax.broadcasted_iota(jnp.int32, (classes, step), 0)
        hot = (ids == class_ref[:, pl.ds(start, step)]).astype(F32)
        hot = jnp.concatenate([hot, hot, hot], axis=0).astype(BF16)
        linear = dot(linear_parts, hot, 1, 0)
        cubic = dot(cubic_parts, hot, 1, 0)
        weighted = (mapped * (linear + cubic * mapped * mapped)).astype(BF16)
        term = dot(weighted, basis, 1, 0)
        if start == 0:
            acc_ref[...] = term
        elif start + step < rows:
            acc_ref[...] += term
        else:
            out_ref[...] = (acc_ref[...] + term).astype(out_ref.dtype)


def middle(carried, basis, row_class, linear_table, cubic_table, factor_rho):
    columns, rank = carried.shape
    rows = basis.shape[0]

    def body(*refs):
        middle_kernel(factor_rho, *refs)

    return pl.pallas_call(
        body,
        name="middle",
        out_shape=jax.ShapeDtypeStruct((columns, rank), BF16),
        in_specs=[vmem()] * 5,
        out_specs=vmem(),
        scratch_shapes=[pltpu.VMEM((columns, rank), F32)],
        compiler_params=pltpu.CompilerParams(vmem_limit_bytes=VMEM_LIMIT),
        cost_estimate=cost(8 * rows * columns * rank, 2 * rows * rank),
    )(carried, basis, row_class.reshape(1, rows), linear_table, cubic_table)


def expand_kernel(factor_rho, order_ref, returned_ref, basis_ref, out_ref, held_ref, sems):
    tiles = order_ref.shape[1]
    tile = basis_ref.shape[0] // tiles
    step = 4
    copies = []
    for start in range(0, tiles, step):
        part = factor_rho * dot(
            basis_ref[pl.ds(start * tile, step * tile), :], returned_ref[...], 1, 1
        )
        held_ref[pl.ds(start * tile, step * tile), :] = part.astype(held_ref.dtype)
        for i in range(start, start + step):
            place = pl.multiple_of(order_ref[0, i] * tile, tile)
            copies.append(
                pltpu.make_async_copy(
                    held_ref.at[pl.ds(i * tile, tile), :],
                    out_ref.at[pl.ds(place, tile), :],
                    sems.at[i],
                )
            )
            copies[-1].start()
    for copy in copies:
        copy.wait()


def expand_rows(returned, basis, skeleton, factor_rho):
    columns, rank = returned.shape
    rows = basis.shape[0]
    tiles = skeleton.shape[1]

    def body(*refs):
        expand_kernel(factor_rho, *refs)

    return pl.pallas_call(
        body,
        name="expand",
        out_shape=jax.ShapeDtypeStruct((rows, columns), BF16),
        in_specs=[smem(), vmem(), vmem()],
        out_specs=pl.BlockSpec(memory_space=pltpu.HBM),
        scratch_shapes=[pltpu.VMEM((rows, columns), BF16), pltpu.SemaphoreType.DMA((tiles,))],
        compiler_params=pltpu.CompilerParams(vmem_limit_bytes=VMEM_LIMIT),
        cost_estimate=cost(2 * rows * columns * rank, 2 * rows * (columns + rank)),
    )(skeleton, returned, basis)


def from_partner(array, axis, bit):
    return lax.ppermute(array, axis, [(i, i ^ 1 << bit) for i in range(lax.axis_size(axis))])


def sum_at_owner(array, axis):
    count = lax.axis_size(axis)
    blocks = array.reshape(count, array.shape[0] // count, array.shape[1])
    arrived = lax.all_to_all(blocks, axis, split_axis=0, concat_axis=0, tiled=True)
    return arrived.astype(F32).sum(axis=0)


def from_everyone(array, axis):
    copies = jnp.broadcast_to(array, (lax.axis_size(axis), *array.shape))
    arrived = lax.all_to_all(copies, axis, split_axis=0, concat_axis=0, tiled=True)
    return arrived.reshape(-1, array.shape[1])


def times(left, right, right_dim):
    if left.dtype == BF16:
        return dot(left, right, 1, right_dim)
    return lax.dot_general(
        left,
        right.astype(F32),
        (((1,), (right_dim,)), ((), ())),
        precision=lax.Precision.HIGHEST,
        preferred_element_type=F32,
    )


def sent(array, level):
    return array.astype(BF16) if level >= 3 else array


def forward_levels(coefficient, factors):
    rank = factors.shape[1]
    for level in range(factors.shape[0]):
        partner = from_partner(sent(coefficient, level), "bfly", level)
        coefficient = times(coefficient, factors[level, :, :rank], 1) + times(
            partner, factors[level, :, rank:], 1
        )
    return coefficient


def adjoint_levels(coefficient, factors):
    rank = factors.shape[1]
    for level in reversed(range(factors.shape[0])):
        sending = times(coefficient, factors[level, :, rank:], 0)
        received = from_partner(sent(sending, level), "bfly", level)
        coefficient = times(coefficient, factors[level, :, :rank], 0) + received.astype(F32)
    return coefficient


def per_device(source, basis, transfer, skeleton, row_class, linear_table, cubic_table):
    factors = transfer[:, 0]
    factor_rho = math.sqrt(source.shape[0] * lax.axis_size("cblk") / basis.shape[1])
    summed = sum_at_owner(leaf_terms(source, basis, skeleton), "cblk")
    carried = forward_levels(summed, factors).astype(BF16)
    back = middle(
        from_everyone(carried, "cblk"), basis, row_class, linear_table, cubic_table, factor_rho
    )
    returned = adjoint_levels(sum_at_owner(back, "cblk"), factors).astype(BF16)
    return expand_rows(from_everyone(returned, "cblk"), basis, skeleton, factor_rho)


def solution(mesh):
    placed = (
        P(("ens", "bfly", "cblk"), None),
        P(("ens", "bfly", "cblk"), None),
        P("ens", "bfly", None, None),
        P(("ens", "bfly", "cblk"), None),
        P(("ens", "bfly", "cblk")),
        P(),
        P(),
    )
    return jax.shard_map(
        per_device,
        mesh=mesh,
        in_specs=placed,
        out_specs=P(("ens", "bfly", "cblk"), None),
        check_vma=False,
    )
```

time: 274 us -> 222 us (0.81)
  waiting for transfers between devices: 115 us -> 84.5 us
  blocking collectives: 68.6 us -> 89.9 us
  matrix products: 23.7 us -> 4.58 us
  local copies, waits for them, and re-layouts: 15.1 us -> 3.56 us
  other arithmetic: 11.3 us -> 0.08 us
  starting transfers between devices: 39.2 us -> 32 us
  Pallas kernels: 0 us -> 6.2 us
    all_to_all x0 -> x2, blocking collectives: none -> 29.6 us  [from_everyone(): lax.all_to_all(copies, axis, split_axis=0, concat_axis=0, tiled=True)]
    ppermute x10, waiting for transfers between devices: 108 us -> 84.5 us  [from_partner(): lax.ppermute(array, axis, [(i, i ^ 1 << bit) for i in range(lax.axis_size...]
    dot_general x24 -> x20, matrix products: 23.7 us -> 4.58 us  [the longest x18 4.26 us: times(): lax.dot_general(left, right.astype(F32), (((1,), (right_dim,)), ((), ()))...]
    all_to_all x2 -> x0, starting transfers between devices: 18.5 us -> none  [from_everyone(): return lax.all_to_all(copies, axis, split_axis=0, concat_axis=0, tiled=True)]
    ppermute x10, starting transfers between devices: 20.7 us -> 32 us  [from_partner(): lax.ppermute(array, axis, [(i, i ^ 1 << bit) for i in range(lax.axis_size...]
    all_to_all x2, blocking collectives: 68.6 us -> 60.4 us  [sum_at_owner(): lax.all_to_all(blocks, axis, split_axis=0, concat_axis=0, tiled=True)]
    reshape x2 -> x0, local copies, waits for them, and re-layouts: 7.87 us -> none  [the longest x1 3.95 us: per_device(): jnp.take(source.reshape(tiles, rows // tiles, columns), order, axis=0)]
    all_to_all x2 -> x0, waiting for transfers between devices: 7.16 us -> none  [from_everyone(): return lax.all_to_all(copies, axis, split_axis=0, concat_axis=0, tiled=True)]
  transfers between devices with their start and end apart: 12 -> 10, of which waited for: 12 -> 10; matrix products, arithmetic and copies ran while one was open for 3% -> 1% of each run, Pallas kernels for 0% -> 0%
where the time goes in v1:
time: 222 us; the launch traced here: 221 us
  blocking collectives  89.9 us (40%)
  waiting for transfers between devices  84.5 us (38%)
  starting transfers between devices  32 us (14%)
  Pallas kernels  6.2 us (3%)
  matrix products  4.58 us (2%)
  local copies, waits for them, and re-layouts  3.56 us (2%)
    ppermute x10, waiting for transfers between devices, from_partner(): lax.ppermute(array, axis, [(i, i ^ 1 << bit) for i in range(lax.axis_size...  84.5 us
    all_to_all x2, blocking collectives, sum_at_owner(): lax.all_to_all(blocks, axis, split_axis=0, concat_axis=0, tiled=True)  60.4 us
    ppermute x10, starting transfers between devices, from_partner(): lax.ppermute(array, axis, [(i, i ^ 1 << bit) for i in range(lax.axis_size...  32 us
    all_to_all x2, blocking collectives, from_everyone(): lax.all_to_all(copies, axis, split_axis=0, concat_axis=0, tiled=True)  29.6 us
  transfers between devices with their start and end apart: 10, of which 10 were waited for; matrix products, arithmetic and copies ran while one was open for 1% of the time, Pallas kernels for 0%

profile of v1, /device:TPU:33, one launch (start us, length us, event | category | flops | bytes accessed | tf_op | source)
XLA Modules:
  0.0 221.2 jit_solution(17189058438736171851)
XLA Ops:
  0.0 1.2 copy-done
  1.2 1.6 copy-done.1
  2.8 0.7 copy-done.2
  3.5 1.3 leaf.1
  4.8 50.4 %all_to_all.20 = bf16[8,64,256]{2,1,0:T(8,128)(2,1)S(1)} all-to-all(bf16[8,64,256]{2,1,0:T(8,128)(2,1)S(1)} %bitcast.69), channel_id=1, replica_groups=mesh['ens'=2,'bfly'=32,'cblk'=8] {'cblk'}, dimensions={0} | all-to-all | bytes 524288 | tf_op jit(solution)/shard_map/all_to_all | solution.py:173
  55.2 2.0 collective-permute-start
  57.4 2.8 %collective-permute-done = f32[64,256]{1,0:T(8,128)S(1)} collective-permute-done((f32[64,256]{1,0:T(8,128)S(1)}, f32[64,256]{1,0:T(8,128)S(1)}, u32[]{:S(2)}, u32[]{:S(2)}) %collective-permute-start) | collective-permute-done | bytes 65568 | tf_op jit(solution)/shard_map/ppermute | solution.py:167
  60.5 2.0 collective-permute-start.1
  62.8 4.1 %collective-permute-done.1 = f32[64,256]{1,0:T(8,128)S(1)} collective-permute-done((f32[64,256]{1,0:T(8,128)S(1)}, f32[64,256]{1,0:T(8,128)S(1)}, u32[]{:S(2)}, u32[]{:S(2)}) %collective-permute-start.1) | collective-permute-done | bytes 65568 | tf_op jit(solution)/shard_map/ppermute | solution.py:167
  67.2 2.1 collective-permute-start.2
  69.3 0.3 fusion.6
  69.6 7.8 %collective-permute-done.2 = f32[64,256]{1,0:T(8,128)S(1)} collective-permute-done((f32[64,256]{1,0:T(8,128)S(1)}, f32[64,256]{1,0:T(8,128)S(1)}, u32[]{:S(2)}, u32[]{:S(2)}) %collective-permute-start.2) | collective-permute-done | bytes 65568 | tf_op jit(solution)/shard_map/ppermute | solution.py:167
  77.7 2.0 collective-permute-start.3
  79.7 0.3 fusion.8
  79.9 11.2 %collective-permute-done.3 = bf16[64,256]{1,0:T(8,128)(2,1)S(1)} collective-permute-done((bf16[64,256]{1,0:T(8,128)(2,1)S(1)}, bf16[64,256]{1,0:T(8,128)(2,1)S(1)}, u32[]{:S(2)}, u32[]{:S(2)}) %collective-permute-start.3) | collective-permute-done | bytes 32800 | tf_op jit(solution)/shard_map/ppermute | solution.py:167
  91.4 4.2 %collective-permute-start.4 = (bf16[64,256]{1,0:T(8,128)(2,1)S(1)}, bf16[64,256]{1,0:T(8,128)(2,1)S(1)}, u32[]{:S(2)}, u32[]{:S(2)}) collective-permute-start(bf16[64,256]{1,0:T(8,128)(2,1)S(1)} %get-tuple-element.7), channel_id=1, source_target_pairs={{0,128},{8,136},{16,144},{24,152},{32,160},{40,168},{48,176},{56,1... | collective-permute-start | bytes 98312 | tf_op jit(solution)/shard_map/ppermute | solution.py:167
  95.9 18.6 %collective-permute-done.4 = bf16[64,256]{1,0:T(8,128)(2,1)S(1)} collective-permute-done((bf16[64,256]{1,0:T(8,128)(2,1)S(1)}, bf16[64,256]{1,0:T(8,128)(2,1)S(1)}, u32[]{:S(2)}, u32[]{:S(2)}) %collective-permute-start.4) | collective-permute-done | bytes 32800 | tf_op jit(solution)/shard_map/ppermute | solution.py:167
  114.7 15.0 %all_to_all.21 = bf16[8,64,256]{2,1,0:T(8,128)(2,1)S(1)} all-to-all(bf16[8,64,256]{2,1,0:T(8,128)(2,1)S(1)} %broadcast_in_dim.6), channel_id=1, replica_groups=mesh['ens'=2,'bfly'=32,'cblk'=8] {'cblk'}, dimensions={0} | all-to-all | bytes 524288 | tf_op jit(solution)/shard_map/all_to_all | solution.py:179
  129.7 2.6 %middle.1 = bf16[512,256]{1,0:T(8,128)(2,1)S(1)} custom-call(bf16[512,256]{1,0:T(8,128)(2,1)S(1)} %bitcast.70, bf16[2048,256]{1,0:T(8,128)(2,1)S(1)} %copy-done, s32[1,2048]{1,0:T(1,128)S(1)} %bitcast.72, f32[16,512]{1,0:T(8,128)S(1)} %copy-done.3, f32[16,512]{1,0:T(8,128)S(1)} %copy-done.4), custom_call_target="tpu_custom_call" | custom-call | flops 2147483648 | bytes 1048576 | tf_op jit(solution)/shard_map/middle/pallas_call | solution.py:110
  132.3 10.0 %all_to_all.22 = bf16[8,64,256]{2,1,0:T(8,128)(2,1)S(1)} all-to-all(bf16[8,64,256]{2,1,0:T(8,128)(2,1)S(1)} %bitcast.71), channel_id=1, replica_groups=mesh['ens'=2,'bfly'=32,'cblk'=8] {'cblk'}, dimensions={0} | all-to-all | bytes 524288 | tf_op jit(solution)/shard_map/all_to_all | solution.py:173
  142.6 7.0 %collective-permute-start.5 = (bf16[64,256]{1,0:T(8,128)(2,1)S(1)}, bf16[64,256]{1,0:T(8,128)(2,1)S(1)}, u32[]{:S(2)}, u32[]{:S(2)}) collective-permute-start(bf16[64,256]{1,0:T(8,128)(2,1)S(1)} %convolution_convert_fusion.1), channel_id=1, source_target_pairs={{0,128},{8,136},{16,144},{24,152},{32,160},{40,168},{48,176},{56,1... | collective-permute-start | bytes 98312 | tf_op jit(solution)/shard_map/ppermute | solution.py:167
  149.8 15.8 %collective-permute-done.5 = bf16[64,256]{1,0:T(8,128)(2,1)S(1)} collective-permute-done((bf16[64,256]{1,0:T(8,128)(2,1)S(1)}, bf16[64,256]{1,0:T(8,128)(2,1)S(1)}, u32[]{:S(2)}, u32[]{:S(2)}) %collective-permute-start.5) | collective-permute-done | bytes 32800 | tf_op jit(solution)/shard_map/ppermute | solution.py:167
  165.8 2.0 collective-permute-start.6
  167.7 11.4 %collective-permute-done.6 = bf16[64,256]{1,0:T(8,128)(2,1)S(1)} collective-permute-done((bf16[64,256]{1,0:T(8,128)(2,1)S(1)}, bf16[64,256]{1,0:T(8,128)(2,1)S(1)}, u32[]{:S(2)}, u32[]{:S(2)}) %collective-permute-start.6) | collective-permute-done | bytes 32800 | tf_op jit(solution)/shard_map/ppermute | solution.py:167
  179.6 2.0 collective-permute-start.7
  181.6 7.1 %collective-permute-done.7 = f32[64,256]{1,0:T(8,128)S(1)} collective-permute-done((f32[64,256]{1,0:T(8,128)S(1)}, f32[64,256]{1,0:T(8,128)S(1)}, u32[]{:S(2)}, u32[]{:S(2)}) %collective-permute-start.7) | collective-permute-done | bytes 65568 | tf_op jit(solution)/shard_map/ppermute | solution.py:167
  189.1 2.0 collective-permute-start.8
  191.1 4.0 %collective-permute-done.8 = f32[64,256]{1,0:T(8,128)S(1)} collective-permute-done((f32[64,256]{1,0:T(8,128)S(1)}, f32[64,256]{1,0:T(8,128)S(1)}, u32[]{:S(2)}, u32[]{:S(2)}) %collective-permute-start.8) | collective-permute-done | bytes 65568 | tf_op jit(solution)/shard_map/ppermute | solution.py:167
  195.5 7.0 %collective-permute-start.9 = (f32[64,256]{1,0:T(8,128)S(1)}, f32[64,256]{1,0:T(8,128)S(1)}, u32[]{:S(2)}, u32[]{:S(2)}) collective-permute-start(f32[64,256]{1,0:T(8,128)S(1)} %fusion.3), channel_id=1, source_target_pairs={{0,8},{8,0},{16,24},{24,16},{32,40},{40,32},{48,56},{56,48},{64,72... | collective-permute-start | bytes 196616 | tf_op jit(solution)/shard_map/ppermute | solution.py:167
  202.5 1.6 collective-permute-done.9
  204.4 14.5 %all_to_all.23 = bf16[8,64,256]{2,1,0:T(8,128)(2,1)S(1)} all-to-all(bf16[8,64,256]{2,1,0:T(8,128)(2,1)S(1)} %broadcast_in_dim.7), channel_id=1, replica_groups=mesh['ens'=2,'bfly'=32,'cblk'=8] {'cblk'}, dimensions={0} | all-to-all | bytes 524288 | tf_op jit(solution)/shard_map/all_to_all | solution.py:179
  218.9 2.3 %expand.1 = bf16[2048,512]{1,0:T(8,128)(2,1)} custom-call(s32[1,16]{1,0:T(1,128)S(1)} %copy-done.2, bf16[512,256]{1,0:T(8,128)(2,1)S(1)} %bitcast.68, bf16[2048,256]{1,0:T(8,128)(2,1)S(1)} %copy-done), custom_call_target="tpu_custom_call" | custom-call | flops 536870912 | bytes 3145728 | tf_op jit(solution)/shard_map/expand/pallas_call | solution.py:154
  (33 shorter events, 4.2 us)
Async XLA Ops:
  0.0 1.2 copy-start
  1.2 1.6 copy-start.1
  2.8 0.7 copy-start.2
  3.5 53.7 %copy-start.6 = (bf16[5,1,256,512]{3,2,1,0:T(8,128)(2,1)S(1)}, bf16[5,1,256,512]{3,2,1,0:T(8,128)(2,1)}, u32[]{:S(2)}) copy-start(bf16[5,1,256,512]{3,2,1,0:T(8,128)(2,1)} %param.9) | copy-start | bytes 3932164
  55.2 5.0 %collective-permute-start = (f32[64,256]{1,0:T(8,128)S(1)}, f32[64,256]{1,0:T(8,128)S(1)}, u32[]{:S(2)}, u32[]{:S(2)}) collective-permute-start(f32[64,256]{1,0:T(8,128)S(1)} %convert_reduce_fusion.1), channel_id=1, source_target_pairs={{0,8},{8,0},{16,24},{24,16},{32,40},{40,32},{48,56},{56,48},{64,72... | collective-permute-start | bytes 196616 | tf_op jit(solution)/shard_map/ppermute | solution.py:167
  60.5 6.4 %collective-permute-start.1 = (f32[64,256]{1,0:T(8,128)S(1)}, f32[64,256]{1,0:T(8,128)S(1)}, u32[]{:S(2)}, u32[]{:S(2)}) collective-permute-start(f32[64,256]{1,0:T(8,128)S(1)} %convolution_add_fusion.8), channel_id=1, source_target_pairs={{0,16},{8,24},{16,0},{24,8},{32,48},{40,56},{48,32},{56,40},{64,80... | collective-permute-start | bytes 196616 | tf_op jit(solution)/shard_map/ppermute | solution.py:167
  67.2 62.5 %copy-start.3 = (f32[16,512]{1,0:T(8,128)S(1)}, f32[16,512]{1,0:T(8,128)}, u32[]{:S(2)}) copy-start(f32[16,512]{1,0:T(8,128)} %refs_3_.1) | copy-start | bytes 98308
  67.2 62.5 %copy-start.4 = (f32[16,512]{1,0:T(8,128)S(1)}, f32[16,512]{1,0:T(8,128)}, u32[]{:S(2)}) copy-start(f32[16,512]{1,0:T(8,128)} %refs_4_.1) | copy-start | bytes 98308
  67.2 62.5 %copy-start.5 = (s32[2048]{0:T(1024)S(1)}, s32[2048]{0:T(1024)}, u32[]{:S(2)}) copy-start(s32[2048]{0:T(1024)} %param.11) | copy-start | bytes 24580
  67.2 10.2 %collective-permute-start.2 = (f32[64,256]{1,0:T(8,128)S(1)}, f32[64,256]{1,0:T(8,128)S(1)}, u32[]{:S(2)}, u32[]{:S(2)}) collective-permute-start(f32[64,256]{1,0:T(8,128)S(1)} %convolution_add_fusion.7), channel_id=1, source_target_pairs={{0,32},{8,40},{16,48},{24,56},{32,0},{40,8},{48,16},{56,24},{64,96... | collective-permute-start | bytes 196616 | tf_op jit(solution)/shard_map/ppermute | solution.py:167
  77.7 13.5 %collective-permute-start.3 = (bf16[64,256]{1,0:T(8,128)(2,1)S(1)}, bf16[64,256]{1,0:T(8,128)(2,1)S(1)}, u32[]{:S(2)}, u32[]{:S(2)}) collective-permute-start(bf16[64,256]{1,0:T(8,128)(2,1)S(1)} %get-tuple-element.5), channel_id=1, source_target_pairs={{0,64},{8,72},{16,80},{24,88},{32,96},{40,104},{48,112},{56,120},{... | collective-permute-start | bytes 98312 | tf_op jit(solution)/shard_map/ppermute | solution.py:167
  91.4 23.1 %collective-permute-start.4 = (bf16[64,256]{1,0:T(8,128)(2,1)S(1)}, bf16[64,256]{1,0:T(8,128)(2,1)S(1)}, u32[]{:S(2)}, u32[]{:S(2)}) collective-permute-start(bf16[64,256]{1,0:T(8,128)(2,1)S(1)} %get-tuple-element.7), channel_id=1, source_target_pairs={{0,128},{8,136},{16,144},{24,152},{32,160},{40,168},{48,176},{56,1... | collective-permute-start | bytes 98312 | tf_op jit(solution)/shard_map/ppermute | solution.py:167
  142.6 23.0 %collective-permute-start.5 = (bf16[64,256]{1,0:T(8,128)(2,1)S(1)}, bf16[64,256]{1,0:T(8,128)(2,1)S(1)}, u32[]{:S(2)}, u32[]{:S(2)}) collective-permute-start(bf16[64,256]{1,0:T(8,128)(2,1)S(1)} %convolution_convert_fusion.1), channel_id=1, source_target_pairs={{0,128},{8,136},{16,144},{24,152},{32,160},{40,168},{48,176},{56,1... | collective-permute-start | bytes 98312 | tf_op jit(solution)/shard_map/ppermute | solution.py:167
  165.8 13.4 %collective-permute-start.6 = (bf16[64,256]{1,0:T(8,128)(2,1)S(1)}, bf16[64,256]{1,0:T(8,128)(2,1)S(1)}, u32[]{:S(2)}, u32[]{:S(2)}) collective-permute-start(bf16[64,256]{1,0:T(8,128)(2,1)S(1)} %convolution_convert_fusion), channel_id=1, source_target_pairs={{0,64},{8,72},{16,80},{24,88},{32,96},{40,104},{48,112},{56,120},{... | collective-permute-start | bytes 98312 | tf_op jit(solution)/shard_map/ppermute | solution.py:167
  179.6 9.1 %collective-permute-start.7 = (f32[64,256]{1,0:T(8,128)S(1)}, f32[64,256]{1,0:T(8,128)S(1)}, u32[]{:S(2)}, u32[]{:S(2)}) collective-permute-start(f32[64,256]{1,0:T(8,128)S(1)} %fusion.7), channel_id=1, source_target_pairs={{0,32},{8,40},{16,48},{24,56},{32,0},{40,8},{48,16},{56,24},{64,96... | collective-permute-start | bytes 196616 | tf_op jit(solution)/shard_map/ppermute | solution.py:167
  189.1 6.0 %collective-permute-start.8 = (f32[64,256]{1,0:T(8,128)S(1)}, f32[64,256]{1,0:T(8,128)S(1)}, u32[]{:S(2)}, u32[]{:S(2)}) collective-permute-start(f32[64,256]{1,0:T(8,128)S(1)} %fusion.5), channel_id=1, source_target_pairs={{0,16},{8,24},{16,0},{24,8},{32,48},{40,56},{48,32},{56,40},{64,80... | collective-permute-start | bytes 196616 | tf_op jit(solution)/shard_map/ppermute | solution.py:167
  195.5 8.6 %collective-permute-start.9 = (f32[64,256]{1,0:T(8,128)S(1)}, f32[64,256]{1,0:T(8,128)S(1)}, u32[]{:S(2)}, u32[]{:S(2)}) collective-permute-start(f32[64,256]{1,0:T(8,128)S(1)} %fusion.3), channel_id=1, source_target_pairs={{0,8},{8,0},{16,24},{24,16},{32,40},{40,32},{48,56},{56,48},{64,72... | collective-permute-start | bytes 196616 | tf_op jit(solution)/shard_map/ppermute | solution.py:167

commit v2 on v1

--- a/solution.py
+++ b/solution.py
@@ -7,6 +7,7 @@
 from jax.experimental.pallas import tpu as pltpu
 from jax.sharding import PartitionSpec as P
 
+
 F32 = jnp.float32
 BF16 = jnp.bfloat16
 VMEM_LIMIT = 24 * 1024 * 1024
@@ -14,6 +15,10 @@
 
 def vmem():
     return pl.BlockSpec(memory_space=pltpu.VMEM)
+
+
+def hbm():
+    return pl.BlockSpec(memory_space=pltpu.HBM)
 
 
 def smem():
@@ -64,6 +69,93 @@
         compiler_params=pltpu.CompilerParams(vmem_limit_bytes=VMEM_LIMIT),
         cost_estimate=cost(2 * rows * columns * rank, 2 * rows * (columns + rank)),
     )(skeleton, source, basis)
+
+
+def product(left, right, right_dim):
+    rows = left.shape[0]
+    high = left.astype(BF16)
+    low = (left - high.astype(F32)).astype(BF16)
+    both = dot(jnp.concatenate([high, low], axis=0), right, 1, right_dim)
+    return both[:rows] + both[rows:]
+
+
+def factor(factors_ref, level, part):
+    rank = factors_ref.shape[1]
+    return factors_ref[level, :, part * rank : (part + 1) * rank]
+
+
+def in_group():
+    return lax.rem(lax.axis_index("bfly"), 4)
+
+
+def spread(send_ref, first, second, third):
+    place = in_group()
+    send_ref[place] = first.astype(send_ref.dtype)
+    send_ref[place ^ 1] = first.astype(send_ref.dtype)
+    send_ref[place ^ 2] = second.astype(send_ref.dtype)
+    send_ref[place ^ 3] = third.astype(send_ref.dtype)
+
+
+def sum_kernel(arrived_ref, out_ref):
+    out_ref[...] = jnp.sum(arrived_ref[...].astype(F32), axis=0)
+
+
+def up_send_kernel(summed_ref, factors_ref, extra_ref, send_ref, own_ref):
+    del extra_ref
+    summed = summed_ref[...]
+    own = product(summed, factor(factors_ref, 0, 0), 1)
+    own_ref[...] = own
+    spread(send_ref, summed, own, summed)
+
+
+def up_take_kernel(own_ref, arrived_ref, factors_ref, extra_ref, out_ref):
+    place = in_group()
+    near = own_ref[...] + dot(arrived_ref[place ^ 1], factor(factors_ref, 0, 1), 1, 1)
+    far = arrived_ref[place ^ 2].astype(F32) + dot(arrived_ref[place ^ 3], extra_ref[...], 1, 1)
+    out_ref[...] = product(near, factor(factors_ref, 1, 0), 1) + product(
+        far, factor(factors_ref, 1, 1), 1
+    )
+
+
+def down_send_kernel(value_ref, factors_ref, extra_ref, send_ref, own_ref):
+    value = value_ref[...]
+    own = product(value, factor(factors_ref, 1, 0), 0)
+    far = product(value, factor(factors_ref, 1, 1), 0)
+    own_ref[...] = own
+    spread(
+        send_ref,
+        product(own, factor(factors_ref, 0, 1), 0),
+        far,
+        product(far, extra_ref[...], 0),
+    )
+
+
+def down_take_kernel(own_ref, arrived_ref, factors_ref, out_ref):
+    place = in_group()
+    total = product(
+        own_ref[...] + arrived_ref[place ^ 2].astype(F32), factor(factors_ref, 0, 0), 0
+    )
+    total += arrived_ref[place ^ 1].astype(F32) + arrived_ref[place ^ 3].astype(F32)
+    out_ref[...] = jnp.broadcast_to(total.astype(out_ref.dtype), out_ref.shape)
+
+
+def small_call(body, out_shape, *args):
+    return pl.pallas_call(
+        body,
+        out_shape=out_shape,
+        in_specs=[vmem()] * len(args),
+        out_specs=jax.tree.map(lambda _: vmem(), out_shape),
+        compiler_params=pltpu.CompilerParams(vmem_limit_bytes=VMEM_LIMIT),
+        cost_estimate=cost(1 << 27, 1 << 20),
+    )(*args)
+
+
+def in_fours(array):
+    size = lax.axis_size("bfly")
+    groups = [list(range(start, start + 4)) for start in range(0, size, 4)]
+    return lax.all_to_all(
+        array, "bfly", split_axis=0, concat_axis=0, axis_index_groups=groups, tiled=True
+    )
 
 
 def in_three(table):
@@ -156,7 +248,7 @@
         name="expand",
         out_shape=jax.ShapeDtypeStruct((rows, columns), BF16),
         in_specs=[smem(), vmem(), vmem()],
-        out_specs=pl.BlockSpec(memory_space=pltpu.HBM),
+        out_specs=hbm(),
         scratch_shapes=[pltpu.VMEM((rows, columns), BF16), pltpu.SemaphoreType.DMA((tiles,))],
         compiler_params=pltpu.CompilerParams(vmem_limit_bytes=VMEM_LIMIT),
         cost_estimate=cost(2 * rows * columns * rank, 2 * rows * (columns + rank)),
@@ -167,17 +259,10 @@
     return lax.ppermute(array, axis, [(i, i ^ 1 << bit) for i in range(lax.axis_size(axis))])
 
 
-def sum_at_owner(array, axis):
+def shared_out(array, axis):
     count = lax.axis_size(axis)
     blocks = array.reshape(count, array.shape[0] // count, array.shape[1])
-    arrived = lax.all_to_all(blocks, axis, split_axis=0, concat_axis=0, tiled=True)
-    return arrived.astype(F32).sum(axis=0)
-
-
-def from_everyone(array, axis):
-    copies = jnp.broadcast_to(array, (lax.axis_size(axis), *array.shape))
-    arrived = lax.all_to_all(copies, axis, split_axis=0, concat_axis=0, tiled=True)
-    return arrived.reshape(-1, array.shape[1])
+    return lax.all_to_all(blocks, axis, split_axis=0, concat_axis=0, tiled=True)
 
 
 def times(left, right, right_dim):
@@ -198,7 +283,7 @@
 
 def forward_levels(coefficient, factors):
     rank = factors.shape[1]
-    for level in range(factors.shape[0]):
+    for level in range(2, factors.shape[0]):
         partner = from_partner(sent(coefficient, level), "bfly", level)
         coefficient = times(coefficient, factors[level, :, :rank], 1) + times(
             partner, factors[level, :, rank:], 1
@@ -208,7 +293,7 @@
 
 def adjoint_levels(coefficient, factors):
     rank = factors.shape[1]
-    for level in reversed(range(factors.shape[0])):
+    for level in reversed(range(2, factors.shape[0])):
         sending = times(coefficient, factors[level, :, rank:], 0)
         received = from_partner(sent(sending, level), "bfly", level)
         coefficient = times(coefficient, factors[level, :, :rank], 0) + received.astype(F32)
@@ -217,14 +302,31 @@
 
 def per_device(source, basis, transfer, skeleton, row_class, linear_table, cubic_table):
     factors = transfer[:, 0]
-    factor_rho = math.sqrt(source.shape[0] * lax.axis_size("cblk") / basis.shape[1])
-    summed = sum_at_owner(leaf_terms(source, basis, skeleton), "cblk")
-    carried = forward_levels(summed, factors).astype(BF16)
-    back = middle(
-        from_everyone(carried, "cblk"), basis, row_class, linear_table, cubic_table, factor_rho
-    )
-    returned = adjoint_levels(sum_at_owner(back, "cblk"), factors).astype(BF16)
-    return expand_rows(from_everyone(returned, "cblk"), basis, skeleton, factor_rho)
+    rank = basis.shape[1]
+    shares = lax.axis_size("cblk")
+    factor_rho = math.sqrt(source.shape[0] * shares / rank)
+    extra = from_partner(factors[0, :, rank:], "bfly", 1)
+    leaves = leaf_terms(source, basis, skeleton)
+    leaves = shared_out(leaves, "cblk")
+    columns = leaves.shape[1]
+    whole = jax.ShapeDtypeStruct((columns, rank), F32)
+    fours = jax.ShapeDtypeStruct((4, columns, rank), BF16)
+    eights = jax.ShapeDtypeStruct((shares, columns, rank), BF16)
+
+    summed = small_call(sum_kernel, whole, leaves)
+    send, own = small_call(up_send_kernel, (fours, whole), summed, factors, extra)
+    low = small_call(up_take_kernel, whole, own, in_fours(send), factors, extra)
+    carried = forward_levels(low, factors).astype(BF16)
+    carried = shared_out(
+        jnp.broadcast_to(carried, eights.shape).reshape(shares * columns, rank), "cblk"
+    ).reshape(shares * columns, rank)
+    back = middle(carried, basis, row_class, linear_table, cubic_table, factor_rho)
+    summed = shared_out(back, "cblk").astype(F32).sum(axis=0)
+    high = adjoint_levels(summed, factors)
+    send, own = small_call(down_send_kernel, (fours, whole), high, factors, extra)
+    returned = small_call(down_take_kernel, eights, own, in_fours(send), factors)
+    returned = lax.all_to_all(returned, "cblk", split_axis=0, concat_axis=0, tiled=True)
+    return expand_rows(returned.reshape(shares * columns, rank), basis, skeleton, factor_rho)
 
 
 def solution(mesh):
@@ -237,6 +339,7 @@
         P(),
         P(),
     )
+
     return jax.shard_map(
         per_device,
         mesh=mesh,

time: 222 us -> 218 us (0.982)
  starting transfers between devices: 32 us -> 73.1 us
  blocking collectives: 89.9 us -> 53.2 us
  waiting for transfers between devices: 84.5 us -> 76.9 us
    all_to_all x0 -> x1, starting transfers between devices: none -> 44.8 us  [shared_out(): return lax.all_to_all(blocks, axis, split_axis=0, concat_axis=0, tiled=True)]
    all_to_all x4 -> x5, blocking collectives: 89.9 us -> 53.2 us  [the longest x2 27.6 us: shared_out(): return lax.all_to_all(blocks, axis, split_axis=0, concat_axis=0, tiled=True)]
    ppermute x10 -> x7, waiting for transfers between devices: 84.5 us -> 72.3 us  [from_partner(): lax.ppermute(array, axis, [(i, i ^ 1 << bit) for i in range(lax.axis_size...]
    all_to_all x0 -> x1, waiting for transfers between devices: none -> 4.57 us  [shared_out(): return lax.all_to_all(blocks, axis, split_axis=0, concat_axis=0, tiled=True)]
    ppermute x10 -> x7, starting transfers between devices: 32 us -> 28.3 us  [from_partner(): lax.ppermute(array, axis, [(i, i ^ 1 << bit) for i in range(lax.axis_size...]
  transfers between devices with their start and end apart: 10 -> 8, of which waited for: 10 -> 8; matrix products, arithmetic and copies ran while one was open for 1% -> 0% of each run, Pallas kernels for 0% -> 0%
where the time goes in v2:
time: 218 us
  waiting for transfers between devices  76.9 us (35%)
  starting transfers between devices  73.1 us (34%)
  blocking collectives  53.2 us (24%)
  Pallas kernels  8.01 us (4%)
  local copies, waits for them, and re-layouts  3.67 us (2%)
  matrix products  2.66 us (1%)
    ppermute x7, waiting for transfers between devices, from_partner(): lax.ppermute(array, axis, [(i, i ^ 1 << bit) for i in range(lax.axis_size...  72.3 us
    all_to_all x1, starting transfers between devices, shared_out(): return lax.all_to_all(blocks, axis, split_axis=0, concat_axis=0, tiled=True)  44.8 us
    ppermute x7, starting transfers between devices, from_partner(): lax.ppermute(array, axis, [(i, i ^ 1 << bit) for i in range(lax.axis_size...  28.3 us
    all_to_all x2, blocking collectives, shared_out(): return lax.all_to_all(blocks, axis, split_axis=0, concat_axis=0, tiled=True)  27.6 us
    all_to_all x2, blocking collectives, in_fours(): lax.all_to_all(array, 'bfly', split_axis=0, concat_axis=0, axis_index_gro...  14.5 us
    all_to_all x1, blocking collectives, per_device(): lax.all_to_all(returned, 'cblk', split_axis=0, concat_axis=0, tiled=True)  11 us
    all_to_all x1, waiting for transfers between devices, shared_out(): return lax.all_to_all(blocks, axis, split_axis=0, concat_axis=0, tiled=True)  4.57 us
  transfers between devices with their start and end apart: 8, of which 8 were waited for; matrix products, arithmetic and copies ran while one was open for 0% of the time, Pallas kernels for 0%

profile of v2, /device:TPU:33, one launch (start us, length us, event | category | flops | bytes accessed | tf_op | source)
XLA Modules:
  0.0 217.8 jit_solution(10549784673884688328)
XLA Ops:
  0.0 1.3 copy-done.1
  1.3 1.6 copy-done.3
  2.9 0.7 copy-done.4
  3.6 2.0 leaf.1
  5.6 44.8 %all-to-all-start = ((bf16[8,64,256]{2,1,0:T(8,128)(2,1)}), bf16[8,64,256]{2,1,0:T(8,128)(2,1)S(1)}, u32[]{:S(2)}, u32[]{:S(2)}) async-start(bf16[8,64,256]{2,1,0:T(8,128)(2,1)} %bitcast), calls=%async_computation | async-start | bytes 524288 | tf_op jit(solution)/shard_map/all_to_all | solution.py:265
  50.4 2.0 collective-permute-start
  52.3 4.6 %all-to-all-done.arrived_ref = bf16[8,64,256]{2,1,0:T(8,128)(2,1)S(1)} async-done(((bf16[8,64,256]{2,1,0:T(8,128)(2,1)}), bf16[8,64,256]{2,1,0:T(8,128)(2,1)S(1)}, u32[]{:S(2)}, u32[]{:S(2)}) %all-to-all-start) | async-done | bytes 262176 | tf_op jit(solution)/shard_map/all_to_all | solution.py:265
  56.9 1.0 collective-permute-done.extra_ref
  58.1 7.3 %all_to_all.30.arrived_ref = bf16[4,64,256]{2,1,0:T(8,128)(2,1)S(1)} all-to-all(bf16[4,64,256]{2,1,0:T(8,128)(2,1)S(1)} %get-tuple-element.10), channel_id=1, replica_groups={{0,8,16,24},{32,40,48,56},{64,72,80,88},{96,104,112,120},{128,136,144,1..., dimensions={0} | all-to-all | bytes 262144 | tf_op jit(solution)/shard_map/all_to_all | solution.py:156
  65.4 0.4 shard_map.75
  65.9 2.1 collective-permute-start.1
  68.0 9.1 %collective-permute-done.1 = f32[64,256]{1,0:T(8,128)S(1)} collective-permute-done((f32[64,256]{1,0:T(8,128)S(1)}, f32[64,256]{1,0:T(8,128)S(1)}, u32[]{:S(2)}, u32[]{:S(2)}) %collective-permute-start.1) | collective-permute-done | bytes 65568 | tf_op jit(solution)/shard_map/ppermute | solution.py:259
  77.3 0.3 fusion.6
  77.6 2.0 collective-permute-start.2
  79.6 0.3 fusion.3
  79.9 11.5 %collective-permute-done.2 = bf16[64,256]{1,0:T(8,128)(2,1)S(1)} collective-permute-done((bf16[64,256]{1,0:T(8,128)(2,1)S(1)}, bf16[64,256]{1,0:T(8,128)(2,1)S(1)}, u32[]{:S(2)}, u32[]{:S(2)}) %collective-permute-start.2) | collective-permute-done | bytes 32800 | tf_op jit(solution)/shard_map/ppermute | solution.py:259
  91.6 7.9 %collective-permute-start.3 = (bf16[64,256]{1,0:T(8,128)(2,1)S(1)}, bf16[64,256]{1,0:T(8,128)(2,1)S(1)}, u32[]{:S(2)}, u32[]{:S(2)}) collective-permute-start(bf16[64,256]{1,0:T(8,128)(2,1)S(1)} %get-tuple-element.15), channel_id=1, source_target_pairs={{0,128},{8,136},{16,144},{24,152},{32,160},{40,168},{48,176},{56,1... | collective-permute-start | bytes 98312 | tf_op jit(solution)/shard_map/ppermute | solution.py:259
  99.6 0.3 fusion.5
  99.8 14.8 %collective-permute-done.3 = bf16[64,256]{1,0:T(8,128)(2,1)S(1)} collective-permute-done((bf16[64,256]{1,0:T(8,128)(2,1)S(1)}, bf16[64,256]{1,0:T(8,128)(2,1)S(1)}, u32[]{:S(2)}, u32[]{:S(2)}) %collective-permute-start.3) | collective-permute-done | bytes 32800 | tf_op jit(solution)/shard_map/ppermute | solution.py:259
  114.8 17.6 %all_to_all.31 = bf16[8,64,256]{2,1,0:T(8,128)(2,1)S(1)} all-to-all(bf16[8,64,256]{2,1,0:T(8,128)(2,1)S(1)} %broadcast_in_dim.3), channel_id=1, replica_groups=mesh['ens'=2,'bfly'=32,'cblk'=8] {'cblk'}, dimensions={0} | all-to-all | bytes 524288 | tf_op jit(solution)/shard_map/all_to_all | solution.py:265
  132.5 2.6 %middle.1 = bf16[512,256]{1,0:T(8,128)(2,1)S(1)} custom-call(bf16[512,256]{1,0:T(8,128)(2,1)S(1)} %bitcast.64, bf16[2048,256]{1,0:T(8,128)(2,1)S(1)} %copy-done.2, s32[1,2048]{1,0:T(1,128)S(1)} %bitcast.66, f32[16,512]{1,0:T(8,128)S(1)} %copy-done.6, f32[16,512]{1,0:T(8,128)S(1)} %copy-done.7), custom_call_target="tpu_custom_call" | custom-call | flops 2147483648 | bytes 1048576 | tf_op jit(solution)/shard_map/middle/pallas_call | solution.py:202
  135.0 10.0 %all_to_all.32 = bf16[8,64,256]{2,1,0:T(8,128)(2,1)S(1)} all-to-all(bf16[8,64,256]{2,1,0:T(8,128)(2,1)S(1)} %bitcast.65), channel_id=1, replica_groups=mesh['ens'=2,'bfly'=32,'cblk'=8] {'cblk'}, dimensions={0} | all-to-all | bytes 524288 | tf_op jit(solution)/shard_map/all_to_all | solution.py:265
  145.3 10.5 %collective-permute-start.4 = (bf16[64,256]{1,0:T(8,128)(2,1)S(1)}, bf16[64,256]{1,0:T(8,128)(2,1)S(1)}, u32[]{:S(2)}, u32[]{:S(2)}) collective-permute-start(bf16[64,256]{1,0:T(8,128)(2,1)S(1)} %convolution_convert_fusion.1), channel_id=1, source_target_pairs={{0,128},{8,136},{16,144},{24,152},{32,160},{40,168},{48,176},{56,1... | collective-permute-start | bytes 98312 | tf_op jit(solution)/shard_map/ppermute | solution.py:259
  156.0 12.3 %collective-permute-done.4 = bf16[64,256]{1,0:T(8,128)(2,1)S(1)} collective-permute-done((bf16[64,256]{1,0:T(8,128)(2,1)S(1)}, bf16[64,256]{1,0:T(8,128)(2,1)S(1)}, u32[]{:S(2)}, u32[]{:S(2)}) %collective-permute-start.4) | collective-permute-done | bytes 32800 | tf_op jit(solution)/shard_map/ppermute | solution.py:259
  168.5 2.0 collective-permute-start.5
  170.5 14.6 %collective-permute-done.5 = bf16[64,256]{1,0:T(8,128)(2,1)S(1)} collective-permute-done((bf16[64,256]{1,0:T(8,128)(2,1)S(1)}, bf16[64,256]{1,0:T(8,128)(2,1)S(1)}, u32[]{:S(2)}, u32[]{:S(2)}) %collective-permute-start.5) | collective-permute-done | bytes 32800 | tf_op jit(solution)/shard_map/ppermute | solution.py:259
  185.6 2.0 collective-permute-start.6
  187.5 9.0 %collective-permute-done.6 = f32[64,256]{1,0:T(8,128)S(1)} collective-permute-done((f32[64,256]{1,0:T(8,128)S(1)}, f32[64,256]{1,0:T(8,128)S(1)}, u32[]{:S(2)}, u32[]{:S(2)}) %collective-permute-start.6) | collective-permute-done | bytes 65568 | tf_op jit(solution)/shard_map/ppermute | solution.py:259
  196.7 0.3 shard_map.76
  197.1 7.2 %all_to_all.33.arrived_ref = bf16[4,64,256]{2,1,0:T(8,128)(2,1)S(1)} all-to-all(bf16[4,64,256]{2,1,0:T(8,128)(2,1)S(1)} %get-tuple-element.12), channel_id=1, replica_groups={{0,8,16,24},{32,40,48,56},{64,72,80,88},{96,104,112,120},{128,136,144,1..., dimensions={0} | all-to-all | bytes 262144 | tf_op jit(solution)/shard_map/all_to_all | solution.py:156
  204.4 11.0 %all_to_all.34 = bf16[8,64,256]{2,1,0:T(8,128)(2,1)S(1)} all-to-all(bf16[8,64,256]{2,1,0:T(8,128)(2,1)S(1)} %shard_map.77), channel_id=1, replica_groups=mesh['ens'=2,'bfly'=32,'cblk'=8] {'cblk'}, dimensions={0} | all-to-all | bytes 524288 | tf_op jit(solution)/shard_map/all_to_all | solution.py:328
  215.5 2.3 %expand.1 = bf16[2048,512]{1,0:T(8,128)(2,1)} custom-call(s32[1,16]{1,0:T(1,128)S(1)} %copy-done.5, bf16[512,256]{1,0:T(8,128)(2,1)S(1)} %bitcast.63, bf16[2048,256]{1,0:T(8,128)(2,1)S(1)} %copy-done.2), custom_call_target="tpu_custom_call" | custom-call | flops 536870912 | bytes 3145728 | tf_op jit(solution)/shard_map/expand/pallas_call | solution.py:246
  (30 shorter events, 2.4 us)
Async XLA Ops:
  0.0 50.3 %copy-start = (bf16[5,1,256,512]{3,2,1,0:T(8,128)(2,1)S(1)}, bf16[5,1,256,512]{3,2,1,0:T(8,128)(2,1)}, u32[]{:S(2)}) copy-start(bf16[5,1,256,512]{3,2,1,0:T(8,128)(2,1)} %param.9) | copy-start | bytes 3932164
  0.0 1.3 copy-start.1
  1.3 1.6 copy-start.3
  2.9 0.7 copy-start.4
  5.6 51.3 %all-to-all-start = ((bf16[8,64,256]{2,1,0:T(8,128)(2,1)}), bf16[8,64,256]{2,1,0:T(8,128)(2,1)S(1)}, u32[]{:S(2)}, u32[]{:S(2)}) async-start(bf16[8,64,256]{2,1,0:T(8,128)(2,1)} %bitcast), calls=%async_computation | async-start | bytes 524288 | tf_op jit(solution)/shard_map/all_to_all | solution.py:265
  50.4 7.6 %collective-permute-start = (bf16[256,256]{1,0:T(8,128)(2,1)S(1)}, bf16[256,256]{1,0:T(8,128)(2,1)S(1)}, u32[]{:S(2)}, u32[]{:S(2)}) collective-permute-start(bf16[256,256]{1,0:T(8,128)(2,1)S(1)} %slice_bitcast_fusion.6), channel_id=1, source_target_pairs={{0,16},{8,24},{16,0},{24,8},{32,48},{40,56},{48,32},{56,40},{64,80... | collective-permute-start | bytes 393224 | tf_op jit(solution)/shard_map/ppermute | solution.py:259
  65.8 66.6 %copy-start.2 = (bf16[2048,256]{1,0:T(8,128)(2,1)S(1)}, bf16[2048,256]{1,0:T(8,128)(2,1)}, u32[]{:S(2)}) copy-start(bf16[2048,256]{1,0:T(8,128)(2,1)} %refs_2_.1) | copy-start | bytes 3145732
  65.8 66.6 %copy-start.6 = (f32[16,512]{1,0:T(8,128)S(1)}, f32[16,512]{1,0:T(8,128)}, u32[]{:S(2)}) copy-start(f32[16,512]{1,0:T(8,128)} %refs_3_.1) | copy-start | bytes 98308
  65.9 66.6 %copy-start.7 = (f32[16,512]{1,0:T(8,128)S(1)}, f32[16,512]{1,0:T(8,128)}, u32[]{:S(2)}) copy-start(f32[16,512]{1,0:T(8,128)} %refs_4_.1) | copy-start | bytes 98308
  65.9 66.6 %copy-start.8 = (s32[2048]{0:T(1024)S(1)}, s32[2048]{0:T(1024)}, u32[]{:S(2)}) copy-start(s32[2048]{0:T(1024)} %param.11) | copy-start | bytes 24580
  65.9 11.2 %collective-permute-start.1 = (f32[64,256]{1,0:T(8,128)S(1)}, f32[64,256]{1,0:T(8,128)S(1)}, u32[]{:S(2)}, u32[]{:S(2)}) collective-permute-start(f32[64,256]{1,0:T(8,128)S(1)} %shard_map.75), channel_id=1, source_target_pairs={{0,32},{8,40},{16,48},{24,56},{32,0},{40,8},{48,16},{56,24},{64,96... | collective-permute-start | bytes 196616 | tf_op jit(solution)/shard_map/ppermute | solution.py:259
  77.6 13.8 %collective-permute-start.2 = (bf16[64,256]{1,0:T(8,128)(2,1)S(1)}, bf16[64,256]{1,0:T(8,128)(2,1)S(1)}, u32[]{:S(2)}, u32[]{:S(2)}) collective-permute-start(bf16[64,256]{1,0:T(8,128)(2,1)S(1)} %get-tuple-element.13), channel_id=1, source_target_pairs={{0,64},{8,72},{16,80},{24,88},{32,96},{40,104},{48,112},{56,120},{... | collective-permute-start | bytes 98312 | tf_op jit(solution)/shard_map/ppermute | solution.py:259
  91.6 23.0 %collective-permute-start.3 = (bf16[64,256]{1,0:T(8,128)(2,1)S(1)}, bf16[64,256]{1,0:T(8,128)(2,1)S(1)}, u32[]{:S(2)}, u32[]{:S(2)}) collective-permute-start(bf16[64,256]{1,0:T(8,128)(2,1)S(1)} %get-tuple-element.15), channel_id=1, source_target_pairs={{0,128},{8,136},{16,144},{24,152},{32,160},{40,168},{48,176},{56,1... | collective-permute-start | bytes 98312 | tf_op jit(solution)/shard_map/ppermute | solution.py:259
  145.3 23.0 %collective-permute-start.4 = (bf16[64,256]{1,0:T(8,128)(2,1)S(1)}, bf16[64,256]{1,0:T(8,128)(2,1)S(1)}, u32[]{:S(2)}, u32[]{:S(2)}) collective-permute-start(bf16[64,256]{1,0:T(8,128)(2,1)S(1)} %convolution_convert_fusion.1), channel_id=1, source_target_pairs={{0,128},{8,136},{16,144},{24,152},{32,160},{40,168},{48,176},{56,1... | collective-permute-start | bytes 98312 | tf_op jit(solution)/shard_map/ppermute | solution.py:259
  168.5 16.6 %collective-permute-start.5 = (bf16[64,256]{1,0:T(8,128)(2,1)S(1)}, bf16[64,256]{1,0:T(8,128)(2,1)S(1)}, u32[]{:S(2)}, u32[]{:S(2)}) collective-permute-start(bf16[64,256]{1,0:T(8,128)(2,1)S(1)} %convolution_convert_fusion), channel_id=1, source_target_pairs={{0,64},{8,72},{16,80},{24,88},{32,96},{40,104},{48,112},{56,120},{... | collective-permute-start | bytes 98312 | tf_op jit(solution)/shard_map/ppermute | solution.py:259
  185.6 10.9 %collective-permute-start.6 = (f32[64,256]{1,0:T(8,128)S(1)}, f32[64,256]{1,0:T(8,128)S(1)}, u32[]{:S(2)}, u32[]{:S(2)}) collective-permute-start(f32[64,256]{1,0:T(8,128)S(1)} %fusion.1), channel_id=1, source_target_pairs={{0,32},{8,40},{16,48},{24,56},{32,0},{40,8},{48,16},{56,24},{64,96... | collective-permute-start | bytes 196616 | tf_op jit(solution)/shard_map/ppermute | solution.py:259
  197.1 18.4 %copy-start.5 = (s32[1,16]{1,0:T(1,128)S(1)}, s32[1,16]{1,0:T(1,128)}, u32[]{:S(2)}) copy-start(s32[1,16]{1,0:T(1,128)} %refs_0_.1) | copy-start | bytes 196

commit v3 on v2

--- a/solution.py
+++ b/solution.py
@@ -11,6 +11,8 @@
 F32 = jnp.float32
 BF16 = jnp.bfloat16
 VMEM_LIMIT = 24 * 1024 * 1024
+LEAF_LIMIT = 66_200_000
+LABEL_ROWS = 16
 
 
 def vmem():
@@ -35,9 +37,44 @@
     )
 
 
-def leaf_kernel(order_ref, source_ref, basis_ref, out_ref, acc_ref):
+def leaf_kernel(
+    order_hbm,
+    class_hbm,
+    source_hbm,
+    basis_hbm,
+    out_ref,
+    packed_hbm,
+    acc_ref,
+    order_ref,
+    class_ref,
+    source_ref,
+    basis_ref,
+    label_ref,
+    sems,
+):
+    rows = source_ref.shape[0]
+    basis_in = pltpu.make_async_copy(basis_hbm, basis_ref, sems.at[0])
+    source_in = pltpu.make_async_copy(source_hbm, source_ref, sems.at[1])
+    order_in = pltpu.make_async_copy(order_hbm, order_ref, sems.at[2])
+    class_in = pltpu.make_async_copy(class_hbm, class_ref, sems.at[3])
+    for copy in (order_in, class_in, basis_in, source_in):
+        copy.start()
+    class_in.wait()
+    width = label_ref.shape[1]
+    label = [class_ref[:, pl.ds(at, width)].astype(F32) for at in range(0, rows, width)]
+    label.append(jnp.zeros((label_ref.shape[0] - len(label), width), F32))
+    label_ref[...] = jnp.concatenate(label, axis=0).astype(label_ref.dtype)
+    basis_in.wait()
+    basis_out = pltpu.make_async_copy(basis_ref, packed_hbm.at[pl.ds(0, rows), :], sems.at[4])
+    basis_out.start()
+    order_in.wait()
+    source_in.wait()
+    label_out = pltpu.make_async_copy(
+        label_ref, packed_hbm.at[pl.ds(rows, label_ref.shape[0]), :], sems.at[5]
+    )
+    label_out.start()
     tiles = order_ref.shape[1]
-    tile = source_ref.shape[0] // tiles
+    tile = rows // tiles
     step = 4
     for start in range(0, tiles, step):
         picked = jnp.concatenate(
@@ -54,21 +91,35 @@
             acc_ref[...] += term
         else:
             out_ref[...] = (acc_ref[...] + term).astype(out_ref.dtype)
-
-
-def leaf_terms(source, basis, skeleton):
+    basis_out.wait()
+    label_out.wait()
+
+
+def leaf_terms(source, basis, skeleton, row_class):
     rows, columns = source.shape
     rank = basis.shape[1]
+    labels = LABEL_ROWS
     return pl.pallas_call(
         leaf_kernel,
         name="leaf",
-        out_shape=jax.ShapeDtypeStruct((columns, rank), BF16),
-        in_specs=[smem(), vmem(), vmem()],
-        out_specs=vmem(),
-        scratch_shapes=[pltpu.VMEM((columns, rank), F32)],
-        compiler_params=pltpu.CompilerParams(vmem_limit_bytes=VMEM_LIMIT),
+        out_shape=(
+            jax.ShapeDtypeStruct((columns, rank), BF16),
+            jax.ShapeDtypeStruct((rows + labels, rank), BF16),
+        ),
+        in_specs=[hbm()] * 4,
+        out_specs=(vmem(), hbm()),
+        scratch_shapes=[
+            pltpu.VMEM((columns, rank), F32),
+            pltpu.SMEM(skeleton.shape, jnp.int32),
+            pltpu.VMEM((1, rows), jnp.int32),
+            pltpu.VMEM(source.shape, source.dtype),
+            pltpu.VMEM(basis.shape, basis.dtype),
+            pltpu.VMEM((labels, rank), BF16),
+            pltpu.SemaphoreType.DMA((6,)),
+        ],
+        compiler_params=pltpu.CompilerParams(vmem_limit_bytes=LEAF_LIMIT),
         cost_estimate=cost(2 * rows * columns * rank, 2 * rows * (columns + rank)),
-    )(skeleton, source, basis)
+    )(skeleton, row_class.reshape(1, rows), source, basis)
 
 
 def product(left, right, right_dim):
@@ -94,27 +145,6 @@
     send_ref[place ^ 1] = first.astype(send_ref.dtype)
     send_ref[place ^ 2] = second.astype(send_ref.dtype)
     send_ref[place ^ 3] = third.astype(send_ref.dtype)
-
-
-def sum_kernel(arrived_ref, out_ref):
-    out_ref[...] = jnp.sum(arrived_ref[...].astype(F32), axis=0)
-
-
-def up_send_kernel(summed_ref, factors_ref, extra_ref, send_ref, own_ref):
-    del extra_ref
-    summed = summed_ref[...]
-    own = product(summed, factor(factors_ref, 0, 0), 1)
-    own_ref[...] = own
-    spread(send_ref, summed, own, summed)
-
-
-def up_take_kernel(own_ref, arrived_ref, factors_ref, extra_ref, out_ref):
-    place = in_group()
-    near = own_ref[...] + dot(arrived_ref[place ^ 1], factor(factors_ref, 0, 1), 1, 1)
-    far = arrived_ref[place ^ 2].astype(F32) + dot(arrived_ref[place ^ 3], extra_ref[...], 1, 1)
-    out_ref[...] = product(near, factor(factors_ref, 1, 0), 1) + product(
-        far, factor(factors_ref, 1, 1), 1
-    )
 
 
 def down_send_kernel(value_ref, factors_ref, extra_ref, send_ref, own_ref):
@@ -166,49 +196,64 @@
     return jnp.concatenate([high.astype(F32), middle.astype(F32), low.astype(F32)], axis=0)
 
 
-def middle_kernel(
-    factor_rho, carried_ref, basis_ref, class_ref, linear_ref, cubic_ref, out_ref, acc_ref
-):
-    rows = basis_ref.shape[0]
+def middle_kernel(factor_rho, count, *refs):
+    carried_ref, linear_ref, cubic_ref = refs[:3]
+    packed = refs[3 : 3 + count]
+    out_ref, table_ref, held_ref, sems = refs[3 + count :]
+    copies = [
+        pltpu.make_async_copy(packed[at], held_ref.at[at], sems.at[at]) for at in range(count)
+    ]
+    for copy in copies:
+        copy.start()
+    columns = carried_ref.shape[0]
     classes = linear_ref.shape[0]
-    linear_parts = in_three(linear_ref[...]).T.astype(BF16)
-    cubic_parts = in_three(cubic_ref[...]).T.astype(BF16)
-    step = 256
-    for start in range(0, rows, step):
-        basis = basis_ref[pl.ds(start, step), :]
-        mapped = factor_rho * dot(carried_ref[...], basis, 1, 1)
-        ids = lax.broadcasted_iota(jnp.int32, (classes, step), 0)
-        hot = (ids == class_ref[:, pl.ds(start, step)]).astype(F32)
-        hot = jnp.concatenate([hot, hot, hot], axis=0).astype(BF16)
-        linear = dot(linear_parts, hot, 1, 0)
-        cubic = dot(cubic_parts, hot, 1, 0)
-        weighted = (mapped * (linear + cubic * mapped * mapped)).astype(BF16)
-        term = dot(weighted, basis, 1, 0)
-        if start == 0:
-            acc_ref[...] = term
-        elif start + step < rows:
-            acc_ref[...] += term
-        else:
-            out_ref[...] = (acc_ref[...] + term).astype(out_ref.dtype)
-
-
-def middle(carried, basis, row_class, linear_table, cubic_table, factor_rho):
+    rows = held_ref.shape[1] - LABEL_ROWS
+    width = held_ref.shape[2]
+    share = pl.ds(pl.multiple_of(lax.axis_index("cblk") * columns, columns), columns)
+    table_ref[0] = in_three(linear_ref[...]).T
+    table_ref[1] = in_three(cubic_ref[...]).T
+    tables = jnp.concatenate([table_ref[0, share, :], table_ref[1, share, :]], axis=0).astype(BF16)
+    step = 2 * width
+    ids = lax.broadcasted_iota(jnp.int32, (classes, step), 0).astype(F32)
+    total = jnp.zeros((columns, width), F32)
+    for at in range(count):
+        copies[at].wait()
+        labels = held_ref[at, pl.ds(rows, LABEL_ROWS), :].astype(F32)
+        for start in range(0, rows, step):
+            basis = held_ref[at, pl.ds(start, step), :]
+            mapped = factor_rho * dot(carried_ref[...], basis, 1, 1)
+            first = start // width
+            label = jnp.concatenate([labels[first : first + 1], labels[first + 1 : first + 2]], axis=1)
+            hot = (ids == label).astype(F32)
+            hot = jnp.concatenate([hot, hot, hot], axis=0).astype(BF16)
+            looked = dot(tables, hot, 1, 0)
+            weighted = mapped * (looked[:columns] + looked[columns:] * mapped * mapped)
+            total += dot(weighted.astype(BF16), basis, 1, 0)
+    out_ref[...] = total
+
+
+def middle(carried, packed, linear_table, cubic_table, factor_rho):
     columns, rank = carried.shape
-    rows = basis.shape[0]
+    count = len(packed)
+    tall = packed[0].shape[0]
 
     def body(*refs):
-        middle_kernel(factor_rho, *refs)
+        middle_kernel(factor_rho, count, *refs)
 
     return pl.pallas_call(
         body,
         name="middle",
-        out_shape=jax.ShapeDtypeStruct((columns, rank), BF16),
-        in_specs=[vmem()] * 5,
+        out_shape=jax.ShapeDtypeStruct((columns, rank), F32),
+        in_specs=[vmem()] * 3 + [pl.BlockSpec(memory_space=pl.ANY)] * count,
         out_specs=vmem(),
-        scratch_shapes=[pltpu.VMEM((columns, rank), F32)],
+        scratch_shapes=[
+            pltpu.VMEM((2, linear_table.shape[1], 3 * linear_table.shape[0]), F32),
+            pltpu.VMEM((count, tall, rank), BF16),
+            pltpu.SemaphoreType.DMA((count,)),
+        ],
         compiler_params=pltpu.CompilerParams(vmem_limit_bytes=VMEM_LIMIT),
-        cost_estimate=cost(8 * rows * columns * rank, 2 * rows * rank),
-    )(carried, basis, row_class.reshape(1, rows), linear_table, cubic_table)
+        cost_estimate=cost(8 * count * tall * columns * rank, 2 * count * tall * rank),
+    )(carried, linear_table, cubic_table, *packed)
 
 
 def expand_kernel(factor_rho, order_ref, returned_ref, basis_ref, out_ref, held_ref, sems):
@@ -283,7 +328,7 @@
 
 def forward_levels(coefficient, factors):
     rank = factors.shape[1]
-    for level in range(2, factors.shape[0]):
+    for level in range(factors.shape[0]):
         partner = from_partner(sent(coefficient, level), "bfly", level)
         coefficient = times(coefficient, factors[level, :, :rank], 1) + times(
             partner, factors[level, :, rank:], 1
@@ -300,29 +345,30 @@
     return coefficient
 
 
+def swapped(array, mask):
+    return lax.ppermute(array, "cblk", [(i, i ^ mask) for i in range(lax.axis_size("cblk"))])
+
+
 def per_device(source, basis, transfer, skeleton, row_class, linear_table, cubic_table):
     factors = transfer[:, 0]
     rank = basis.shape[1]
     shares = lax.axis_size("cblk")
     factor_rho = math.sqrt(source.shape[0] * shares / rank)
-    extra = from_partner(factors[0, :, rank:], "bfly", 1)
-    leaves = leaf_terms(source, basis, skeleton)
+    leaves, packed = leaf_terms(source, basis, skeleton, row_class)
     leaves = shared_out(leaves, "cblk")
     columns = leaves.shape[1]
     whole = jax.ShapeDtypeStruct((columns, rank), F32)
     fours = jax.ShapeDtypeStruct((4, columns, rank), BF16)
     eights = jax.ShapeDtypeStruct((shares, columns, rank), BF16)
 
-    summed = small_call(sum_kernel, whole, leaves)
-    send, own = small_call(up_send_kernel, (fours, whole), summed, factors, extra)
-    low = small_call(up_take_kernel, whole, own, in_fours(send), factors, extra)
-    carried = forward_levels(low, factors).astype(BF16)
-    carried = shared_out(
-        jnp.broadcast_to(carried, eights.shape).reshape(shares * columns, rank), "cblk"
-    ).reshape(shares * columns, rank)
-    back = middle(carried, basis, row_class, linear_table, cubic_table, factor_rho)
-    summed = shared_out(back, "cblk").astype(F32).sum(axis=0)
-    high = adjoint_levels(summed, factors)
+    far = [swapped(packed, mask) for mask in range(2, shares, 2)]
+    near = [swapped(packed, 1)]
+    near += [swapped(array, 1) for array in far]
+    extra = from_partner(factors[0, :, rank:], "bfly", 1)
+
+    carried = forward_levels(leaves.astype(F32).sum(axis=0), factors).astype(BF16)
+    back = middle(carried, [packed, *far, *near], linear_table, cubic_table, factor_rho)
+    high = adjoint_levels(back, factors)
     send, own = small_call(down_send_kernel, (fours, whole), high, factors, extra)
     returned = small_call(down_take_kernel, eights, own, in_fours(send), factors)
     returned = lax.all_to_all(returned, "cblk", split_axis=0, concat_axis=0, tiled=True)

time: 218 us -> 227 us (1.041)
  blocking collectives: 53.2 us -> 25.8 us
  waiting for transfers between devices: 76.9 us -> 93.1 us
  starting transfers between devices: 73.1 us -> 86.3 us
  Pallas kernels: 8.01 us -> 14.4 us
  local copies, waits for them, and re-layouts: 3.67 us -> 0.05 us
  matrix products: 2.66 us -> 5.55 us
    all_to_all x2 -> x0, blocking collectives: 27.6 us -> none  [shared_out(): return lax.all_to_all(blocks, axis, split_axis=0, concat_axis=0, tiled=True)]
    ppermute x0 -> x7, starting transfers between devices: none -> 19.5 us  [swapped(): lax.ppermute(array, 'cblk', [(i, i ^ mask) for i in range(lax.axis_size('...]
    ppermute x0 -> x7, waiting for transfers between devices: none -> 19 us  [swapped(): lax.ppermute(array, 'cblk', [(i, i ^ mask) for i in range(lax.axis_size('...]
    all_to_all x1, blocking collectives: 11 us -> 18.4 us  [per_device(): lax.all_to_all(returned, 'cblk', split_axis=0, concat_axis=0, tiled=True)]
    all_to_all x2 -> x1, blocking collectives: 14.5 us -> 7.34 us  [in_fours(): lax.all_to_all(array, 'bfly', split_axis=0, concat_axis=0, axis_index_gro...]
    ppermute x7 -> x9, starting transfers between devices: 28.3 us -> 21.2 us  [from_partner(): lax.ppermute(array, axis, [(i, i ^ 1 << bit) for i in range(lax.axis_size...]
    pallas_call x1, Pallas kernels: 2.56 us -> 7.85 us  [middle(): pl.pallas_call(body, name='middle', out_shape=jax.ShapeDtypeStruct((colum...]
    all_to_all x1, waiting for transfers between devices: 4.57 us -> 0.01 us  [shared_out(): return lax.all_to_all(blocks, axis, split_axis=0, concat_axis=0, tiled=True)]
  transfers between devices with their start and end apart: 8 -> 17, of which waited for: 8 -> 9; matrix products, arithmetic and copies ran while one was open for 0% -> 2% of each run, Pallas kernels for 0% -> 0%
where the time goes in v3:
time: 227 us
  waiting for transfers between devices  93.1 us (41%)
  starting transfers between devices  86.3 us (38%)
  blocking collectives  25.8 us (11%)
  Pallas kernels  14.4 us (6%)
  matrix products  5.55 us (2%)
    ppermute x9, waiting for transfers between devices, from_partner(): lax.ppermute(array, axis, [(i, i ^ 1 << bit) for i in range(lax.axis_size...  74.1 us
    all_to_all x1, starting transfers between devices, shared_out(): return lax.all_to_all(blocks, axis, split_axis=0, concat_axis=0, tiled=True)  45.5 us
    ppermute x9, starting transfers between devices, from_partner(): lax.ppermute(array, axis, [(i, i ^ 1 << bit) for i in range(lax.axis_size...  21.2 us
    ppermute x7, starting transfers between devices, swapped(): lax.ppermute(array, 'cblk', [(i, i ^ mask) for i in range(lax.axis_size('...  19.5 us
    ppermute x7, waiting for transfers between devices, swapped(): lax.ppermute(array, 'cblk', [(i, i ^ mask) for i in range(lax.axis_size('...  19 us
    all_to_all x1, blocking collectives, per_device(): lax.all_to_all(returned, 'cblk', split_axis=0, concat_axis=0, tiled=True)  18.4 us
    pallas_call x1, Pallas kernels, middle(): pl.pallas_call(body, name='middle', out_shape=jax.ShapeDtypeStruct((colum...  7.85 us
    all_to_all x1, blocking collectives, in_fours(): lax.all_to_all(array, 'bfly', split_axis=0, concat_axis=0, axis_index_gro...  7.34 us
  transfers between devices with their start and end apart: 17, of which 9 were waited for; matrix products, arithmetic and copies ran while one was open for 2% of the time, Pallas kernels for 0%

profile of v3, /device:TPU:33, one launch (start us, length us, event | category | flops | bytes accessed | tf_op | source)
XLA Modules:
  0.0 226.6 jit_solution(174103028496644646)
XLA Ops:
  0.0 3.7 %leaf.1 = (bf16[512,256]{1,0:T(8,128)(2,1)}, bf16[2064,256]{1,0:T(8,128)(2,1)}) custom-call(s32[1,16]{1,0:T(1,128)} %refs_0_.1, s32[1,2048]{1,0:T(1,128)} %bitcast.81, bf16[2048,512]{1,0:T(8,128)(2,1)} %source_hbm.1, bf16[2048,256]{1,0:T(8,128)(2,1)} %refs_2_.3), custom_call_target="tpu_custom_call" | custom-call | flops 536870912 | bytes 3145728 | tf_op jit(solution)/shard_map/leaf/pallas_call | solution.py:102
  3.7 45.5 %all-to-all-start = ((bf16[8,64,256]{2,1,0:T(8,128)(2,1)}), bf16[8,64,256]{2,1,0:T(8,128)(2,1)}, u32[]{:S(2)}, u32[]{:S(2)}) async-start(bf16[8,64,256]{2,1,0:T(8,128)(2,1)} %bitcast.80), calls=%async_computation | async-start | bytes 524288 | tf_op jit(solution)/shard_map/all_to_all | solution.py:310
  49.2 4.9 %collective-permute-start.6 = (bf16[2064,256]{1,0:T(8,128)(2,1)}, bf16[2064,256]{1,0:T(8,128)(2,1)S(1)}, u32[]{:S(2)}, u32[]{:S(2)}) collective-permute-start(bf16[2064,256]{1,0:T(8,128)(2,1)} %get-tuple-element.10.refs_3_), channel_id=1, source_target_pairs={{0,4},{1,5},{2,6},{3,7},{4,0},{5,1},{6,2},{7,3},{8,12},{9,13},{10,... | collective-permute-start | bytes 3170312 | tf_op jit(solution)/shard_map/ppermute | solution.py:349
  54.1 2.8 %collective-permute-start.7 = (bf16[2064,256]{1,0:T(8,128)(2,1)}, bf16[2064,256]{1,0:T(8,128)(2,1)S(1)}, u32[]{:S(2)}, u32[]{:S(2)}) collective-permute-start(bf16[2064,256]{1,0:T(8,128)(2,1)} %get-tuple-element.10.refs_3_), channel_id=1, source_target_pairs={{0,6},{1,7},{2,4},{3,5},{4,2},{5,3},{6,0},{7,1},{8,14},{9,15},{10,... | collective-permute-start | bytes 3170312 | tf_op jit(solution)/shard_map/ppermute | solution.py:349
  56.9 2.0 collective-permute-start.5
  58.8 2.9 %collective-permute-start.8 = (bf16[2064,256]{1,0:T(8,128)(2,1)}, bf16[2064,256]{1,0:T(8,128)(2,1)}, u32[]{:S(2)}, u32[]{:S(2)}) collective-permute-start(bf16[2064,256]{1,0:T(8,128)(2,1)} %get-tuple-element.10.refs_3_), channel_id=1, source_target_pairs={{0,1},{1,0},{2,3},{3,2},{4,5},{5,4},{6,7},{7,6},{8,9},{9,8},{10,11... | collective-permute-start | bytes 3170312 | tf_op jit(solution)/shard_map/ppermute | solution.py:349
  62.7 2.0 collective-permute-start
  64.7 1.2 fusion.2
  65.9 2.4 %collective-permute-done = f32[64,256]{1,0:T(8,128)S(1)} collective-permute-done((f32[64,256]{1,0:T(8,128)S(1)}, f32[64,256]{1,0:T(8,128)S(1)}, u32[]{:S(2)}, u32[]{:S(2)}) %collective-permute-start) | collective-permute-done | bytes 65568 | tf_op jit(solution)/shard_map/ppermute | solution.py:304
  68.3 1.2 convolution_add_fusion.7
  69.5 2.0 collective-permute-start.1
  71.7 5.7 %collective-permute-done.1 = f32[64,256]{1,0:T(8,128)S(1)} collective-permute-done((f32[64,256]{1,0:T(8,128)S(1)}, f32[64,256]{1,0:T(8,128)S(1)}, u32[]{:S(2)}, u32[]{:S(2)}) %collective-permute-start.1) | collective-permute-done | bytes 65568 | tf_op jit(solution)/shard_map/ppermute | solution.py:304
  77.7 2.0 collective-permute-start.2
  80.0 2.7 %collective-permute-start.10 = (bf16[2064,256]{1,0:T(8,128)(2,1)S(1)}, bf16[2064,256]{1,0:T(8,128)(2,1)S(1)}, u32[]{:S(2)}, u32[]{:S(2)}) collective-permute-start(bf16[2064,256]{1,0:T(8,128)(2,1)S(1)} %collective-permute-done.6.refs_5_), channel_id=1, source_target_pairs={{0,1},{1,0},{2,3},{3,2},{4,5},{5,4},{6,7},{7,6},{8,9},{9,8},{10,11... | collective-permute-start | bytes 3170312 | tf_op jit(solution)/shard_map/ppermute | solution.py:349
  82.7 18.9 %collective-permute-done.7.refs_6_ = bf16[2064,256]{1,0:T(8,128)(2,1)S(1)} collective-permute-done((bf16[2064,256]{1,0:T(8,128)(2,1)}, bf16[2064,256]{1,0:T(8,128)(2,1)S(1)}, u32[]{:S(2)}, u32[]{:S(2)}) %collective-permute-start.7) | collective-permute-done | bytes 1056800 | tf_op jit(solution)/shard_map/ppermute | solution.py:349
  101.6 2.4 %collective-permute-start.11 = (bf16[2064,256]{1,0:T(8,128)(2,1)S(1)}, bf16[2064,256]{1,0:T(8,128)(2,1)S(1)}, u32[]{:S(2)}, u32[]{:S(2)}) collective-permute-start(bf16[2064,256]{1,0:T(8,128)(2,1)S(1)} %collective-permute-done.7.refs_6_), channel_id=1, source_target_pairs={{0,1},{1,0},{2,3},{3,2},{4,5},{5,4},{6,7},{7,6},{8,9},{9,8},{10,11... | collective-permute-start | bytes 3170312 | tf_op jit(solution)/shard_map/ppermute | solution.py:349
  104.1 2.0 collective-permute-start.9
  106.3 2.0 collective-permute-start.3
  108.5 11.2 %collective-permute-done.3 = bf16[64,256]{1,0:T(8,128)(2,1)S(1)} collective-permute-done((bf16[64,256]{1,0:T(8,128)(2,1)S(1)}, bf16[64,256]{1,0:T(8,128)(2,1)S(1)}, u32[]{:S(2)}, u32[]{:S(2)}) %collective-permute-start.3) | collective-permute-done | bytes 32800 | tf_op jit(solution)/shard_map/ppermute | solution.py:304
  119.9 3.7 %collective-permute-start.4 = (bf16[64,256]{1,0:T(8,128)(2,1)S(1)}, bf16[64,256]{1,0:T(8,128)(2,1)S(1)}, u32[]{:S(2)}, u32[]{:S(2)}) collective-permute-start(bf16[64,256]{1,0:T(8,128)(2,1)S(1)} %get-tuple-element.15), channel_id=1, source_target_pairs={{0,128},{8,136},{16,144},{24,152},{32,160},{40,168},{48,176},{56,1... | collective-permute-start | bytes 98312 | tf_op jit(solution)/shard_map/ppermute | solution.py:304
  123.8 19.1 %collective-permute-done.4 = bf16[64,256]{1,0:T(8,128)(2,1)S(1)} collective-permute-done((bf16[64,256]{1,0:T(8,128)(2,1)S(1)}, bf16[64,256]{1,0:T(8,128)(2,1)S(1)}, u32[]{:S(2)}, u32[]{:S(2)}) %collective-permute-start.4) | collective-permute-done | bytes 32800 | tf_op jit(solution)/shard_map/ppermute | solution.py:304
  143.2 7.8 %middle.1 = f32[64,256]{1,0:T(8,128)S(1)} custom-call(bf16[64,256]{1,0:T(8,128)(2,1)S(1)} %fusion.refs_0_, f32[16,512]{1,0:T(8,128)S(1)} %copy-done.3, f32[16,512]{1,0:T(8,128)S(1)} %copy-done.4, bf16[2064,256]{1,0:T(8,128)(2,1)S(1)} %copy-done.2, bf16[2064,256]{1,0:T(8,128)(2,1)} %collective-permute-done.5.refs_4_, ...), custom_call_target="tpu_custom_call" | custom-call | flops 2164260864 | bytes 8454144 | tf_op jit(solution)/shard_map/middle/pallas_call | solution.py:243
  151.2 3.7 %collective-permute-start.12 = (bf16[64,256]{1,0:T(8,128)(2,1)S(1)}, bf16[64,256]{1,0:T(8,128)(2,1)S(1)}, u32[]{:S(2)}, u32[]{:S(2)}) collective-permute-start(bf16[64,256]{1,0:T(8,128)(2,1)S(1)} %convolution_convert_fusion.1), channel_id=1, source_target_pairs={{0,128},{8,136},{16,144},{24,152},{32,160},{40,168},{48,176},{56,1... | collective-permute-start | bytes 98312 | tf_op jit(solution)/shard_map/ppermute | solution.py:304
  154.9 19.3 %collective-permute-done.12 = bf16[64,256]{1,0:T(8,128)(2,1)S(1)} collective-permute-done((bf16[64,256]{1,0:T(8,128)(2,1)S(1)}, bf16[64,256]{1,0:T(8,128)(2,1)S(1)}, u32[]{:S(2)}, u32[]{:S(2)}) %collective-permute-start.12) | collective-permute-done | bytes 32800 | tf_op jit(solution)/shard_map/ppermute | solution.py:304
  174.7 2.2 collective-permute-start.13
  176.9 11.3 %collective-permute-done.13 = bf16[64,256]{1,0:T(8,128)(2,1)S(1)} collective-permute-done((bf16[64,256]{1,0:T(8,128)(2,1)S(1)}, bf16[64,256]{1,0:T(8,128)(2,1)S(1)}, u32[]{:S(2)}, u32[]{:S(2)}) %collective-permute-start.13) | collective-permute-done | bytes 32800 | tf_op jit(solution)/shard_map/ppermute | solution.py:304
  188.6 2.0 collective-permute-start.14
  190.6 2.0 collective-permute-start.15
  192.6 5.1 %collective-permute-done.14 = f32[64,256]{1,0:T(8,128)S(1)} collective-permute-done((f32[64,256]{1,0:T(8,128)S(1)}, f32[64,256]{1,0:T(8,128)S(1)}, u32[]{:S(2)}, u32[]{:S(2)}) %collective-permute-start.14) | collective-permute-done | bytes 65568 | tf_op jit(solution)/shard_map/ppermute | solution.py:304
  198.3 7.3 %all_to_all.15.arrived_ref = bf16[4,64,256]{2,1,0:T(8,128)(2,1)S(1)} all-to-all(bf16[4,64,256]{2,1,0:T(8,128)(2,1)S(1)} %get-tuple-element.12), channel_id=1, replica_groups={{0,8,16,24},{32,40,48,56},{64,72,80,88},{96,104,112,120},{128,136,144,1..., dimensions={0} | all-to-all | bytes 262144 | tf_op jit(solution)/shard_map/all_to_all | solution.py:186
  205.8 18.4 %all_to_all.16 = bf16[8,64,256]{2,1,0:T(8,128)(2,1)S(1)} all-to-all(bf16[8,64,256]{2,1,0:T(8,128)(2,1)S(1)} %shard_map.74), channel_id=1, replica_groups=mesh['ens'=2,'bfly'=32,'cblk'=8] {'cblk'}, dimensions={0} | all-to-all | bytes 524288 | tf_op jit(solution)/shard_map/all_to_all | solution.py:374
  224.3 2.3 %expand.1 = bf16[2048,512]{1,0:T(8,128)(2,1)} custom-call(s32[1,16]{1,0:T(1,128)S(1)} %copy-done.5, bf16[512,256]{1,0:T(8,128)(2,1)S(1)} %bitcast.79, bf16[2048,256]{1,0:T(8,128)(2,1)S(1)} %copy-done.1), custom_call_target="tpu_custom_call" | custom-call | flops 536870912 | bytes 3145728 | tf_op jit(solution)/shard_map/expand/pallas_call | solution.py:291
  (39 shorter events, 4.8 us)
Async XLA Ops:
  3.7 67.7 %copy-start = (bf16[5,1,256,512]{3,2,1,0:T(8,128)(2,1)S(1)}, bf16[5,1,256,512]{3,2,1,0:T(8,128)(2,1)}, u32[]{:S(2)}) copy-start(bf16[5,1,256,512]{3,2,1,0:T(8,128)(2,1)} %param.9) | copy-start | bytes 3932164
  3.7 58.0 %all-to-all-start = ((bf16[8,64,256]{2,1,0:T(8,128)(2,1)}), bf16[8,64,256]{2,1,0:T(8,128)(2,1)}, u32[]{:S(2)}, u32[]{:S(2)}) async-start(bf16[8,64,256]{2,1,0:T(8,128)(2,1)} %bitcast.80), calls=%async_computation | async-start | bytes 524288 | tf_op jit(solution)/shard_map/all_to_all | solution.py:310
  49.2 30.8 %collective-permute-start.6 = (bf16[2064,256]{1,0:T(8,128)(2,1)}, bf16[2064,256]{1,0:T(8,128)(2,1)S(1)}, u32[]{:S(2)}, u32[]{:S(2)}) collective-permute-start(bf16[2064,256]{1,0:T(8,128)(2,1)} %get-tuple-element.10.refs_3_), channel_id=1, source_target_pairs={{0,4},{1,5},{2,6},{3,7},{4,0},{5,1},{6,2},{7,3},{8,12},{9,13},{10,... | collective-permute-start | bytes 3170312 | tf_op jit(solution)/shard_map/ppermute | solution.py:349
  54.1 47.5 %collective-permute-start.7 = (bf16[2064,256]{1,0:T(8,128)(2,1)}, bf16[2064,256]{1,0:T(8,128)(2,1)S(1)}, u32[]{:S(2)}, u32[]{:S(2)}) collective-permute-start(bf16[2064,256]{1,0:T(8,128)(2,1)} %get-tuple-element.10.refs_3_), channel_id=1, source_target_pairs={{0,6},{1,7},{2,4},{3,5},{4,2},{5,3},{6,0},{7,1},{8,14},{9,15},{10,... | collective-permute-start | bytes 3170312 | tf_op jit(solution)/shard_map/ppermute | solution.py:349
  56.9 47.2 %collective-permute-start.5 = (bf16[2064,256]{1,0:T(8,128)(2,1)}, bf16[2064,256]{1,0:T(8,128)(2,1)}, u32[]{:S(2)}, u32[]{:S(2)}) collective-permute-start(bf16[2064,256]{1,0:T(8,128)(2,1)} %get-tuple-element.10.refs_3_), channel_id=1, source_target_pairs={{0,2},{1,3},{2,0},{3,1},{4,6},{5,7},{6,4},{7,5},{8,10},{9,11},{10,... | collective-permute-start | bytes 3170312 | tf_op jit(solution)/shard_map/ppermute | solution.py:349
  58.8 84.2 %collective-permute-start.8 = (bf16[2064,256]{1,0:T(8,128)(2,1)}, bf16[2064,256]{1,0:T(8,128)(2,1)}, u32[]{:S(2)}, u32[]{:S(2)}) collective-permute-start(bf16[2064,256]{1,0:T(8,128)(2,1)} %get-tuple-element.10.refs_3_), channel_id=1, source_target_pairs={{0,1},{1,0},{2,3},{3,2},{4,5},{5,4},{6,7},{7,6},{8,9},{9,8},{10,11... | collective-permute-start | bytes 3170312 | tf_op jit(solution)/shard_map/ppermute | solution.py:349
  62.7 5.6 %collective-permute-start = (f32[64,256]{1,0:T(8,128)S(1)}, f32[64,256]{1,0:T(8,128)S(1)}, u32[]{:S(2)}, u32[]{:S(2)}) collective-permute-start(f32[64,256]{1,0:T(8,128)S(1)} %convert_reduce_fusion), channel_id=1, source_target_pairs={{0,8},{8,0},{16,24},{24,16},{32,40},{40,32},{48,56},{56,48},{64,72... | collective-permute-start | bytes 196616 | tf_op jit(solution)/shard_map/ppermute | solution.py:304
  65.9 77.3 %copy-start.2 = (bf16[2064,256]{1,0:T(8,128)(2,1)S(1)}, bf16[2064,256]{1,0:T(8,128)(2,1)}, u32[]{:S(2)}) copy-start(bf16[2064,256]{1,0:T(8,128)(2,1)} %get-tuple-element.10.refs_3_) | copy-start | bytes 3170308
  65.9 77.3 %copy-start.3 = (f32[16,512]{1,0:T(8,128)S(1)}, f32[16,512]{1,0:T(8,128)}, u32[]{:S(2)}) copy-start(f32[16,512]{1,0:T(8,128)} %refs_1_.1) | copy-start | bytes 98308
  65.9 77.3 %copy-start.4 = (f32[16,512]{1,0:T(8,128)S(1)}, f32[16,512]{1,0:T(8,128)}, u32[]{:S(2)}) copy-start(f32[16,512]{1,0:T(8,128)} %refs_2_.2) | copy-start | bytes 98308
  69.5 8.0 %collective-permute-start.1 = (f32[64,256]{1,0:T(8,128)S(1)}, f32[64,256]{1,0:T(8,128)S(1)}, u32[]{:S(2)}, u32[]{:S(2)}) collective-permute-start(f32[64,256]{1,0:T(8,128)S(1)} %convolution_add_fusion.7), channel_id=1, source_target_pairs={{0,16},{8,24},{16,0},{24,8},{32,48},{40,56},{48,32},{56,40},{64,80... | collective-permute-start | bytes 196616 | tf_op jit(solution)/shard_map/ppermute | solution.py:304
  77.7 28.3 %collective-permute-start.2 = (f32[64,256]{1,0:T(8,128)S(1)}, f32[64,256]{1,0:T(8,128)S(1)}, u32[]{:S(2)}, u32[]{:S(2)}) collective-permute-start(f32[64,256]{1,0:T(8,128)S(1)} %convolution_add_fusion.6), channel_id=1, source_target_pairs={{0,32},{8,40},{16,48},{24,56},{32,0},{40,8},{48,16},{56,24},{64,96... | collective-permute-start | bytes 196616 | tf_op jit(solution)/shard_map/ppermute | solution.py:304
  80.0 63.1 %collective-permute-start.10 = (bf16[2064,256]{1,0:T(8,128)(2,1)S(1)}, bf16[2064,256]{1,0:T(8,128)(2,1)S(1)}, u32[]{:S(2)}, u32[]{:S(2)}) collective-permute-start(bf16[2064,256]{1,0:T(8,128)(2,1)S(1)} %collective-permute-done.6.refs_5_), channel_id=1, source_target_pairs={{0,1},{1,0},{2,3},{3,2},{4,5},{5,4},{6,7},{7,6},{8,9},{9,8},{10,11... | collective-permute-start | bytes 3170312 | tf_op jit(solution)/shard_map/ppermute | solution.py:349
  101.6 41.5 %collective-permute-start.11 = (bf16[2064,256]{1,0:T(8,128)(2,1)S(1)}, bf16[2064,256]{1,0:T(8,128)(2,1)S(1)}, u32[]{:S(2)}, u32[]{:S(2)}) collective-permute-start(bf16[2064,256]{1,0:T(8,128)(2,1)S(1)} %collective-permute-done.7.refs_6_), channel_id=1, source_target_pairs={{0,1},{1,0},{2,3},{3,2},{4,5},{5,4},{6,7},{7,6},{8,9},{9,8},{10,11... | collective-permute-start | bytes 3170312 | tf_op jit(solution)/shard_map/ppermute | solution.py:349
  104.1 39.1 %collective-permute-start.9 = (bf16[2064,256]{1,0:T(8,128)(2,1)}, bf16[2064,256]{1,0:T(8,128)(2,1)S(1)}, u32[]{:S(2)}, u32[]{:S(2)}) collective-permute-start(bf16[2064,256]{1,0:T(8,128)(2,1)} %collective-permute-done.5.refs_4_), channel_id=1, source_target_pairs={{0,1},{1,0},{2,3},{3,2},{4,5},{5,4},{6,7},{7,6},{8,9},{9,8},{10,11... | collective-permute-start | bytes 3170312 | tf_op jit(solution)/shard_map/ppermute | solution.py:349
  106.3 13.4 %collective-permute-start.3 = (bf16[64,256]{1,0:T(8,128)(2,1)S(1)}, bf16[64,256]{1,0:T(8,128)(2,1)S(1)}, u32[]{:S(2)}, u32[]{:S(2)}) collective-permute-start(bf16[64,256]{1,0:T(8,128)(2,1)S(1)} %get-tuple-element.13), channel_id=1, source_target_pairs={{0,64},{8,72},{16,80},{24,88},{32,96},{40,104},{48,112},{56,120},{... | collective-permute-start | bytes 98312 | tf_op jit(solution)/shard_map/ppermute | solution.py:304
  119.9 23.0 %collective-permute-start.4 = (bf16[64,256]{1,0:T(8,128)(2,1)S(1)}, bf16[64,256]{1,0:T(8,128)(2,1)S(1)}, u32[]{:S(2)}, u32[]{:S(2)}) collective-permute-start(bf16[64,256]{1,0:T(8,128)(2,1)S(1)} %get-tuple-element.15), channel_id=1, source_target_pairs={{0,128},{8,136},{16,144},{24,152},{32,160},{40,168},{48,176},{56,1... | collective-permute-start | bytes 98312 | tf_op jit(solution)/shard_map/ppermute | solution.py:304
  151.2 23.0 %collective-permute-start.12 = (bf16[64,256]{1,0:T(8,128)(2,1)S(1)}, bf16[64,256]{1,0:T(8,128)(2,1)S(1)}, u32[]{:S(2)}, u32[]{:S(2)}) collective-permute-start(bf16[64,256]{1,0:T(8,128)(2,1)S(1)} %convolution_convert_fusion.1), channel_id=1, source_target_pairs={{0,128},{8,136},{16,144},{24,152},{32,160},{40,168},{48,176},{56,1... | collective-permute-start | bytes 98312 | tf_op jit(solution)/shard_map/ppermute | solution.py:304
  174.7 13.5 %collective-permute-start.13 = (bf16[64,256]{1,0:T(8,128)(2,1)S(1)}, bf16[64,256]{1,0:T(8,128)(2,1)S(1)}, u32[]{:S(2)}, u32[]{:S(2)}) collective-permute-start(bf16[64,256]{1,0:T(8,128)(2,1)S(1)} %convolution_convert_fusion), channel_id=1, source_target_pairs={{0,64},{8,72},{16,80},{24,88},{32,96},{40,104},{48,112},{56,120},{... | collective-permute-start | bytes 98312 | tf_op jit(solution)/shard_map/ppermute | solution.py:304
  188.6 9.0 %collective-permute-start.14 = (f32[64,256]{1,0:T(8,128)S(1)}, f32[64,256]{1,0:T(8,128)S(1)}, u32[]{:S(2)}, u32[]{:S(2)}) collective-permute-start(f32[64,256]{1,0:T(8,128)S(1)} %fusion.4), channel_id=1, source_target_pairs={{0,32},{8,40},{16,48},{24,56},{32,0},{40,8},{48,16},{56,24},{64,96... | collective-permute-start | bytes 196616 | tf_op jit(solution)/shard_map/ppermute | solution.py:304
  190.6 7.3 %collective-permute-start.15 = (bf16[256,256]{1,0:T(8,128)(2,1)S(1)}, bf16[256,256]{1,0:T(8,128)(2,1)S(1)}, u32[]{:S(2)}, u32[]{:S(2)}) collective-permute-start(bf16[256,256]{1,0:T(8,128)(2,1)S(1)} %slice_bitcast_fusion.10), channel_id=1, source_target_pairs={{0,16},{8,24},{16,0},{24,8},{32,48},{40,56},{48,32},{56,40},{64,80... | collective-permute-start | bytes 393224 | tf_op jit(solution)/shard_map/ppermute | solution.py:304
  198.3 26.0 %copy-start.1 = (bf16[2048,256]{1,0:T(8,128)(2,1)S(1)}, bf16[2048,256]{1,0:T(8,128)(2,1)}, u32[]{:S(2)}) copy-start(bf16[2048,256]{1,0:T(8,128)(2,1)} %refs_2_.3) | copy-start | bytes 3145732
  198.3 26.0 %copy-start.5 = (s32[1,16]{1,0:T(1,128)S(1)}, s32[1,16]{1,0:T(1,128)}, u32[]{:S(2)}) copy-start(s32[1,16]{1,0:T(1,128)} %refs_0_.1) | copy-start | bytes 196

commit v4 on v3

--- a/solution.py
+++ b/solution.py
@@ -11,7 +11,7 @@
 F32 = jnp.float32
 BF16 = jnp.bfloat16
 VMEM_LIMIT = 24 * 1024 * 1024
-LEAF_LIMIT = 66_200_000
+LEAF_LIMIT = 65600000
 LABEL_ROWS = 16
 
 
@@ -46,51 +46,64 @@
     packed_hbm,
     acc_ref,
     order_ref,
+    place_ref,
     class_ref,
     source_ref,
     basis_ref,
     label_ref,
     sems,
+    source_sems,
 ):
     rows = source_ref.shape[0]
-    basis_in = pltpu.make_async_copy(basis_hbm, basis_ref, sems.at[0])
-    source_in = pltpu.make_async_copy(source_hbm, source_ref, sems.at[1])
-    order_in = pltpu.make_async_copy(order_hbm, order_ref, sems.at[2])
-    class_in = pltpu.make_async_copy(class_hbm, class_ref, sems.at[3])
-    for copy in (order_in, class_in, basis_in, source_in):
-        copy.start()
-    class_in.wait()
-    width = label_ref.shape[1]
-    label = [class_ref[:, pl.ds(at, width)].astype(F32) for at in range(0, rows, width)]
-    label.append(jnp.zeros((label_ref.shape[0] - len(label), width), F32))
-    label_ref[...] = jnp.concatenate(label, axis=0).astype(label_ref.dtype)
-    basis_in.wait()
-    basis_out = pltpu.make_async_copy(basis_ref, packed_hbm.at[pl.ds(0, rows), :], sems.at[4])
-    basis_out.start()
-    order_in.wait()
-    source_in.wait()
-    label_out = pltpu.make_async_copy(
-        label_ref, packed_hbm.at[pl.ds(rows, label_ref.shape[0]), :], sems.at[5]
-    )
-    label_out.start()
     tiles = order_ref.shape[1]
     tile = rows // tiles
     step = 4
+    order_in = pltpu.make_async_copy(order_hbm, order_ref, sems.at[0])
+    basis_in = pltpu.make_async_copy(basis_hbm, basis_ref, sems.at[1])
+    source_in = [
+        pltpu.make_async_copy(
+            source_hbm.at[pl.ds(at * tile, step * tile), :],
+            source_ref.at[pl.ds(at * tile, step * tile), :],
+            source_sems.at[at // step],
+        )
+        for at in range(0, tiles, step)
+    ]
+    class_in = pltpu.make_async_copy(class_hbm, class_ref, sems.at[2])
+    for copy in (order_in, basis_in, *source_in, class_in):
+        copy.start()
+    order_in.wait()
+    for i in range(tiles):
+        place_ref[order_ref[0, i]] = i
+    basis_in.wait()
+    basis_out = pltpu.make_async_copy(basis_ref, packed_hbm.at[pl.ds(0, rows), :], sems.at[3])
+    basis_out.start()
     for start in range(0, tiles, step):
-        picked = jnp.concatenate(
+        source_in[start // step].wait()
+        matched = jnp.concatenate(
             [
-                source_ref[pl.ds(pl.multiple_of(order_ref[0, start + i] * tile, tile), tile), :]
+                basis_ref[pl.ds(pl.multiple_of(place_ref[start + i] * tile, tile), tile), :]
                 for i in range(step)
             ],
             axis=0,
         )
-        term = dot(picked, basis_ref[pl.ds(start * tile, step * tile), :], 0, 0)
+        term = dot(source_ref[pl.ds(start * tile, step * tile), :], matched, 0, 0)
         if start == 0:
             acc_ref[...] = term
         elif start + step < tiles:
             acc_ref[...] += term
         else:
             out_ref[...] = (acc_ref[...] + term).astype(out_ref.dtype)
+        if start == 0:
+            class_in.wait()
+            width = label_ref.shape[1]
+            label = [class_ref[:, pl.ds(at, width)].astype(F32) for at in range(0, rows, width)]
+            label.append(jnp.zeros((label_ref.shape[0] - len(label), width), F32))
+            label_ref[...] = jnp.concatenate(label, axis=0).astype(label_ref.dtype)
+        elif start == step:
+            label_out = pltpu.make_async_copy(
+                label_ref, packed_hbm.at[pl.ds(rows, label_ref.shape[0]), :], sems.at[4]
+            )
+            label_out.start()
     basis_out.wait()
     label_out.wait()
 
@@ -111,11 +124,13 @@
         scratch_shapes=[
             pltpu.VMEM((columns, rank), F32),
             pltpu.SMEM(skeleton.shape, jnp.int32),
+            pltpu.SMEM((skeleton.shape[1],), jnp.int32),
             pltpu.VMEM((1, rows), jnp.int32),
             pltpu.VMEM(source.shape, source.dtype),
             pltpu.VMEM(basis.shape, basis.dtype),
             pltpu.VMEM((labels, rank), BF16),
-            pltpu.SemaphoreType.DMA((6,)),
+            pltpu.SemaphoreType.DMA((5,)),
+            pltpu.SemaphoreType.DMA((skeleton.shape[1] // 4,)),
         ],
         compiler_params=pltpu.CompilerParams(vmem_limit_bytes=LEAF_LIMIT),
         cost_estimate=cost(2 * rows * columns * rank, 2 * rows * (columns + rank)),
@@ -199,28 +214,26 @@
 def middle_kernel(factor_rho, count, *refs):
     carried_ref, linear_ref, cubic_ref = refs[:3]
     packed = refs[3 : 3 + count]
-    out_ref, table_ref, held_ref, sems = refs[3 + count :]
-    copies = [
-        pltpu.make_async_copy(packed[at], held_ref.at[at], sems.at[at]) for at in range(count)
-    ]
-    for copy in copies:
-        copy.start()
+    out_ref, table_ref = refs[3 + count :]
     columns = carried_ref.shape[0]
     classes = linear_ref.shape[0]
-    rows = held_ref.shape[1] - LABEL_ROWS
-    width = held_ref.shape[2]
-    share = pl.ds(pl.multiple_of(lax.axis_index("cblk") * columns, columns), columns)
-    table_ref[0] = in_three(linear_ref[...]).T
-    table_ref[1] = in_three(cubic_ref[...]).T
+    rows = packed[0].shape[0] - LABEL_ROWS
+    width = packed[0].shape[1]
+    lanes = table_ref.shape[1]
+    shares = lanes // columns
+    mine = lax.axis_index("cblk")
+    wide = pl.ds(pl.multiple_of(mine // shares * lanes, lanes), lanes)
+    share = pl.ds(pl.multiple_of(lax.rem(mine, shares) * columns, columns), columns)
+    table_ref[0] = in_three(linear_ref[:, wide]).T
+    table_ref[1] = in_three(cubic_ref[:, wide]).T
     tables = jnp.concatenate([table_ref[0, share, :], table_ref[1, share, :]], axis=0).astype(BF16)
     step = 2 * width
     ids = lax.broadcasted_iota(jnp.int32, (classes, step), 0).astype(F32)
     total = jnp.zeros((columns, width), F32)
-    for at in range(count):
-        copies[at].wait()
-        labels = held_ref[at, pl.ds(rows, LABEL_ROWS), :].astype(F32)
+    for ref in packed:
+        labels = ref[pl.ds(rows, LABEL_ROWS), :].astype(F32)
         for start in range(0, rows, step):
-            basis = held_ref[at, pl.ds(start, step), :]
+            basis = ref[pl.ds(start, step), :]
             mapped = factor_rho * dot(carried_ref[...], basis, 1, 1)
             first = start // width
             label = jnp.concatenate([labels[first : first + 1], labels[first + 1 : first + 2]], axis=1)
@@ -244,13 +257,9 @@
         body,
         name="middle",
         out_shape=jax.ShapeDtypeStruct((columns, rank), F32),
-        in_specs=[vmem()] * 3 + [pl.BlockSpec(memory_space=pl.ANY)] * count,
+        in_specs=[vmem()] * (3 + count),
         out_specs=vmem(),
-        scratch_shapes=[
-            pltpu.VMEM((2, linear_table.shape[1], 3 * linear_table.shape[0]), F32),
-            pltpu.VMEM((count, tall, rank), BF16),
-            pltpu.SemaphoreType.DMA((count,)),
-        ],
+        scratch_shapes=[pltpu.VMEM((2, max(columns, 128), 3 * linear_table.shape[0]), F32)],
         compiler_params=pltpu.CompilerParams(vmem_limit_bytes=VMEM_LIMIT),
         cost_estimate=cost(8 * count * tall * columns * rank, 2 * count * tall * rank),
     )(carried, linear_table, cubic_table, *packed)
@@ -323,16 +332,15 @@
 
 
 def sent(array, level):
-    return array.astype(BF16) if level >= 3 else array
+    return array.astype(BF16) if level >= 2 else array
 
 
 def forward_levels(coefficient, factors):
     rank = factors.shape[1]
     for level in range(factors.shape[0]):
         partner = from_partner(sent(coefficient, level), "bfly", level)
-        coefficient = times(coefficient, factors[level, :, :rank], 1) + times(
-            partner, factors[level, :, rank:], 1
-        )
+        own = times(coefficient, factors[level, :, :rank], 1)
+        coefficient = own + times(partner, factors[level, :, rank:], 1)
     return coefficient
 
 

time: 227 us -> 228 us (level)
    dot_general x14 -> x13, matrix products: 5.24 us -> 3.15 us  [times(): lax.dot_general(left, right.astype(F32), (((1,), (right_dim,)), ((), ()))...]
where the time goes in v4:
time: 228 us; the launch traced here: 227 us
  waiting for transfers between devices  94.4 us (41%)
  starting transfers between devices  86.3 us (38%)
  blocking collectives  25.7 us (11%)
  Pallas kernels  15.2 us (7%)
  matrix products  3.62 us (2%)
    ppermute x9, waiting for transfers between devices, from_partner(): lax.ppermute(array, axis, [(i, i ^ 1 << bit) for i in range(lax.axis_size...  74.7 us
    all_to_all x1, starting transfers between devices, shared_out(): return lax.all_to_all(blocks, axis, split_axis=0, concat_axis=0, tiled=True)  45.4 us
    ppermute x9, starting transfers between devices, from_partner(): lax.ppermute(array, axis, [(i, i ^ 1 << bit) for i in range(lax.axis_size...  21.2 us
    ppermute x7, starting transfers between devices, swapped(): lax.ppermute(array, 'cblk', [(i, i ^ mask) for i in range(lax.axis_size('...  19.7 us
    ppermute x7, waiting for transfers between devices, swapped(): lax.ppermute(array, 'cblk', [(i, i ^ mask) for i in range(lax.axis_size('...  19.7 us
    all_to_all x1, blocking collectives, per_device(): lax.all_to_all(returned, 'cblk', split_axis=0, concat_axis=0, tiled=True)  18.4 us
    pallas_call x1, Pallas kernels, middle(): pl.pallas_call(body, name='middle', out_shape=jax.ShapeDtypeStruct((colum...  8.41 us
    all_to_all x1, blocking collectives, in_fours(): lax.all_to_all(array, 'bfly', split_axis=0, concat_axis=0, axis_index_gro...  7.34 us
  transfers between devices with their start and end apart: 17, of which 9 were waited for; matrix products, arithmetic and copies ran while one was open for 2% of the time, Pallas kernels for 0%

profile of v4, /device:TPU:33, one launch (start us, length us, event | category | flops | bytes accessed | tf_op | source)
XLA Modules:
  0.0 226.8 jit_solution(16026451959321278161)
XLA Ops:
  0.0 4.0 %leaf.1 = (bf16[512,256]{1,0:T(8,128)(2,1)}, bf16[2064,256]{1,0:T(8,128)(2,1)}) custom-call(s32[1,16]{1,0:T(1,128)} %refs_0_.1, s32[1,2048]{1,0:T(1,128)} %bitcast.83, bf16[2048,512]{1,0:T(8,128)(2,1)} %source_hbm.1, bf16[2048,256]{1,0:T(8,128)(2,1)} %refs_2_.3), custom_call_target="tpu_custom_call" | custom-call | flops 536870912 | bytes 3145728 | tf_op jit(solution)/shard_map/leaf/pallas_call | solution.py:115
  4.0 45.4 %all-to-all-start = ((bf16[8,64,256]{2,1,0:T(8,128)(2,1)}), bf16[8,64,256]{2,1,0:T(8,128)(2,1)}, u32[]{:S(2)}, u32[]{:S(2)}) async-start(bf16[8,64,256]{2,1,0:T(8,128)(2,1)} %bitcast.82), calls=%async_computation | async-start | bytes 524288 | tf_op jit(solution)/shard_map/all_to_all | solution.py:319
  49.4 4.9 %collective-permute-start.6 = (bf16[2064,256]{1,0:T(8,128)(2,1)}, bf16[2064,256]{1,0:T(8,128)(2,1)S(1)}, u32[]{:S(2)}, u32[]{:S(2)}) collective-permute-start(bf16[2064,256]{1,0:T(8,128)(2,1)} %get-tuple-element.10.refs_3_), channel_id=1, source_target_pairs={{0,4},{1,5},{2,6},{3,7},{4,0},{5,1},{6,2},{7,3},{8,12},{9,13},{10,... | collective-permute-start | bytes 3170312 | tf_op jit(solution)/shard_map/ppermute | solution.py:357
  54.2 2.8 %collective-permute-start.7 = (bf16[2064,256]{1,0:T(8,128)(2,1)}, bf16[2064,256]{1,0:T(8,128)(2,1)S(1)}, u32[]{:S(2)}, u32[]{:S(2)}) collective-permute-start(bf16[2064,256]{1,0:T(8,128)(2,1)} %get-tuple-element.10.refs_3_), channel_id=1, source_target_pairs={{0,6},{1,7},{2,4},{3,5},{4,2},{5,3},{6,0},{7,1},{8,14},{9,15},{10,... | collective-permute-start | bytes 3170312 | tf_op jit(solution)/shard_map/ppermute | solution.py:357
  57.0 2.0 collective-permute-start.5
  59.0 2.9 %collective-permute-start.8 = (bf16[2064,256]{1,0:T(8,128)(2,1)}, bf16[2064,256]{1,0:T(8,128)(2,1)}, u32[]{:S(2)}, u32[]{:S(2)}) collective-permute-start(bf16[2064,256]{1,0:T(8,128)(2,1)} %get-tuple-element.10.refs_3_), channel_id=1, source_target_pairs={{0,1},{1,0},{2,3},{3,2},{4,5},{5,4},{6,7},{7,6},{8,9},{9,8},{10,11... | collective-permute-start | bytes 3170312 | tf_op jit(solution)/shard_map/ppermute | solution.py:357
  61.9 1.0 convert_reduce_fusion
  62.9 2.0 collective-permute-start
  65.2 3.3 %collective-permute-done = f32[64,256]{1,0:T(8,128)S(1)} collective-permute-done((f32[64,256]{1,0:T(8,128)S(1)}, f32[64,256]{1,0:T(8,128)S(1)}, u32[]{:S(2)}, u32[]{:S(2)}) %collective-permute-start) | collective-permute-done | bytes 65568 | tf_op jit(solution)/shard_map/ppermute | solution.py:313
  68.7 2.0 collective-permute-start.1
  71.0 5.7 %collective-permute-done.1 = f32[64,256]{1,0:T(8,128)S(1)} collective-permute-done((f32[64,256]{1,0:T(8,128)S(1)}, f32[64,256]{1,0:T(8,128)S(1)}, u32[]{:S(2)}, u32[]{:S(2)}) %collective-permute-start.1) | collective-permute-done | bytes 65568 | tf_op jit(solution)/shard_map/ppermute | solution.py:313
  77.0 2.0 collective-permute-start.2
  79.2 2.9 %collective-permute-start.10 = (bf16[2064,256]{1,0:T(8,128)(2,1)S(1)}, bf16[2064,256]{1,0:T(8,128)(2,1)S(1)}, u32[]{:S(2)}, u32[]{:S(2)}) collective-permute-start(bf16[2064,256]{1,0:T(8,128)(2,1)S(1)} %collective-permute-done.6.refs_5_), channel_id=1, source_target_pairs={{0,1},{1,0},{2,3},{3,2},{4,5},{5,4},{6,7},{7,6},{8,9},{9,8},{10,11... | collective-permute-start | bytes 3170312 | tf_op jit(solution)/shard_map/ppermute | solution.py:357
  82.1 19.6 %collective-permute-done.7.refs_6_ = bf16[2064,256]{1,0:T(8,128)(2,1)S(1)} collective-permute-done((bf16[2064,256]{1,0:T(8,128)(2,1)}, bf16[2064,256]{1,0:T(8,128)(2,1)S(1)}, u32[]{:S(2)}, u32[]{:S(2)}) %collective-permute-start.7) | collective-permute-done | bytes 1056800 | tf_op jit(solution)/shard_map/ppermute | solution.py:357
  101.8 2.4 %collective-permute-start.11 = (bf16[2064,256]{1,0:T(8,128)(2,1)S(1)}, bf16[2064,256]{1,0:T(8,128)(2,1)S(1)}, u32[]{:S(2)}, u32[]{:S(2)}) collective-permute-start(bf16[2064,256]{1,0:T(8,128)(2,1)S(1)} %collective-permute-done.7.refs_6_), channel_id=1, source_target_pairs={{0,1},{1,0},{2,3},{3,2},{4,5},{5,4},{6,7},{7,6},{8,9},{9,8},{10,11... | collective-permute-start | bytes 3170312 | tf_op jit(solution)/shard_map/ppermute | solution.py:357
  104.2 2.0 collective-permute-start.9
  106.4 2.0 collective-permute-start.3
  108.6 11.2 %collective-permute-done.3 = bf16[64,256]{1,0:T(8,128)(2,1)S(1)} collective-permute-done((bf16[64,256]{1,0:T(8,128)(2,1)S(1)}, bf16[64,256]{1,0:T(8,128)(2,1)S(1)}, u32[]{:S(2)}, u32[]{:S(2)}) %collective-permute-start.3) | collective-permute-done | bytes 32800 | tf_op jit(solution)/shard_map/ppermute | solution.py:313
  120.0 3.7 %collective-permute-start.4 = (bf16[64,256]{1,0:T(8,128)(2,1)S(1)}, bf16[64,256]{1,0:T(8,128)(2,1)S(1)}, u32[]{:S(2)}, u32[]{:S(2)}) collective-permute-start(bf16[64,256]{1,0:T(8,128)(2,1)S(1)} %get-tuple-element.17), channel_id=1, source_target_pairs={{0,128},{8,136},{16,144},{24,152},{32,160},{40,168},{48,176},{56,1... | collective-permute-start | bytes 98312 | tf_op jit(solution)/shard_map/ppermute | solution.py:313
  123.9 19.1 %collective-permute-done.4 = bf16[64,256]{1,0:T(8,128)(2,1)S(1)} collective-permute-done((bf16[64,256]{1,0:T(8,128)(2,1)S(1)}, bf16[64,256]{1,0:T(8,128)(2,1)S(1)}, u32[]{:S(2)}, u32[]{:S(2)}) %collective-permute-start.4) | collective-permute-done | bytes 32800 | tf_op jit(solution)/shard_map/ppermute | solution.py:313
  143.2 8.4 %middle.1 = f32[64,256]{1,0:T(8,128)S(1)} custom-call(bf16[64,256]{1,0:T(8,128)(2,1)S(1)} %fusion.refs_0_, f32[16,512]{1,0:T(8,128)S(1)} %copy-done.3, f32[16,512]{1,0:T(8,128)S(1)} %copy-done.4, bf16[2064,256]{1,0:T(8,128)(2,1)S(1)} %copy-done.2, bf16[2064,256]{1,0:T(8,128)(2,1)} %collective-permute-done.5.refs_4_, ...), custom_call_target="tpu_custom_call" | custom-call | flops 2164260864 | bytes 8454144 | tf_op jit(solution)/shard_map/middle/pallas_call | solution.py:256
  151.8 3.7 %collective-permute-start.12 = (bf16[64,256]{1,0:T(8,128)(2,1)S(1)}, bf16[64,256]{1,0:T(8,128)(2,1)S(1)}, u32[]{:S(2)}, u32[]{:S(2)}) collective-permute-start(bf16[64,256]{1,0:T(8,128)(2,1)S(1)} %convolution_convert_fusion.2), channel_id=1, source_target_pairs={{0,128},{8,136},{16,144},{24,152},{32,160},{40,168},{48,176},{56,1... | collective-permute-start | bytes 98312 | tf_op jit(solution)/shard_map/ppermute | solution.py:313
  155.5 19.3 %collective-permute-done.12 = bf16[64,256]{1,0:T(8,128)(2,1)S(1)} collective-permute-done((bf16[64,256]{1,0:T(8,128)(2,1)S(1)}, bf16[64,256]{1,0:T(8,128)(2,1)S(1)}, u32[]{:S(2)}, u32[]{:S(2)}) %collective-permute-start.12) | collective-permute-done | bytes 32800 | tf_op jit(solution)/shard_map/ppermute | solution.py:313
  175.3 2.2 collective-permute-start.13
  177.5 11.3 %collective-permute-done.13 = bf16[64,256]{1,0:T(8,128)(2,1)S(1)} collective-permute-done((bf16[64,256]{1,0:T(8,128)(2,1)S(1)}, bf16[64,256]{1,0:T(8,128)(2,1)S(1)}, u32[]{:S(2)}, u32[]{:S(2)}) %collective-permute-start.13) | collective-permute-done | bytes 32800 | tf_op jit(solution)/shard_map/ppermute | solution.py:313
  189.2 2.0 collective-permute-start.14
  191.2 2.0 collective-permute-start.15
  193.2 4.8 %collective-permute-done.14 = bf16[64,256]{1,0:T(8,128)(2,1)S(1)} collective-permute-done((bf16[64,256]{1,0:T(8,128)(2,1)S(1)}, bf16[64,256]{1,0:T(8,128)(2,1)S(1)}, u32[]{:S(2)}, u32[]{:S(2)}) %collective-permute-start.14) | collective-permute-done | bytes 32800 | tf_op jit(solution)/shard_map/ppermute | solution.py:313
  198.2 0.3 shard_map.73
  198.6 7.3 %all_to_all.15.arrived_ref = bf16[4,64,256]{2,1,0:T(8,128)(2,1)S(1)} all-to-all(bf16[4,64,256]{2,1,0:T(8,128)(2,1)S(1)} %get-tuple-element.12), channel_id=1, replica_groups={{0,8,16,24},{32,40,48,56},{64,72,80,88},{96,104,112,120},{128,136,144,1..., dimensions={0} | all-to-all | bytes 262144 | tf_op jit(solution)/shard_map/all_to_all | solution.py:201
  206.1 18.4 %all_to_all.16 = bf16[8,64,256]{2,1,0:T(8,128)(2,1)S(1)} all-to-all(bf16[8,64,256]{2,1,0:T(8,128)(2,1)S(1)} %shard_map.74), channel_id=1, replica_groups=mesh['ens'=2,'bfly'=32,'cblk'=8] {'cblk'}, dimensions={0} | all-to-all | bytes 524288 | tf_op jit(solution)/shard_map/all_to_all | solution.py:382
  224.5 2.3 %expand.1 = bf16[2048,512]{1,0:T(8,128)(2,1)} custom-call(s32[1,16]{1,0:T(1,128)S(1)} %copy-done.5, bf16[512,256]{1,0:T(8,128)(2,1)S(1)} %bitcast.81, bf16[2048,256]{1,0:T(8,128)(2,1)S(1)} %copy-done.1), custom_call_target="tpu_custom_call" | custom-call | flops 536870912 | bytes 3145728 | tf_op jit(solution)/shard_map/expand/pallas_call | solution.py:300
  (39 shorter events, 3.9 us)
Async XLA Ops:
  0.0 64.8 %copy-start = (bf16[5,1,256,512]{3,2,1,0:T(8,128)(2,1)S(1)}, bf16[5,1,256,512]{3,2,1,0:T(8,128)(2,1)}, u32[]{:S(2)}) copy-start(bf16[5,1,256,512]{3,2,1,0:T(8,128)(2,1)} %param.9) | copy-start | bytes 3932164
  4.0 57.9 %all-to-all-start = ((bf16[8,64,256]{2,1,0:T(8,128)(2,1)}), bf16[8,64,256]{2,1,0:T(8,128)(2,1)}, u32[]{:S(2)}, u32[]{:S(2)}) async-start(bf16[8,64,256]{2,1,0:T(8,128)(2,1)} %bitcast.82), calls=%async_computation | async-start | bytes 524288 | tf_op jit(solution)/shard_map/all_to_all | solution.py:319
  49.4 29.9 %collective-permute-start.6 = (bf16[2064,256]{1,0:T(8,128)(2,1)}, bf16[2064,256]{1,0:T(8,128)(2,1)S(1)}, u32[]{:S(2)}, u32[]{:S(2)}) collective-permute-start(bf16[2064,256]{1,0:T(8,128)(2,1)} %get-tuple-element.10.refs_3_), channel_id=1, source_target_pairs={{0,4},{1,5},{2,6},{3,7},{4,0},{5,1},{6,2},{7,3},{8,12},{9,13},{10,... | collective-permute-start | bytes 3170312 | tf_op jit(solution)/shard_map/ppermute | solution.py:357
  54.2 47.5 %collective-permute-start.7 = (bf16[2064,256]{1,0:T(8,128)(2,1)}, bf16[2064,256]{1,0:T(8,128)(2,1)S(1)}, u32[]{:S(2)}, u32[]{:S(2)}) collective-permute-start(bf16[2064,256]{1,0:T(8,128)(2,1)} %get-tuple-element.10.refs_3_), channel_id=1, source_target_pairs={{0,6},{1,7},{2,4},{3,5},{4,2},{5,3},{6,0},{7,1},{8,14},{9,15},{10,... | collective-permute-start | bytes 3170312 | tf_op jit(solution)/shard_map/ppermute | solution.py:357
  57.0 47.2 %collective-permute-start.5 = (bf16[2064,256]{1,0:T(8,128)(2,1)}, bf16[2064,256]{1,0:T(8,128)(2,1)}, u32[]{:S(2)}, u32[]{:S(2)}) collective-permute-start(bf16[2064,256]{1,0:T(8,128)(2,1)} %get-tuple-element.10.refs_3_), channel_id=1, source_target_pairs={{0,2},{1,3},{2,0},{3,1},{4,6},{5,7},{6,4},{7,5},{8,10},{9,11},{10,... | collective-permute-start | bytes 3170312 | tf_op jit(solution)/shard_map/ppermute | solution.py:357
  59.0 84.2 %collective-permute-start.8 = (bf16[2064,256]{1,0:T(8,128)(2,1)}, bf16[2064,256]{1,0:T(8,128)(2,1)}, u32[]{:S(2)}, u32[]{:S(2)}) collective-permute-start(bf16[2064,256]{1,0:T(8,128)(2,1)} %get-tuple-element.10.refs_3_), channel_id=1, source_target_pairs={{0,1},{1,0},{2,3},{3,2},{4,5},{5,4},{6,7},{7,6},{8,9},{9,8},{10,11... | collective-permute-start | bytes 3170312 | tf_op jit(solution)/shard_map/ppermute | solution.py:357
  62.9 5.6 %collective-permute-start = (f32[64,256]{1,0:T(8,128)S(1)}, f32[64,256]{1,0:T(8,128)S(1)}, u32[]{:S(2)}, u32[]{:S(2)}) collective-permute-start(f32[64,256]{1,0:T(8,128)S(1)} %convert_reduce_fusion), channel_id=1, source_target_pairs={{0,8},{8,0},{16,24},{24,16},{32,40},{40,32},{48,56},{56,48},{64,72... | collective-permute-start | bytes 196616 | tf_op jit(solution)/shard_map/ppermute | solution.py:313
  65.1 78.1 %copy-start.2 = (bf16[2064,256]{1,0:T(8,128)(2,1)S(1)}, bf16[2064,256]{1,0:T(8,128)(2,1)}, u32[]{:S(2)}) copy-start(bf16[2064,256]{1,0:T(8,128)(2,1)} %get-tuple-element.10.refs_3_) | copy-start | bytes 3170308
  65.1 78.1 %copy-start.3 = (f32[16,512]{1,0:T(8,128)S(1)}, f32[16,512]{1,0:T(8,128)}, u32[]{:S(2)}) copy-start(f32[16,512]{1,0:T(8,128)} %refs_1_.1) | copy-start | bytes 98308
  65.2 78.1 %copy-start.4 = (f32[16,512]{1,0:T(8,128)S(1)}, f32[16,512]{1,0:T(8,128)}, u32[]{:S(2)}) copy-start(f32[16,512]{1,0:T(8,128)} %refs_2_.2) | copy-start | bytes 98308
  68.7 8.0 %collective-permute-start.1 = (f32[64,256]{1,0:T(8,128)S(1)}, f32[64,256]{1,0:T(8,128)S(1)}, u32[]{:S(2)}, u32[]{:S(2)}) collective-permute-start(f32[64,256]{1,0:T(8,128)S(1)} %convolution_add_fusion.7), channel_id=1, source_target_pairs={{0,16},{8,24},{16,0},{24,8},{32,48},{40,56},{48,32},{56,40},{64,80... | collective-permute-start | bytes 196616 | tf_op jit(solution)/shard_map/ppermute | solution.py:313
  77.0 29.2 %collective-permute-start.2 = (bf16[64,256]{1,0:T(8,128)(2,1)S(1)}, bf16[64,256]{1,0:T(8,128)(2,1)S(1)}, u32[]{:S(2)}, u32[]{:S(2)}) collective-permute-start(bf16[64,256]{1,0:T(8,128)(2,1)S(1)} %get-tuple-element.13), channel_id=1, source_target_pairs={{0,32},{8,40},{16,48},{24,56},{32,0},{40,8},{48,16},{56,24},{64,96... | collective-permute-start | bytes 98312 | tf_op jit(solution)/shard_map/ppermute | solution.py:313
  79.2 63.9 %collective-permute-start.10 = (bf16[2064,256]{1,0:T(8,128)(2,1)S(1)}, bf16[2064,256]{1,0:T(8,128)(2,1)S(1)}, u32[]{:S(2)}, u32[]{:S(2)}) collective-permute-start(bf16[2064,256]{1,0:T(8,128)(2,1)S(1)} %collective-permute-done.6.refs_5_), channel_id=1, source_target_pairs={{0,1},{1,0},{2,3},{3,2},{4,5},{5,4},{6,7},{7,6},{8,9},{9,8},{10,11... | collective-permute-start | bytes 3170312 | tf_op jit(solution)/shard_map/ppermute | solution.py:357
  101.8 41.4 %collective-permute-start.11 = (bf16[2064,256]{1,0:T(8,128)(2,1)S(1)}, bf16[2064,256]{1,0:T(8,128)(2,1)S(1)}, u32[]{:S(2)}, u32[]{:S(2)}) collective-permute-start(bf16[2064,256]{1,0:T(8,128)(2,1)S(1)} %collective-permute-done.7.refs_6_), channel_id=1, source_target_pairs={{0,1},{1,0},{2,3},{3,2},{4,5},{5,4},{6,7},{7,6},{8,9},{9,8},{10,11... | collective-permute-start | bytes 3170312 | tf_op jit(solution)/shard_map/ppermute | solution.py:357
  104.2 39.0 %collective-permute-start.9 = (bf16[2064,256]{1,0:T(8,128)(2,1)}, bf16[2064,256]{1,0:T(8,128)(2,1)S(1)}, u32[]{:S(2)}, u32[]{:S(2)}) collective-permute-start(bf16[2064,256]{1,0:T(8,128)(2,1)} %collective-permute-done.5.refs_4_), channel_id=1, source_target_pairs={{0,1},{1,0},{2,3},{3,2},{4,5},{5,4},{6,7},{7,6},{8,9},{9,8},{10,11... | collective-permute-start | bytes 3170312 | tf_op jit(solution)/shard_map/ppermute | solution.py:357
  106.4 13.4 %collective-permute-start.3 = (bf16[64,256]{1,0:T(8,128)(2,1)S(1)}, bf16[64,256]{1,0:T(8,128)(2,1)S(1)}, u32[]{:S(2)}, u32[]{:S(2)}) collective-permute-start(bf16[64,256]{1,0:T(8,128)(2,1)S(1)} %get-tuple-element.15), channel_id=1, source_target_pairs={{0,64},{8,72},{16,80},{24,88},{32,96},{40,104},{48,112},{56,120},{... | collective-permute-start | bytes 98312 | tf_op jit(solution)/shard_map/ppermute | solution.py:313
  120.0 23.0 %collective-permute-start.4 = (bf16[64,256]{1,0:T(8,128)(2,1)S(1)}, bf16[64,256]{1,0:T(8,128)(2,1)S(1)}, u32[]{:S(2)}, u32[]{:S(2)}) collective-permute-start(bf16[64,256]{1,0:T(8,128)(2,1)S(1)} %get-tuple-element.17), channel_id=1, source_target_pairs={{0,128},{8,136},{16,144},{24,152},{32,160},{40,168},{48,176},{56,1... | collective-permute-start | bytes 98312 | tf_op jit(solution)/shard_map/ppermute | solution.py:313
  151.8 23.0 %collective-permute-start.12 = (bf16[64,256]{1,0:T(8,128)(2,1)S(1)}, bf16[64,256]{1,0:T(8,128)(2,1)S(1)}, u32[]{:S(2)}, u32[]{:S(2)}) collective-permute-start(bf16[64,256]{1,0:T(8,128)(2,1)S(1)} %convolution_convert_fusion.2), channel_id=1, source_target_pairs={{0,128},{8,136},{16,144},{24,152},{32,160},{40,168},{48,176},{56,1... | collective-permute-start | bytes 98312 | tf_op jit(solution)/shard_map/ppermute | solution.py:313
  175.3 13.5 %collective-permute-start.13 = (bf16[64,256]{1,0:T(8,128)(2,1)S(1)}, bf16[64,256]{1,0:T(8,128)(2,1)S(1)}, u32[]{:S(2)}, u32[]{:S(2)}) collective-permute-start(bf16[64,256]{1,0:T(8,128)(2,1)S(1)} %convolution_convert_fusion.1), channel_id=1, source_target_pairs={{0,64},{8,72},{16,80},{24,88},{32,96},{40,104},{48,112},{56,120},{... | collective-permute-start | bytes 98312 | tf_op jit(solution)/shard_map/ppermute | solution.py:313
  189.2 8.7 %collective-permute-start.14 = (bf16[64,256]{1,0:T(8,128)(2,1)S(1)}, bf16[64,256]{1,0:T(8,128)(2,1)S(1)}, u32[]{:S(2)}, u32[]{:S(2)}) collective-permute-start(bf16[64,256]{1,0:T(8,128)(2,1)S(1)} %convolution_convert_fusion), channel_id=1, source_target_pairs={{0,32},{8,40},{16,48},{24,56},{32,0},{40,8},{48,16},{56,24},{64,96... | collective-permute-start | bytes 98312 | tf_op jit(solution)/shard_map/ppermute | solution.py:313
  191.2 7.0 %collective-permute-start.15 = (bf16[256,256]{1,0:T(8,128)(2,1)S(1)}, bf16[256,256]{1,0:T(8,128)(2,1)S(1)}, u32[]{:S(2)}, u32[]{:S(2)}) collective-permute-start(bf16[256,256]{1,0:T(8,128)(2,1)S(1)} %slice_bitcast_fusion.10), channel_id=1, source_target_pairs={{0,16},{8,24},{16,0},{24,8},{32,48},{40,56},{48,32},{56,40},{64,80... | collective-permute-start | bytes 393224 | tf_op jit(solution)/shard_map/ppermute | solution.py:313
  198.5 25.9 %copy-start.1 = (bf16[2048,256]{1,0:T(8,128)(2,1)S(1)}, bf16[2048,256]{1,0:T(8,128)(2,1)}, u32[]{:S(2)}) copy-start(bf16[2048,256]{1,0:T(8,128)(2,1)} %refs_2_.3) | copy-start | bytes 3145732
  198.6 25.9 %copy-start.5 = (s32[1,16]{1,0:T(1,128)S(1)}, s32[1,16]{1,0:T(1,128)}, u32[]{:S(2)}) copy-start(s32[1,16]{1,0:T(1,128)} %refs_0_.1) | copy-start | bytes 196

commit v5 on v4

--- a/solution.py
+++ b/solution.py
@@ -43,20 +43,21 @@
     source_hbm,
     basis_hbm,
     out_ref,
-    packed_hbm,
     acc_ref,
     order_ref,
     place_ref,
     class_ref,
     source_ref,
     basis_ref,
-    label_ref,
     sems,
     source_sems,
 ):
     rows = source_ref.shape[0]
     tiles = order_ref.shape[1]
     tile = rows // tiles
+    shares = out_ref.shape[0]
+    width = out_ref.shape[2]
+    columns = source_ref.shape[1] // shares
     step = 4
     order_in = pltpu.make_async_copy(order_hbm, order_ref, sems.at[0])
     basis_in = pltpu.make_async_copy(basis_hbm, basis_ref, sems.at[1])
@@ -69,14 +70,18 @@
         for at in range(0, tiles, step)
     ]
     class_in = pltpu.make_async_copy(class_hbm, class_ref, sems.at[2])
-    for copy in (order_in, basis_in, *source_in, class_in):
+    for copy in (order_in, class_in, basis_in, *source_in):
         copy.start()
     order_in.wait()
     for i in range(tiles):
         place_ref[order_ref[0, i]] = i
+    class_in.wait()
+    label = [class_ref[:, pl.ds(at, width)].astype(F32) for at in range(0, rows, width)]
+    label.append(jnp.zeros((LABEL_ROWS - len(label), width), F32))
+    label = jnp.concatenate(label, axis=0).astype(out_ref.dtype)
+    for share in range(shares):
+        out_ref[share, columns:, :] = label
     basis_in.wait()
-    basis_out = pltpu.make_async_copy(basis_ref, packed_hbm.at[pl.ds(0, rows), :], sems.at[3])
-    basis_out.start()
     for start in range(0, tiles, step):
         source_in[start // step].wait()
         matched = jnp.concatenate(
@@ -92,35 +97,20 @@
         elif start + step < tiles:
             acc_ref[...] += term
         else:
-            out_ref[...] = (acc_ref[...] + term).astype(out_ref.dtype)
-        if start == 0:
-            class_in.wait()
-            width = label_ref.shape[1]
-            label = [class_ref[:, pl.ds(at, width)].astype(F32) for at in range(0, rows, width)]
-            label.append(jnp.zeros((label_ref.shape[0] - len(label), width), F32))
-            label_ref[...] = jnp.concatenate(label, axis=0).astype(label_ref.dtype)
-        elif start == step:
-            label_out = pltpu.make_async_copy(
-                label_ref, packed_hbm.at[pl.ds(rows, label_ref.shape[0]), :], sems.at[4]
-            )
-            label_out.start()
-    basis_out.wait()
-    label_out.wait()
-
-
-def leaf_terms(source, basis, skeleton, row_class):
+            total = (acc_ref[...] + term).astype(out_ref.dtype)
+            for share in range(shares):
+                out_ref[share, :columns, :] = total[share * columns : (share + 1) * columns]
+
+
+def leaf_terms(source, basis, skeleton, row_class, shares):
     rows, columns = source.shape
     rank = basis.shape[1]
-    labels = LABEL_ROWS
     return pl.pallas_call(
         leaf_kernel,
         name="leaf",
-        out_shape=(
-            jax.ShapeDtypeStruct((columns, rank), BF16),
-            jax.ShapeDtypeStruct((rows + labels, rank), BF16),
-        ),
+        out_shape=jax.ShapeDtypeStruct((shares, columns // shares + LABEL_ROWS, rank), BF16),
         in_specs=[hbm()] * 4,
-        out_specs=(vmem(), hbm()),
+        out_specs=vmem(),
         scratch_shapes=[
             pltpu.VMEM((columns, rank), F32),
             pltpu.SMEM(skeleton.shape, jnp.int32),
@@ -128,8 +118,7 @@
             pltpu.VMEM((1, rows), jnp.int32),
             pltpu.VMEM(source.shape, source.dtype),
             pltpu.VMEM(basis.shape, basis.dtype),
-            pltpu.VMEM((labels, rank), BF16),
-            pltpu.SemaphoreType.DMA((5,)),
+            pltpu.SemaphoreType.DMA((3,)),
             pltpu.SemaphoreType.DMA((skeleton.shape[1] // 4,)),
         ],
         compiler_params=pltpu.CompilerParams(vmem_limit_bytes=LEAF_LIMIT),
@@ -211,14 +200,10 @@
     return jnp.concatenate([high.astype(F32), middle.astype(F32), low.astype(F32)], axis=0)
 
 
-def middle_kernel(factor_rho, count, *refs):
-    carried_ref, linear_ref, cubic_ref = refs[:3]
-    packed = refs[3 : 3 + count]
-    out_ref, table_ref = refs[3 + count :]
-    columns = carried_ref.shape[0]
+def looked_kernel(rows, arrived_ref, linear_ref, cubic_ref, out_ref, table_ref):
+    count, tall, width = arrived_ref.shape
+    columns = tall - LABEL_ROWS
     classes = linear_ref.shape[0]
-    rows = packed[0].shape[0] - LABEL_ROWS
-    width = packed[0].shape[1]
     lanes = table_ref.shape[1]
     shares = lanes // columns
     mine = lax.axis_index("cblk")
@@ -227,42 +212,69 @@
     table_ref[0] = in_three(linear_ref[:, wide]).T
     table_ref[1] = in_three(cubic_ref[:, wide]).T
     tables = jnp.concatenate([table_ref[0, share, :], table_ref[1, share, :]], axis=0).astype(BF16)
+    ids = lax.broadcasted_iota(jnp.int32, (classes, width), 0).astype(F32)
+    for at in range(count):
+        labels = arrived_ref[mine ^ at, columns:, :].astype(F32)
+        for part in range(rows // width):
+            hot = (ids == labels[part : part + 1]).astype(F32)
+            hot = jnp.concatenate([hot, hot, hot], axis=0).astype(BF16)
+            out_ref[:, pl.ds(at * rows + part * width, width)] = dot(tables, hot, 1, 0)
+
+
+def looked_up(arrived, linear_table, cubic_table, rows):
+    count, tall, _ = arrived.shape
+    columns = tall - LABEL_ROWS
+
+    def body(*refs):
+        looked_kernel(rows, *refs)
+
+    return pl.pallas_call(
+        body,
+        name="looked",
+        out_shape=jax.ShapeDtypeStruct((2 * columns, count * rows), F32),
+        in_specs=[vmem()] * 3,
+        out_specs=vmem(),
+        scratch_shapes=[pltpu.VMEM((2, max(columns, 128), 3 * linear_table.shape[0]), F32)],
+        compiler_params=pltpu.CompilerParams(vmem_limit_bytes=VMEM_LIMIT),
+        cost_estimate=cost(1 << 30, 1 << 23),
+    )(arrived, linear_table, cubic_table)
+
+
+def middle_kernel(factor_rho, carried_ref, looked_ref, *refs):
+    bases, out_ref = refs[:-1], refs[-1]
+    columns, width = carried_ref.shape
+    rows = bases[0].shape[0]
     step = 2 * width
-    ids = lax.broadcasted_iota(jnp.int32, (classes, step), 0).astype(F32)
     total = jnp.zeros((columns, width), F32)
-    for ref in packed:
-        labels = ref[pl.ds(rows, LABEL_ROWS), :].astype(F32)
+    for at, ref in enumerate(bases):
         for start in range(0, rows, step):
             basis = ref[pl.ds(start, step), :]
             mapped = factor_rho * dot(carried_ref[...], basis, 1, 1)
-            first = start // width
-            label = jnp.concatenate([labels[first : first + 1], labels[first + 1 : first + 2]], axis=1)
-            hot = (ids == label).astype(F32)
-            hot = jnp.concatenate([hot, hot, hot], axis=0).astype(BF16)
-            looked = dot(tables, hot, 1, 0)
-            weighted = mapped * (looked[:columns] + looked[columns:] * mapped * mapped)
+            here = pl.ds(at * rows + start, step)
+            linear = looked_ref[:columns, here]
+            cubic = looked_ref[columns:, here]
+            weighted = mapped * (linear + cubic * mapped * mapped)
             total += dot(weighted.astype(BF16), basis, 1, 0)
     out_ref[...] = total
 
 
-def middle(carried, packed, linear_table, cubic_table, factor_rho):
+def middle(carried, looked, bases, factor_rho):
     columns, rank = carried.shape
-    count = len(packed)
-    tall = packed[0].shape[0]
+    count = len(bases)
+    rows = bases[0].shape[0]
 
     def body(*refs):
-        middle_kernel(factor_rho, count, *refs)
+        middle_kernel(factor_rho, *refs)
 
     return pl.pallas_call(
         body,
         name="middle",
         out_shape=jax.ShapeDtypeStruct((columns, rank), F32),
-        in_specs=[vmem()] * (3 + count),
+        in_specs=[vmem()] * (2 + count),
         out_specs=vmem(),
-        scratch_shapes=[pltpu.VMEM((2, max(columns, 128), 3 * linear_table.shape[0]), F32)],
         compiler_params=pltpu.CompilerParams(vmem_limit_bytes=VMEM_LIMIT),
-        cost_estimate=cost(8 * count * tall * columns * rank, 2 * count * tall * rank),
-    )(carried, linear_table, cubic_table, *packed)
+        cost_estimate=cost(8 * count * rows * columns * rank, 2 * count * rows * rank),
+    )(carried, looked, *bases)
 
 
 def expand_kernel(factor_rho, order_ref, returned_ref, basis_ref, out_ref, held_ref, sems):
@@ -313,12 +325,6 @@
     return lax.ppermute(array, axis, [(i, i ^ 1 << bit) for i in range(lax.axis_size(axis))])
 
 
-def shared_out(array, axis):
-    count = lax.axis_size(axis)
-    blocks = array.reshape(count, array.shape[0] // count, array.shape[1])
-    return lax.all_to_all(blocks, axis, split_axis=0, concat_axis=0, tiled=True)
-
-
 def times(left, right, right_dim):
     if left.dtype == BF16:
         return dot(left, right, 1, right_dim)
@@ -357,25 +363,33 @@
     return lax.ppermute(array, "cblk", [(i, i ^ mask) for i in range(lax.axis_size("cblk"))])
 
 
+def in_mask_order(basis, far, near):
+    even = [basis, *far]
+    return [array for pair in zip(even, near) for array in pair]
+
+
 def per_device(source, basis, transfer, skeleton, row_class, linear_table, cubic_table):
     factors = transfer[:, 0]
     rank = basis.shape[1]
     shares = lax.axis_size("cblk")
     factor_rho = math.sqrt(source.shape[0] * shares / rank)
-    leaves, packed = leaf_terms(source, basis, skeleton, row_class)
-    leaves = shared_out(leaves, "cblk")
-    columns = leaves.shape[1]
+    columns = source.shape[1] // shares
+    leaves = leaf_terms(source, basis, skeleton, row_class, shares)
+    leaves = lax.all_to_all(leaves, "cblk", split_axis=0, concat_axis=0, tiled=True)
     whole = jax.ShapeDtypeStruct((columns, rank), F32)
     fours = jax.ShapeDtypeStruct((4, columns, rank), BF16)
     eights = jax.ShapeDtypeStruct((shares, columns, rank), BF16)
 
-    far = [swapped(packed, mask) for mask in range(2, shares, 2)]
-    near = [swapped(packed, 1)]
+    far = [swapped(basis, mask) for mask in range(2, shares, 2)]
+    near = [swapped(basis, 1)]
     near += [swapped(array, 1) for array in far]
     extra = from_partner(factors[0, :, rank:], "bfly", 1)
-
-    carried = forward_levels(leaves.astype(F32).sum(axis=0), factors).astype(BF16)
-    back = middle(carried, [packed, *far, *near], linear_table, cubic_table, factor_rho)
+    looked = looked_up(leaves, linear_table, cubic_table, source.shape[0])
+
+    summed = leaves[:, :columns].astype(F32).sum(axis=0)
+    carried = forward_levels(summed, factors).astype(BF16)
+    bases = in_mask_order(basis, far, near)
+    back = middle(carried, looked, bases, factor_rho)
     high = adjoint_levels(back, factors)
     send, own = small_call(down_send_kernel, (fours, whole), high, factors, extra)
     returned = small_call(down_take_kernel, eights, own, in_fours(send), factors)

time: 228 us -> 224 us (0.982)
  waiting for transfers between devices: 94.4 us -> 89.2 us
  starting transfers between devices: 86.3 us -> 90.5 us
    ppermute x9, waiting for transfers between devices: 74.7 us -> 70.9 us  [from_partner(): lax.ppermute(array, axis, [(i, i ^ 1 << bit) for i in range(lax.axis_size...]
    ppermute x9, starting transfers between devices: 21.2 us -> 23.8 us  [from_partner(): lax.ppermute(array, axis, [(i, i ^ 1 << bit) for i in range(lax.axis_size...]
    pallas_call x1 -> x2, Pallas kernels: 3.98 us -> 5.47 us  [the longest x1 4.14 us: leaf_terms(): pl.pallas_call(leaf_kernel, name='leaf', out_shape=jax.ShapeDtypeStruct((...]
  transfers between devices with their start and end apart: 17 -> 17, of which waited for: 9 -> 10; matrix products, arithmetic and copies ran while one was open for 2% -> 1% of each run, Pallas kernels for 0% -> 1%
where the time goes in v5:
time: 224 us
  starting transfers between devices  90.5 us (40%)
  waiting for transfers between devices  89.2 us (40%)
  blocking collectives  24.9 us (11%)
  Pallas kernels  15.1 us (7%)
  matrix products  3.64 us (2%)
    ppermute x9, waiting for transfers between devices, from_partner(): lax.ppermute(array, axis, [(i, i ^ 1 << bit) for i in range(lax.axis_size...  70.9 us
    all_to_all x1, starting transfers between devices, per_device(): lax.all_to_all(leaves, 'cblk', split_axis=0, concat_axis=0, tiled=True)  44.8 us
    ppermute x9, starting transfers between devices, from_partner(): lax.ppermute(array, axis, [(i, i ^ 1 << bit) for i in range(lax.axis_size...  23.8 us
    ppermute x7, starting transfers between devices, swapped(): lax.ppermute(array, 'cblk', [(i, i ^ mask) for i in range(lax.axis_size('...  21.8 us
    ppermute x7, waiting for transfers between devices, swapped(): lax.ppermute(array, 'cblk', [(i, i ^ mask) for i in range(lax.axis_size('...  18.3 us
    all_to_all x1, blocking collectives, per_device(): lax.all_to_all(returned, 'cblk', split_axis=0, concat_axis=0, tiled=True)  17.6 us
    all_to_all x1, blocking collectives, in_fours(): lax.all_to_all(array, 'bfly', split_axis=0, concat_axis=0, axis_index_gro...  7.21 us
    pallas_call x1, Pallas kernels, middle(): pl.pallas_call(body, name='middle', out_shape=jax.ShapeDtypeStruct((colum...  6.81 us
  transfers between devices with their start and end apart: 17, of which 10 were waited for; matrix products, arithmetic and copies ran while one was open for 1% of the time, Pallas kernels for 1%

profile of v5, /device:TPU:33, one launch (start us, length us, event | category | flops | bytes accessed | tf_op | source)
XLA Modules:
  0.0 223.7 jit_solution(12107459260735355136)
XLA Ops:
  0.0 4.1 %leaf.1 = bf16[8,80,256]{2,1,0:T(8,128)(2,1)} custom-call(s32[1,16]{1,0:T(1,128)} %refs_0_.1, s32[1,2048]{1,0:T(1,128)} %bitcast.81, bf16[2048,512]{1,0:T(8,128)(2,1)} %source_hbm.1, bf16[2048,256]{1,0:T(8,128)(2,1)} %refs_2_.5), custom_call_target="tpu_custom_call" | custom-call | flops 536870912 | bytes 3145728 | tf_op jit(solution)/shard_map/leaf/pallas_call | solution.py:108
  4.2 44.8 %all-to-all-start = ((bf16[8,80,256]{2,1,0:T(8,128)(2,1)}), bf16[8,80,256]{2,1,0:T(8,128)(2,1)S(1)}, u32[]{:S(2)}, u32[]{:S(2)}) async-start(bf16[8,80,256]{2,1,0:T(8,128)(2,1)} %leaf.1), calls=%async_computation | async-start | bytes 655360 | tf_op jit(solution)/shard_map/all_to_all | solution.py:378
  48.9 4.6 %collective-permute-start.10 = (bf16[2048,256]{1,0:T(8,128)(2,1)}, bf16[2048,256]{1,0:T(8,128)(2,1)S(1)}, u32[]{:S(2)}, u32[]{:S(2)}) collective-permute-start(bf16[2048,256]{1,0:T(8,128)(2,1)} %refs_2_.5), channel_id=1, source_target_pairs={{0,6},{1,7},{2,4},{3,5},{4,2},{5,3},{6,0},{7,1},{8,14},{9,15},{10,... | collective-permute-start | bytes 3145736 | tf_op jit(solution)/shard_map/ppermute | solution.py:363
  53.6 2.0 collective-permute-start.6
  55.5 3.1 %collective-permute-start.8 = (bf16[2048,256]{1,0:T(8,128)(2,1)}, bf16[2048,256]{1,0:T(8,128)(2,1)}, u32[]{:S(2)}, u32[]{:S(2)}) collective-permute-start(bf16[2048,256]{1,0:T(8,128)(2,1)} %refs_2_.5), channel_id=1, source_target_pairs={{0,4},{1,5},{2,6},{3,7},{4,0},{5,1},{6,2},{7,3},{8,12},{9,13},{10,... | collective-permute-start | bytes 3145736 | tf_op jit(solution)/shard_map/ppermute | solution.py:363
  58.7 3.1 %collective-permute-start.5 = (bf16[2048,256]{1,0:T(8,128)(2,1)}, bf16[2048,256]{1,0:T(8,128)(2,1)}, u32[]{:S(2)}, u32[]{:S(2)}) collective-permute-start(bf16[2048,256]{1,0:T(8,128)(2,1)} %refs_2_.5), channel_id=1, source_target_pairs={{0,1},{1,0},{2,3},{3,2},{4,5},{5,4},{6,7},{7,6},{8,9},{9,8},{10,11... | collective-permute-start | bytes 3145736 | tf_op jit(solution)/shard_map/ppermute | solution.py:363
  61.8 2.0 collective-permute-start
  64.1 1.3 looked.1.refs_1_
  65.4 2.0 collective-permute-done
  67.7 2.0 collective-permute-start.1
  70.0 5.7 %collective-permute-done.1 = f32[64,256]{1,0:T(8,128)S(1)} collective-permute-done((f32[64,256]{1,0:T(8,128)S(1)}, f32[64,256]{1,0:T(8,128)S(1)}, u32[]{:S(2)}, u32[]{:S(2)}) %collective-permute-start.1) | collective-permute-done | bytes 65568 | tf_op jit(solution)/shard_map/ppermute | solution.py:325
  75.9 2.0 collective-permute-start.2
  78.2 0.5 collective-permute-done.10.refs_8_
  78.7 2.7 %collective-permute-start.11 = (bf16[2048,256]{1,0:T(8,128)(2,1)S(1)}, bf16[2048,256]{1,0:T(8,128)(2,1)S(1)}, u32[]{:S(2)}, u32[]{:S(2)}) collective-permute-start(bf16[2048,256]{1,0:T(8,128)(2,1)S(1)} %collective-permute-done.10.refs_8_), channel_id=1, source_target_pairs={{0,1},{1,0},{2,3},{3,2},{4,5},{5,4},{6,7},{7,6},{8,9},{9,8},{10,11... | collective-permute-start | bytes 3145736 | tf_op jit(solution)/shard_map/ppermute | solution.py:363
  81.4 3.0 %collective-permute-start.7 = (bf16[2048,256]{1,0:T(8,128)(2,1)}, bf16[2048,256]{1,0:T(8,128)(2,1)S(1)}, u32[]{:S(2)}, u32[]{:S(2)}) collective-permute-start(bf16[2048,256]{1,0:T(8,128)(2,1)} %collective-permute-done.6.refs_4_), channel_id=1, source_target_pairs={{0,1},{1,0},{2,3},{3,2},{4,5},{5,4},{6,7},{7,6},{8,9},{9,8},{10,11... | collective-permute-start | bytes 3145736 | tf_op jit(solution)/shard_map/ppermute | solution.py:363
  84.4 17.7 %collective-permute-done.8.refs_6_ = bf16[2048,256]{1,0:T(8,128)(2,1)} collective-permute-done((bf16[2048,256]{1,0:T(8,128)(2,1)}, bf16[2048,256]{1,0:T(8,128)(2,1)}, u32[]{:S(2)}, u32[]{:S(2)}) %collective-permute-start.8) | collective-permute-done | bytes 1048608 | tf_op jit(solution)/shard_map/ppermute | solution.py:363
  102.1 3.4 %collective-permute-start.9 = (bf16[2048,256]{1,0:T(8,128)(2,1)}, bf16[2048,256]{1,0:T(8,128)(2,1)S(1)}, u32[]{:S(2)}, u32[]{:S(2)}) collective-permute-start(bf16[2048,256]{1,0:T(8,128)(2,1)} %collective-permute-done.8.refs_6_), channel_id=1, source_target_pairs={{0,1},{1,0},{2,3},{3,2},{4,5},{5,4},{6,7},{7,6},{8,9},{9,8},{10,11... | collective-permute-start | bytes 3145736 | tf_op jit(solution)/shard_map/ppermute | solution.py:363
  105.7 2.0 collective-permute-start.3
  108.0 11.2 %collective-permute-done.3 = bf16[64,256]{1,0:T(8,128)(2,1)S(1)} collective-permute-done((bf16[64,256]{1,0:T(8,128)(2,1)S(1)}, bf16[64,256]{1,0:T(8,128)(2,1)S(1)}, u32[]{:S(2)}, u32[]{:S(2)}) %collective-permute-start.3) | collective-permute-done | bytes 32800 | tf_op jit(solution)/shard_map/ppermute | solution.py:325
  119.3 4.8 %collective-permute-start.4 = (bf16[64,256]{1,0:T(8,128)(2,1)S(1)}, bf16[64,256]{1,0:T(8,128)(2,1)S(1)}, u32[]{:S(2)}, u32[]{:S(2)}) collective-permute-start(bf16[64,256]{1,0:T(8,128)(2,1)S(1)} %get-tuple-element.13), channel_id=1, source_target_pairs={{0,128},{8,136},{16,144},{24,152},{32,160},{40,168},{48,176},{56,1... | collective-permute-start | bytes 98312 | tf_op jit(solution)/shard_map/ppermute | solution.py:325
  124.4 18.0 %collective-permute-done.4 = bf16[64,256]{1,0:T(8,128)(2,1)S(1)} collective-permute-done((bf16[64,256]{1,0:T(8,128)(2,1)S(1)}, bf16[64,256]{1,0:T(8,128)(2,1)S(1)}, u32[]{:S(2)}, u32[]{:S(2)}) %collective-permute-start.4) | collective-permute-done | bytes 32800 | tf_op jit(solution)/shard_map/ppermute | solution.py:325
  142.6 6.8 %middle.1 = f32[64,256]{1,0:T(8,128)S(1)} custom-call(bf16[64,256]{1,0:T(8,128)(2,1)S(1)} %fusion.refs_0_, f32[128,16384]{1,0:T(8,128)S(1)} %looked.1.refs_1_, bf16[2048,256]{1,0:T(8,128)(2,1)S(1)} %copy-done.1, bf16[2048,256]{1,0:T(8,128)(2,1)} %collective-permute-done.5.refs_3_, bf16[2048,256]{1,0:T(8,128)(2,1)} %collective-permute-done.6.refs_4_, ...), custom_call_target="tpu_custom_call" | custom-call | flops 2147483648 | bytes 8388608 | tf_op jit(solution)/shard_map/middle/pallas_call | solution.py:269
  149.6 4.9 %collective-permute-start.12 = (bf16[64,256]{1,0:T(8,128)(2,1)S(1)}, bf16[64,256]{1,0:T(8,128)(2,1)S(1)}, u32[]{:S(2)}, u32[]{:S(2)}) collective-permute-start(bf16[64,256]{1,0:T(8,128)(2,1)S(1)} %convolution_convert_fusion.2), channel_id=1, source_target_pairs={{0,128},{8,136},{16,144},{24,152},{32,160},{40,168},{48,176},{56,1... | collective-permute-start | bytes 98312 | tf_op jit(solution)/shard_map/ppermute | solution.py:325
  154.4 18.2 %collective-permute-done.12 = bf16[64,256]{1,0:T(8,128)(2,1)S(1)} collective-permute-done((bf16[64,256]{1,0:T(8,128)(2,1)S(1)}, bf16[64,256]{1,0:T(8,128)(2,1)S(1)}, u32[]{:S(2)}, u32[]{:S(2)}) %collective-permute-start.12) | collective-permute-done | bytes 32800 | tf_op jit(solution)/shard_map/ppermute | solution.py:325
  173.0 2.5 %collective-permute-start.13 = (bf16[64,256]{1,0:T(8,128)(2,1)S(1)}, bf16[64,256]{1,0:T(8,128)(2,1)S(1)}, u32[]{:S(2)}, u32[]{:S(2)}) collective-permute-start(bf16[64,256]{1,0:T(8,128)(2,1)S(1)} %convolution_convert_fusion.1), channel_id=1, source_target_pairs={{0,64},{8,72},{16,80},{24,88},{32,96},{40,104},{48,112},{56,120},{... | collective-permute-start | bytes 98312 | tf_op jit(solution)/shard_map/ppermute | solution.py:325
  175.6 10.9 %collective-permute-done.13 = bf16[64,256]{1,0:T(8,128)(2,1)S(1)} collective-permute-done((bf16[64,256]{1,0:T(8,128)(2,1)S(1)}, bf16[64,256]{1,0:T(8,128)(2,1)S(1)}, u32[]{:S(2)}, u32[]{:S(2)}) %collective-permute-start.13) | collective-permute-done | bytes 32800 | tf_op jit(solution)/shard_map/ppermute | solution.py:325
  186.9 2.0 collective-permute-start.14
  188.8 2.0 collective-permute-start.15
  190.8 4.8 %collective-permute-done.14 = bf16[64,256]{1,0:T(8,128)(2,1)S(1)} collective-permute-done((bf16[64,256]{1,0:T(8,128)(2,1)S(1)}, bf16[64,256]{1,0:T(8,128)(2,1)S(1)}, u32[]{:S(2)}, u32[]{:S(2)}) %collective-permute-start.14) | collective-permute-done | bytes 32800 | tf_op jit(solution)/shard_map/ppermute | solution.py:325
  196.4 7.2 %all_to_all.15.arrived_ref = bf16[4,64,256]{2,1,0:T(8,128)(2,1)S(1)} all-to-all(bf16[4,64,256]{2,1,0:T(8,128)(2,1)S(1)} %get-tuple-element.8), channel_id=1, replica_groups={{0,8,16,24},{32,40,48,56},{64,72,80,88},{96,104,112,120},{128,136,144,1..., dimensions={0} | all-to-all | bytes 262144 | tf_op jit(solution)/shard_map/all_to_all | solution.py:190
  203.8 17.6 %all_to_all.16 = bf16[8,64,256]{2,1,0:T(8,128)(2,1)S(1)} all-to-all(bf16[8,64,256]{2,1,0:T(8,128)(2,1)S(1)} %shard_map.74), channel_id=1, replica_groups=mesh['ens'=2,'bfly'=32,'cblk'=8] {'cblk'}, dimensions={0} | all-to-all | bytes 524288 | tf_op jit(solution)/shard_map/all_to_all | solution.py:396
  221.4 2.3 %expand.1 = bf16[2048,512]{1,0:T(8,128)(2,1)} custom-call(s32[1,16]{1,0:T(1,128)S(1)} %copy-done.4, bf16[512,256]{1,0:T(8,128)(2,1)S(1)} %bitcast.80, bf16[2048,256]{1,0:T(8,128)(2,1)S(1)} %copy-done.1), custom_call_target="tpu_custom_call" | custom-call | flops 536870912 | bytes 3145728 | tf_op jit(solution)/shard_map/expand/pallas_call | solution.py:312
  (38 shorter events, 4.5 us)
Async XLA Ops:
  0.0 63.8 %copy-start = (bf16[5,1,256,512]{3,2,1,0:T(8,128)(2,1)S(1)}, bf16[5,1,256,512]{3,2,1,0:T(8,128)(2,1)}, u32[]{:S(2)}) copy-start(bf16[5,1,256,512]{3,2,1,0:T(8,128)(2,1)} %param.9) | copy-start | bytes 3932164
  0.0 64.0 %copy-start.2 = (f32[16,512]{1,0:T(8,128)S(1)}, f32[16,512]{1,0:T(8,128)}, u32[]{:S(2)}) copy-start(f32[16,512]{1,0:T(8,128)} %refs_1_.1) | copy-start | bytes 98308
  0.0 64.1 %copy-start.3 = (f32[16,512]{1,0:T(8,128)S(1)}, f32[16,512]{1,0:T(8,128)}, u32[]{:S(2)}) copy-start(f32[16,512]{1,0:T(8,128)} %refs_2_.3) | copy-start | bytes 98308
  4.2 57.6 %all-to-all-start = ((bf16[8,80,256]{2,1,0:T(8,128)(2,1)}), bf16[8,80,256]{2,1,0:T(8,128)(2,1)S(1)}, u32[]{:S(2)}, u32[]{:S(2)}) async-start(bf16[8,80,256]{2,1,0:T(8,128)(2,1)} %leaf.1), calls=%async_computation | async-start | bytes 655360 | tf_op jit(solution)/shard_map/all_to_all | solution.py:378
  48.9 29.8 %collective-permute-start.10 = (bf16[2048,256]{1,0:T(8,128)(2,1)}, bf16[2048,256]{1,0:T(8,128)(2,1)S(1)}, u32[]{:S(2)}, u32[]{:S(2)}) collective-permute-start(bf16[2048,256]{1,0:T(8,128)(2,1)} %refs_2_.5), channel_id=1, source_target_pairs={{0,6},{1,7},{2,4},{3,5},{4,2},{5,3},{6,0},{7,1},{8,14},{9,15},{10,... | collective-permute-start | bytes 3145736 | tf_op jit(solution)/shard_map/ppermute | solution.py:363
  53.6 27.8 %collective-permute-start.6 = (bf16[2048,256]{1,0:T(8,128)(2,1)}, bf16[2048,256]{1,0:T(8,128)(2,1)}, u32[]{:S(2)}, u32[]{:S(2)}) collective-permute-start(bf16[2048,256]{1,0:T(8,128)(2,1)} %refs_2_.5), channel_id=1, source_target_pairs={{0,2},{1,3},{2,0},{3,1},{4,6},{5,7},{6,4},{7,5},{8,10},{9,11},{10,... | collective-permute-start | bytes 3145736 | tf_op jit(solution)/shard_map/ppermute | solution.py:363
  55.5 46.6 %collective-permute-start.8 = (bf16[2048,256]{1,0:T(8,128)(2,1)}, bf16[2048,256]{1,0:T(8,128)(2,1)}, u32[]{:S(2)}, u32[]{:S(2)}) collective-permute-start(bf16[2048,256]{1,0:T(8,128)(2,1)} %refs_2_.5), channel_id=1, source_target_pairs={{0,4},{1,5},{2,6},{3,7},{4,0},{5,1},{6,2},{7,3},{8,12},{9,13},{10,... | collective-permute-start | bytes 3145736 | tf_op jit(solution)/shard_map/ppermute | solution.py:363
  58.7 83.9 %collective-permute-start.5 = (bf16[2048,256]{1,0:T(8,128)(2,1)}, bf16[2048,256]{1,0:T(8,128)(2,1)}, u32[]{:S(2)}, u32[]{:S(2)}) collective-permute-start(bf16[2048,256]{1,0:T(8,128)(2,1)} %refs_2_.5), channel_id=1, source_target_pairs={{0,1},{1,0},{2,3},{3,2},{4,5},{5,4},{6,7},{7,6},{8,9},{9,8},{10,11... | collective-permute-start | bytes 3145736 | tf_op jit(solution)/shard_map/ppermute | solution.py:363
  61.8 5.7 %collective-permute-start = (f32[64,256]{1,0:T(8,128)S(1)}, f32[64,256]{1,0:T(8,128)S(1)}, u32[]{:S(2)}, u32[]{:S(2)}) collective-permute-start(f32[64,256]{1,0:T(8,128)S(1)} %convert_reduce_fusion), channel_id=1, source_target_pairs={{0,8},{8,0},{16,24},{24,16},{32,40},{40,32},{48,56},{56,48},{64,72... | collective-permute-start | bytes 196616 | tf_op jit(solution)/shard_map/ppermute | solution.py:325
  65.4 77.2 %copy-start.1 = (bf16[2048,256]{1,0:T(8,128)(2,1)S(1)}, bf16[2048,256]{1,0:T(8,128)(2,1)}, u32[]{:S(2)}) copy-start(bf16[2048,256]{1,0:T(8,128)(2,1)} %refs_2_.5) | copy-start | bytes 3145732
  67.7 7.9 %collective-permute-start.1 = (f32[64,256]{1,0:T(8,128)S(1)}, f32[64,256]{1,0:T(8,128)S(1)}, u32[]{:S(2)}, u32[]{:S(2)}) collective-permute-start(f32[64,256]{1,0:T(8,128)S(1)} %convolution_add_fusion.7), channel_id=1, source_target_pairs={{0,16},{8,24},{16,0},{24,8},{32,48},{40,56},{48,32},{56,40},{64,80... | collective-permute-start | bytes 196616 | tf_op jit(solution)/shard_map/ppermute | solution.py:325
  75.9 29.6 %collective-permute-start.2 = (bf16[64,256]{1,0:T(8,128)(2,1)S(1)}, bf16[64,256]{1,0:T(8,128)(2,1)S(1)}, u32[]{:S(2)}, u32[]{:S(2)}) collective-permute-start(bf16[64,256]{1,0:T(8,128)(2,1)S(1)} %get-tuple-element.9), channel_id=1, source_target_pairs={{0,32},{8,40},{16,48},{24,56},{32,0},{40,8},{48,16},{56,24},{64,96... | collective-permute-start | bytes 98312 | tf_op jit(solution)/shard_map/ppermute | solution.py:325
  78.7 63.8 %collective-permute-start.11 = (bf16[2048,256]{1,0:T(8,128)(2,1)S(1)}, bf16[2048,256]{1,0:T(8,128)(2,1)S(1)}, u32[]{:S(2)}, u32[]{:S(2)}) collective-permute-start(bf16[2048,256]{1,0:T(8,128)(2,1)S(1)} %collective-permute-done.10.refs_8_), channel_id=1, source_target_pairs={{0,1},{1,0},{2,3},{3,2},{4,5},{5,4},{6,7},{7,6},{8,9},{9,8},{10,11... | collective-permute-start | bytes 3145736 | tf_op jit(solution)/shard_map/ppermute | solution.py:363
  81.4 61.1 %collective-permute-start.7 = (bf16[2048,256]{1,0:T(8,128)(2,1)}, bf16[2048,256]{1,0:T(8,128)(2,1)S(1)}, u32[]{:S(2)}, u32[]{:S(2)}) collective-permute-start(bf16[2048,256]{1,0:T(8,128)(2,1)} %collective-permute-done.6.refs_4_), channel_id=1, source_target_pairs={{0,1},{1,0},{2,3},{3,2},{4,5},{5,4},{6,7},{7,6},{8,9},{9,8},{10,11... | collective-permute-start | bytes 3145736 | tf_op jit(solution)/shard_map/ppermute | solution.py:363
  102.1 40.4 %collective-permute-start.9 = (bf16[2048,256]{1,0:T(8,128)(2,1)}, bf16[2048,256]{1,0:T(8,128)(2,1)S(1)}, u32[]{:S(2)}, u32[]{:S(2)}) collective-permute-start(bf16[2048,256]{1,0:T(8,128)(2,1)} %collective-permute-done.8.refs_6_), channel_id=1, source_target_pairs={{0,1},{1,0},{2,3},{3,2},{4,5},{5,4},{6,7},{7,6},{8,9},{9,8},{10,11... | collective-permute-start | bytes 3145736 | tf_op jit(solution)/shard_map/ppermute | solution.py:363
  105.7 13.4 %collective-permute-start.3 = (bf16[64,256]{1,0:T(8,128)(2,1)S(1)}, bf16[64,256]{1,0:T(8,128)(2,1)S(1)}, u32[]{:S(2)}, u32[]{:S(2)}) collective-permute-start(bf16[64,256]{1,0:T(8,128)(2,1)S(1)} %get-tuple-element.11), channel_id=1, source_target_pairs={{0,64},{8,72},{16,80},{24,88},{32,96},{40,104},{48,112},{56,120},{... | collective-permute-start | bytes 98312 | tf_op jit(solution)/shard_map/ppermute | solution.py:325
  119.3 23.0 %collective-permute-start.4 = (bf16[64,256]{1,0:T(8,128)(2,1)S(1)}, bf16[64,256]{1,0:T(8,128)(2,1)S(1)}, u32[]{:S(2)}, u32[]{:S(2)}) collective-permute-start(bf16[64,256]{1,0:T(8,128)(2,1)S(1)} %get-tuple-element.13), channel_id=1, source_target_pairs={{0,128},{8,136},{16,144},{24,152},{32,160},{40,168},{48,176},{56,1... | collective-permute-start | bytes 98312 | tf_op jit(solution)/shard_map/ppermute | solution.py:325
  149.6 23.0 %collective-permute-start.12 = (bf16[64,256]{1,0:T(8,128)(2,1)S(1)}, bf16[64,256]{1,0:T(8,128)(2,1)S(1)}, u32[]{:S(2)}, u32[]{:S(2)}) collective-permute-start(bf16[64,256]{1,0:T(8,128)(2,1)S(1)} %convolution_convert_fusion.2), channel_id=1, source_target_pairs={{0,128},{8,136},{16,144},{24,152},{32,160},{40,168},{48,176},{56,1... | collective-permute-start | bytes 98312 | tf_op jit(solution)/shard_map/ppermute | solution.py:325
  173.0 13.4 %collective-permute-start.13 = (bf16[64,256]{1,0:T(8,128)(2,1)S(1)}, bf16[64,256]{1,0:T(8,128)(2,1)S(1)}, u32[]{:S(2)}, u32[]{:S(2)}) collective-permute-start(bf16[64,256]{1,0:T(8,128)(2,1)S(1)} %convolution_convert_fusion.1), channel_id=1, source_target_pairs={{0,64},{8,72},{16,80},{24,88},{32,96},{40,104},{48,112},{56,120},{... | collective-permute-start | bytes 98312 | tf_op jit(solution)/shard_map/ppermute | solution.py:325
  186.9 8.7 %collective-permute-start.14 = (bf16[64,256]{1,0:T(8,128)(2,1)S(1)}, bf16[64,256]{1,0:T(8,128)(2,1)S(1)}, u32[]{:S(2)}, u32[]{:S(2)}) collective-permute-start(bf16[64,256]{1,0:T(8,128)(2,1)S(1)} %convolution_convert_fusion), channel_id=1, source_target_pairs={{0,32},{8,40},{16,48},{24,56},{32,0},{40,8},{48,16},{56,24},{64,96... | collective-permute-start | bytes 98312 | tf_op jit(solution)/shard_map/ppermute | solution.py:325
  188.8 7.2 %collective-permute-start.15 = (bf16[256,256]{1,0:T(8,128)(2,1)S(1)}, bf16[256,256]{1,0:T(8,128)(2,1)S(1)}, u32[]{:S(2)}, u32[]{:S(2)}) collective-permute-start(bf16[256,256]{1,0:T(8,128)(2,1)S(1)} %slice_bitcast_fusion.10), channel_id=1, source_target_pairs={{0,16},{8,24},{16,0},{24,8},{32,48},{40,56},{48,32},{56,40},{64,80... | collective-permute-start | bytes 393224 | tf_op jit(solution)/shard_map/ppermute | solution.py:325
  196.4 25.0 %copy-start.4 = (s32[1,16]{1,0:T(1,128)S(1)}, s32[1,16]{1,0:T(1,128)}, u32[]{:S(2)}) copy-start(s32[1,16]{1,0:T(1,128)} %refs_0_.1) | copy-start | bytes 196
